TPU v7x, 32 devices: a whole 2x2x4 slice. The times are simulated.
32 devices in a mesh: dp: 16 (over z, y, core), tensor: 2 (over x).
Axes of the slice: x: 2, y: 2, z: 4, core: 2. Of those that a mesh axis runs over, the one named last changes fastest.
Arguments:
- tokens: bfloat16 [32, 1024, 768], P(None, ('dp', 'tensor')), may hold values from -6 to 6
- out_grad: bfloat16 [32, 1024, 768], P(None, ('dp', 'tensor')), may hold values from -6 to 6
- lengths: int32 [32], replicated, may hold values from 256 to 1024, as said below
- order: int32 [1024], replicated, may hold values from 0 to 1023, each once
- w_qkv: bfloat16 [3, 768, 768], P(None, 'dp', 'tensor'), may hold values from -0.21875 to 0.21875
- b_qkv: float32 [3, 768], P(None, 'tensor'), may hold values from -3 to 3
- w_out: bfloat16 [768, 768], P('tensor', 'dp'), may hold values from -6 to 6
- b_out: float32 [768], replicated, may hold values from -3 to 3
- norm1_gain: float32 [768], replicated, may hold values from 0.25 to 1.75
- norm1_bias: float32 [768], replicated, may hold values from -2 to 2
- w_up: bfloat16 [768, 3072], P('dp', 'tensor'), may hold values from -0.21875 to 0.21875
- b_up: float32 [3072], P('tensor'), may hold values from -3 to 3
- w_down: bfloat16 [3072, 768], P('tensor', 'dp'), may hold values from -0.15625 to 0.15625
- b_down: float32 [768], replicated, may hold values from -3 to 3
- norm2_gain: float32 [768], replicated, may hold values from 0.25 to 1.75
- norm2_bias: float32 [768], replicated, may hold values from -2 to 2
Outputs:
- mixed: bfloat16 [32, 1024, 768], P(None, ('dp', 'tensor'))
- grad_tokens: bfloat16 [32, 1024, 768], P(None, ('dp', 'tensor'))
- grad_w_qkv: float32 [3, 768, 768], P(None, 'dp', 'tensor')
- grad_b_qkv: float32 [3, 768], replicated
- grad_w_out: float32 [768, 768], P('tensor', 'dp')
- grad_b_out: float32 [768], replicated
- grad_norm1_gain: float32 [768], replicated
- grad_norm1_bias: float32 [768], replicated
- grad_w_up: float32 [768, 3072], P('dp', 'tensor')
- grad_b_up: float32 [3072], replicated
- grad_w_down: float32 [3072, 768], P('tensor', 'dp')
- grad_b_down: float32 [768], replicated
- grad_norm2_gain: float32 [768], replicated
- grad_norm2_bias: float32 [768], replicated
Inputs may be any that keep to these rules, and one draw needn't show every extreme that they name: `lengths`: one sequence in every draw has length 1024. `order`: the same for every sequence, each position once.
All inputs are finite; a program needn't handle non-finite values.
Results may differ from a plain program's by a relative error of at most 0.019.
Values may be sent and summed in bfloat16 or wider, within the bound.
A program may use at most 192 MiB of HBM per device.

v0:
```python
import jax
import jax.numpy as jnp
from jax import lax
from jax.sharding import PartitionSpec as P

HD = 64


NORM_EPS = 1e-12
ROPE_BASE = 10000.0
MASK_FILL = -1e30
SCORE_SCALE = 0.125
INV_ROOT_TWO = 0.7071067811865476
INV_ROOT_TAU = 0.3989422804014327


def rope_tables(positions):
    steps = jnp.arange(HD // 2).astype(jnp.float32)
    inverse = jnp.power(ROPE_BASE, -2.0 * steps / HD)
    angles = positions.astype(jnp.float32)[:, None] * inverse[None, :]
    return (jnp.cos(angles), jnp.sin(angles))


def rotate(values, cos_table, sine_table, forward_turn):
    slot_rows, cols = values.shape
    shaped = values.reshape(slot_rows, cols // HD, HD // 2, 2)
    first = shaped[..., 0]
    second = shaped[..., 1]
    cos_part = cos_table[:, None, :]
    sine_part = sine_table[:, None, :]
    if forward_turn:
        turned = jnp.stack(
            [first * cos_part - second * sine_part, first * sine_part + second * cos_part], axis=-1
        )
    else:
        turned = jnp.stack(
            [first * cos_part + second * sine_part, second * cos_part - first * sine_part], axis=-1
        )
    return turned.reshape(slot_rows, cols)


def normalize(hidden, gain_vec, shift_vec):
    row_mean = jnp.mean(hidden, axis=-1, keepdims=True)
    centred = hidden - row_mean
    row_var = jnp.mean(centred * centred, axis=-1, keepdims=True)
    inv_std = lax.rsqrt(row_var + NORM_EPS)
    normed = centred * inv_std
    return (normed * gain_vec + shift_vec, normed, inv_std)


def normalize_back(grad_unit, normed, inv_std):
    first_mean = jnp.mean(grad_unit, axis=-1, keepdims=True)
    second_mean = jnp.mean(grad_unit * normed, axis=-1, keepdims=True)
    return inv_std * (grad_unit - first_mean - normed * second_mean)


def gelu_slope(up_proj):
    return (
        0.5 * (1.0 + lax.erf(up_proj * INV_ROOT_TWO))
        + up_proj * jnp.exp(-0.5 * up_proj * up_proj) * INV_ROOT_TAU
    )


def head_part(source, col_start, head_cols, head_block):
    return lax.dynamic_slice_in_dim(source, col_start, head_cols, 1).reshape(
        source.shape[0], head_block, HD
    )


def score_block(query_part, key_part, key_keep):
    scores = (
        jnp.einsum("qhe,khe->hqk", query_part, key_part, preferred_element_type=jnp.float32)
        * SCORE_SCALE
    )
    return jnp.where(key_keep[None, None, :], scores, MASK_FILL)


def block_shape(cols):
    heads_dev = cols // HD
    head_block = 2
    return (heads_dev, head_block, head_block * HD)


def attend(query, keys_rot, value, key_keep):
    slot_rows, cols = query.shape
    heads_dev, head_block, head_cols = block_shape(cols)

    def one_block(block_idx, carry_val):
        ctx_buf, lse_buf = carry_val
        col_start = block_idx * head_cols
        scores = score_block(
            head_part(query, col_start, head_cols, head_block),
            head_part(keys_rot, col_start, head_cols, head_block),
            key_keep,
        )
        row_max = jnp.max(scores, axis=-1, keepdims=True)
        expo_vals = jnp.exp(scores - row_max)
        row_total = jnp.sum(expo_vals, axis=-1, keepdims=True)
        prob_low = (expo_vals / row_total).astype(jnp.bfloat16)
        block_out = jnp.einsum(
            "hqk,khe->qhe",
            prob_low,
            head_part(value, col_start, head_cols, head_block),
            preferred_element_type=jnp.float32,
        )
        ctx_buf = lax.dynamic_update_slice_in_dim(
            ctx_buf, block_out.reshape(slot_rows, head_cols).astype(jnp.bfloat16), col_start, 1
        )
        lse_buf = lax.dynamic_update_slice_in_dim(
            lse_buf, (row_max + jnp.log(row_total))[..., 0], block_idx * head_block, 0
        )
        return (ctx_buf, lse_buf)

    start_val = (
        jnp.zeros((slot_rows, cols), jnp.bfloat16),
        jnp.zeros((heads_dev, slot_rows), jnp.float32),
    )
    return lax.fori_loop(0, heads_dev // head_block, one_block, start_val)


def attend_back(query, keys_rot, value, key_keep, lse_buf, grad_ctx):
    slot_rows, cols = query.shape
    heads_dev, head_block, head_cols = block_shape(cols)

    def one_block(block_idx, carry_val):
        grad_query, grad_keys, grad_value = carry_val
        col_start = block_idx * head_cols
        query_part = head_part(query, col_start, head_cols, head_block)
        key_part = head_part(keys_rot, col_start, head_cols, head_block)
        value_part = head_part(value, col_start, head_cols, head_block)
        grad_part = head_part(grad_ctx, col_start, head_cols, head_block)
        lse_part = lax.dynamic_slice_in_dim(lse_buf, block_idx * head_block, head_block, 0)
        prob_vals = jnp.exp(score_block(query_part, key_part, key_keep) - lse_part[:, :, None])
        prob_low = prob_vals.astype(jnp.bfloat16)
        value_grad = jnp.einsum(
            "hqk,qhe->khe", prob_low, grad_part, preferred_element_type=jnp.float32
        )
        grad_prob = jnp.einsum(
            "qhe,khe->hqk", grad_part, value_part, preferred_element_type=jnp.float32
        )
        inner = jnp.sum(grad_prob * prob_vals, axis=-1, keepdims=True)
        grad_score = (prob_vals * (grad_prob - inner)).astype(jnp.bfloat16)
        query_grad = (
            jnp.einsum("hqk,khe->qhe", grad_score, key_part, preferred_element_type=jnp.float32)
            * SCORE_SCALE
        )
        key_grad = (
            jnp.einsum("hqk,qhe->khe", grad_score, query_part, preferred_element_type=jnp.float32)
            * SCORE_SCALE
        )
        grad_query = lax.dynamic_update_slice_in_dim(
            grad_query, query_grad.reshape(slot_rows, head_cols), col_start, 1
        )
        grad_keys = lax.dynamic_update_slice_in_dim(
            grad_keys, key_grad.reshape(slot_rows, head_cols), col_start, 1
        )
        grad_value = lax.dynamic_update_slice_in_dim(
            grad_value, value_grad.reshape(slot_rows, head_cols), col_start, 1
        )
        return (grad_query, grad_keys, grad_value)

    empty = jnp.zeros((slot_rows, cols), jnp.float32)
    return lax.fori_loop(0, heads_dev // head_block, one_block, (empty, empty, empty))


def fetch_forward(w_qkv, w_out, w_up, w_down):
    attn_part = (
        lax.all_gather(w_qkv, "dp", axis=1, tiled=True),
        lax.all_gather(w_out, "dp", axis=1, tiled=True),
    )
    ffn_part = (
        lax.all_gather(w_up, "dp", axis=0, tiled=True),
        lax.all_gather(w_down, "dp", axis=1, tiled=True),
    )
    return (attn_part[0], attn_part[1], ffn_part[0], ffn_part[1])


def fetch_backward(w_qkv, w_out, w_up, w_down):
    attn_part = (
        lax.all_gather(w_qkv, "dp", axis=1, tiled=True),
        lax.all_gather(w_out, "dp", axis=1, tiled=True),
    )
    ffn_part = (
        lax.all_gather(w_up, "dp", axis=0, tiled=True),
        lax.all_gather(w_down, "dp", axis=1, tiled=True),
    )
    return (attn_part[0], attn_part[1], ffn_part[0], ffn_part[1])


def spread_forward(rows_val):
    return lax.all_gather(rows_val, "tensor", axis=0, tiled=True)


def collect_forward(terms):
    return lax.psum_scatter(terms, "tensor", scatter_dimension=0, tiled=True)


def spread_backward(rows_val):
    return lax.all_gather(rows_val, "tensor", axis=0, tiled=True)


def collect_backward(terms):
    return lax.psum_scatter(
        terms.astype(jnp.bfloat16), "tensor", scatter_dimension=0, tiled=True
    ).astype(jnp.float32)


def body(
    tokens,
    out_grad,
    lengths,
    order,
    w_qkv,
    b_qkv,
    w_out,
    b_out,
    norm1_gain,
    norm1_bias,
    w_up,
    b_up,
    w_down,
    b_down,
    norm2_gain,
    norm2_bias,
):
    dp_size = lax.axis_size("dp")
    tp_size = lax.axis_size("tensor")
    dp_rank = lax.axis_index("dp")
    member = lax.axis_index("tensor")
    stored, stripe, features = tokens.shape
    batches = stored // dp_size
    dev_rows = dp_size * stripe
    slot_rows = dev_rows * tp_size
    head_cols_dev = w_qkv.shape[2]
    unit_cols = w_up.shape[1]
    dealt = (
        lax.all_to_all(
            tokens.reshape(batches, dp_size, stripe, features),
            "dp",
            split_axis=1,
            concat_axis=2,
            tiled=True,
        ),
        lax.all_to_all(
            out_grad.reshape(batches, dp_size, stripe, features),
            "dp",
            split_axis=1,
            concat_axis=2,
            tiled=True,
        ),
    )
    inputs = dealt[0].reshape(batches, dev_rows, features)
    cotangents = dealt[1].reshape(batches, dev_rows, features)
    local_row = jnp.arange(dev_rows, dtype=jnp.int32)
    stored_local = (local_row // stripe * tp_size + member) * stripe + local_row % stripe
    full_row = jnp.arange(slot_rows, dtype=jnp.int32)
    stored_full = (
        full_row % dev_rows // stripe * tp_size + full_row // dev_rows
    ) * stripe + full_row % stripe
    place_local = jnp.take(order, stored_local)
    place_full = jnp.take(order, stored_full)
    cos_table, sine_table = rope_tables(place_full)
    grad_wq = jnp.zeros((3, features, head_cols_dev), jnp.float32)
    grad_wo = jnp.zeros((head_cols_dev, features), jnp.float32)
    grad_wu = jnp.zeros((features, unit_cols), jnp.float32)
    grad_wd = jnp.zeros((unit_cols, features), jnp.float32)
    grad_bq = jnp.zeros((3, head_cols_dev), jnp.float32)
    grad_bu = jnp.zeros((unit_cols,), jnp.float32)
    grad_bo = jnp.zeros((features,), jnp.float32)
    grad_bd = jnp.zeros((features,), jnp.float32)
    grad_gain_one = jnp.zeros((features,), jnp.float32)
    grad_shift_one = jnp.zeros((features,), jnp.float32)
    grad_gain_two = jnp.zeros((features,), jnp.float32)
    grad_shift_two = jnp.zeros((features,), jnp.float32)
    results = []
    input_grads = []
    for micro in range(batches):
        length = lax.dynamic_index_in_dim(lengths, micro * dp_size + dp_rank, 0, keepdims=False)
        key_keep = place_full < length
        row_keep = place_local < length
        weight_q, weight_o, weight_u, weight_d = fetch_forward(w_qkv, w_out, w_up, w_down)
        own_rows = inputs[micro]
        gathered_in = spread_forward(own_rows)
        raw_proj = (
            jnp.einsum("sd,kde->kse", gathered_in, weight_q, preferred_element_type=jnp.float32)
            + b_qkv[:, None, :]
        )
        query = rotate(raw_proj[0], cos_table, sine_table, True).astype(jnp.bfloat16)
        keys_rot = rotate(raw_proj[1], cos_table, sine_table, True).astype(jnp.bfloat16)
        value = raw_proj[2].astype(jnp.bfloat16)
        context, lse_buf = attend(query, keys_rot, value, key_keep)
        attended = collect_forward(jnp.dot(context, weight_o, preferred_element_type=jnp.float32))
        first_sum = own_rows.astype(jnp.float32) + attended + b_out
        normed_one, unit_one, inv_one = normalize(first_sum, norm1_gain, norm1_bias)
        gathered_mid = spread_forward(normed_one.astype(jnp.bfloat16))
        up_proj = jnp.dot(gathered_mid, weight_u, preferred_element_type=jnp.float32) + b_up
        activated = jax.nn.gelu(up_proj, approximate=False).astype(jnp.bfloat16)
        down_sum = collect_forward(jnp.dot(activated, weight_d, preferred_element_type=jnp.float32))
        second_sum = normed_one + down_sum + b_down
        result_rows, unit_two, inv_two = normalize(second_sum, norm2_gain, norm2_bias)
        results.append(result_rows.astype(jnp.bfloat16))
        weight_q, weight_o, weight_u, weight_d = fetch_backward(w_qkv, w_out, w_up, w_down)
        grad_out = jnp.where(row_keep[:, None], cotangents[micro].astype(jnp.float32), 0.0)
        grad_gain_two = grad_gain_two + jnp.sum(grad_out * unit_two, axis=0)
        grad_shift_two = grad_shift_two + jnp.sum(grad_out, axis=0)
        grad_second = normalize_back(grad_out * norm2_gain, unit_two, inv_two)
        grad_bd = grad_bd + jnp.sum(grad_second, axis=0)
        grad_down_full = spread_backward(grad_second.astype(jnp.bfloat16))
        grad_wd = grad_wd + jnp.einsum(
            "sf,sd->fd", activated, grad_down_full, preferred_element_type=jnp.float32
        )
        grad_act = jnp.einsum(
            "sd,fd->sf", grad_down_full, weight_d, preferred_element_type=jnp.float32
        )
        grad_up = (grad_act * gelu_slope(up_proj)).astype(jnp.bfloat16)
        grad_bu = grad_bu + jnp.sum(grad_up.astype(jnp.float32), axis=0)
        grad_wu = grad_wu + jnp.einsum(
            "sd,sf->df", gathered_mid, grad_up, preferred_element_type=jnp.float32
        )
        mid_sum = collect_backward(
            jnp.einsum("sf,df->sd", grad_up, weight_u, preferred_element_type=jnp.float32)
        )
        grad_mid = grad_second + mid_sum
        grad_gain_one = grad_gain_one + jnp.sum(grad_mid * unit_one, axis=0)
        grad_shift_one = grad_shift_one + jnp.sum(grad_mid, axis=0)
        grad_first = normalize_back(grad_mid * norm1_gain, unit_one, inv_one)
        grad_bo = grad_bo + jnp.sum(grad_first, axis=0)
        grad_attn_full = spread_backward(grad_first.astype(jnp.bfloat16))
        grad_wo = grad_wo + jnp.einsum(
            "sc,sd->cd", context, grad_attn_full, preferred_element_type=jnp.float32
        )
        grad_ctx = jnp.einsum(
            "sd,cd->sc", grad_attn_full, weight_o, preferred_element_type=jnp.float32
        ).astype(jnp.bfloat16)
        grad_query, grad_keys, grad_value = attend_back(
            query, keys_rot, value, key_keep, lse_buf, grad_ctx
        )
        grad_q_low = rotate(grad_query, cos_table, sine_table, False).astype(jnp.bfloat16)
        grad_k_low = rotate(grad_keys, cos_table, sine_table, False).astype(jnp.bfloat16)
        grad_v_low = grad_value.astype(jnp.bfloat16)
        grad_raw = jnp.stack([grad_q_low, grad_k_low, grad_v_low], axis=0)
        grad_bq = grad_bq + jnp.sum(grad_raw.astype(jnp.float32), axis=1)
        grad_wq = grad_wq + jnp.einsum(
            "sd,kse->kde", gathered_in, grad_raw, preferred_element_type=jnp.float32
        )
        in_sum = collect_backward(
            jnp.einsum("kse,kde->sd", grad_raw, weight_q, preferred_element_type=jnp.float32)
        )
        grad_rows = grad_first + in_sum
        input_grads.append(grad_rows.astype(jnp.bfloat16))
    out_rows = jnp.stack(results, axis=0).reshape(batches, 1, dev_rows, features)
    grad_rows_all = jnp.stack(input_grads, axis=0).reshape(batches, 1, dev_rows, features)
    returned = (
        lax.all_to_all(out_rows, "dp", split_axis=2, concat_axis=1, tiled=True),
        lax.all_to_all(grad_rows_all, "dp", split_axis=2, concat_axis=1, tiled=True),
    )
    mixed = returned[0].reshape(stored, stripe, features)
    grad_tokens = returned[1].reshape(stored, stripe, features)
    weight_sums = (
        lax.psum_scatter(grad_wq, "dp", scatter_dimension=1, tiled=True),
        lax.psum_scatter(grad_wo, "dp", scatter_dimension=1, tiled=True),
        lax.psum_scatter(grad_wu, "dp", scatter_dimension=0, tiled=True),
        lax.psum_scatter(grad_wd, "dp", scatter_dimension=1, tiled=True),
    )
    bias_q_full = lax.dynamic_update_slice_in_dim(
        jnp.zeros((3, head_cols_dev * tp_size), jnp.float32), grad_bq, member * head_cols_dev, 1
    )
    bias_u_full = lax.dynamic_update_slice_in_dim(
        jnp.zeros((unit_cols * tp_size,), jnp.float32), grad_bu, member * unit_cols, 0
    )
    small_sums = lax.psum(
        (
            bias_q_full,
            grad_bo,
            grad_gain_one,
            grad_shift_one,
            bias_u_full,
            grad_bd,
            grad_gain_two,
            grad_shift_two,
        ),
        ("dp", "tensor"),
    )
    return (
        mixed,
        grad_tokens,
        weight_sums[0],
        small_sums[0],
        weight_sums[1],
        small_sums[1],
        small_sums[2],
        small_sums[3],
        weight_sums[2],
        small_sums[4],
        weight_sums[3],
        small_sums[5],
        small_sums[6],
        small_sums[7],
    )


def solution(mesh):
    in_specs = (
        P(None, ("dp", "tensor"), None),
        P(None, ("dp", "tensor"), None),
        P(),
        P(),
        P(None, "dp", "tensor"),
        P(None, "tensor"),
        P("tensor", "dp"),
        P(),
        P(),
        P(),
        P("dp", "tensor"),
        P("tensor"),
        P("tensor", "dp"),
        P(),
        P(),
        P(),
    )
    out_specs = (
        P(None, ("dp", "tensor"), None),
        P(None, ("dp", "tensor"), None),
        P(None, "dp", "tensor"),
        P(),
        P("tensor", "dp"),
        P(),
        P(),
        P(),
        P("dp", "tensor"),
        P(),
        P("tensor", "dp"),
        P(),
        P(),
        P(),
    )
    return jax.shard_map(body, mesh=mesh, in_specs=in_specs, out_specs=out_specs, check_vma=False)
```

profile of v0, /device:TPU:0, one launch (start us, length us, event | category | flops | bytes accessed | tf_op | source)
XLA Modules:
  0.0 1358.5 jit_solution(11162640923174364690)
XLA Ops:
  9.5 53.8 %all_to_all.16 = bf16[2,16,32,768]{3,2,0,1:T(8,128)(2,1)S(1)} all-to-all(bf16[2,16,32,768]{3,2,0,1:T(8,128)(2,1)S(1)} %copy.98), channel_id=1, replica_groups=mesh['dp'=16,'tensor'=2] {'dp'}, dimensions={1} | all-to-all | bytes 3145728 | tf_op jit(solution)/shard_map/all_to_all | solution.py:237
  64.8 4.5 gather_fusion
  71.9 23.8 %all_gather.50 = bf16[384,768]{0,1:T(8,128)(2,1)} all-gather(bf16[384,48]{0,1:T(8,128)(2,1)S(1)} %copy-done.54), channel_id=1, replica_groups=mesh['dp'=16,'tensor'=2] {'dp'}, dimensions={1}, use_global_device_ids=true | all-gather | bytes 626688 | tf_op jit(solution)/shard_map/all_gather | solution.py:169
  102.1 19.0 %all-gather.14.cloned.1.call-done = bf16[1024,768]{1,0:T(8,128)(2,1)} async-done(((bf16[512,768]{1,0:T(8,128)(2,1)}), bf16[1024,768]{1,0:T(8,128)(2,1)}) %all-gather.14.cloned.1.call-update) | async-done | bytes 1572880 | tf_op jit(solution)/shard_map/all_gather | solution.py:191
  138.4 11.5 subtract_convert_fusion.6
  157.8 39.1 %while.65 = (s32[]{:T(128)}, bf16[1024,384]{0,1:T(8,128)(2,1)}, f32[6,1024]{1,0:T(8,128)S(1)}, bf16[1024,384]{0,1:T(8,128)(2,1)S(1)}, pred[1024]{0:T(1024)(128)(...) while((s32[]{:T(128)}, bf16[1024,384]{0,1:T(8,128)(2,1)}, ...), condition=%wide.region_13.14_spmd, body=%wide.region_10.13_spmd.sunk | while | flops 562165760 | bytes 61934852 | solution.py:118
  165.4 4.9 fusion.256
  178.4 4.9 fusion.256
  191.3 4.9 fusion.256
  196.9 4.8 fusion.139
  201.8 5.0 pad_maximum_fusion.2
  208.4 38.9 %while.64 = (s32[]{:T(128)}, bf16[1024,384]{0,1:T(8,128)(2,1)}, f32[6,1024]{1,0:T(8,128)S(1)}, bf16[1024,384]{0,1:T(8,128)(2,1)S(1)}, pred[1024]{0:T(1024)(128)(...) while((s32[]{:T(128)}, bf16[1024,384]{0,1:T(8,128)(2,1)}, ...), condition=%wide.region_3.4_spmd, body=%wide.region_0.3_spmd.sunk | while | flops 562165760 | bytes 61934852 | solution.py:118
  215.8 4.9 fusion.250
  228.7 4.9 fusion.250
  241.7 4.9 fusion.250
  247.3 4.4 fusion.137
  252.4 42.9 %reduce-scatter.12.cloned.1.call-done = f32[512,768]{1,0:T(8,128)} async-done(((f32[1024,768]{1,0:T(8,128)}), f32[512,768]{1,0:T(8,128)}) %reduce-scatter.12.cloned.1.call-update) | async-done | bytes 1572880 | tf_op jit(solution)/shard_map/reduce_scatter | solution.py:195
  302.1 37.7 %all-gather.18.cloned.1.call-done = bf16[768,1536]{1,0:T(8,128)(2,1)} async-done(((bf16[48,1536]{1,0:T(8,128)(2,1)}), bf16[768,1536]{1,0:T(8,128)(2,1)}) %all-gather.18.cloned.1.call-update) | async-done | bytes 2359312 | tf_op jit(solution)/shard_map/all_gather | solution.py:172
  339.8 28.0 %all-gather.24.cloned.1.call-done = bf16[1024,768]{1,0:T(8,128)(2,1)} async-done(((bf16[512,768]{1,0:T(8,128)(2,1)}), bf16[1024,768]{1,0:T(8,128)(2,1)}) %all-gather.24.cloned.1.call-update) | async-done | bytes 1572880 | tf_op jit(solution)/shard_map/all_gather | solution.py:191
  367.8 7.4 fusion.140
  375.3 21.9 %all-gather.16.cloned.1.call-done = bf16[1024,768]{1,0:T(8,128)(2,1)} async-done(((bf16[512,768]{1,0:T(8,128)(2,1)}), bf16[1024,768]{1,0:T(8,128)(2,1)}) %all-gather.16.cloned.1.call-update) | async-done | bytes 1572880 | tf_op jit(solution)/shard_map/all_gather | solution.py:191
  397.2 32.7 %fusion.26 = (bf16[1024,1536]{1,0:T(8,128)(2,1)}, bf16[1024,1536]{1,0:T(8,128)(2,1)}, f32[1024,1536]{1,0:T(8,128)}) fusion(f32[1536]{0:T(1024)S(1)} %copy-done.82, f32[1024,1536]{1,0:T(8,128)} %fusion.140, bf16[1024,768]{1,0:T(8,128)(2,1)} %all-gather.16.cloned.1.call-done, bf16[768,1536]{1,0:T(8,128)(2,1)} %all-gather.18.cloned.1.call-done), kind=kOutput, calls=%fused_computation.72 | convolution fusion | flops 2623537152 | bytes 22812672 | tf_op jit(solution)/shard_map/dot_general | solution.py:296
  429.9 11.9 all-gather.20.cloned.1.call-done
  441.8 7.0 fusion.138
  448.9 6.9 fusion.141
  458.5 4.5 all-to-all-start.2
  468.4 26.5 %all-to-all-done.2 = bf16[2,16,32,768]{3,2,0,1:T(8,128)(2,1)} async-done(((bf16[2,16,32,768]{3,2,0,1:T(8,128)(2,1)}), bf16[2,16,32,768]{3,2,0,1:T(8,128)(2,1)}, u32[]{:S(2)}, u32[]{:S(2)}) %all-to-all-start.2) | async-done | bytes 1572896 | tf_op jit(solution)/shard_map/all_to_all | solution.py:244
  497.8 39.1 %reduce-scatter.18.cloned.1.call-done = f32[512,768]{1,0:T(8,128)} async-done(((f32[1024,768]{1,0:T(8,128)}), f32[512,768]{1,0:T(8,128)}) %reduce-scatter.18.cloned.1.call-update) | async-done | bytes 1572880 | tf_op jit(solution)/shard_map/reduce_scatter | solution.py:195
  543.6 4.5 fusion.126
  548.9 26.5 %all-gather.26.cloned.1.call-done = bf16[1024,768]{1,0:T(8,128)(2,1)} async-done(((bf16[512,768]{1,0:T(8,128)(2,1)}), bf16[1024,768]{1,0:T(8,128)(2,1)}) %all-gather.26.cloned.1.call-update) | async-done | bytes 1572880 | tf_op jit(solution)/shard_map/all_gather | solution.py:199
  575.4 7.7 convert_reduce_fusion.1
  588.7 15.5 %all-gather.30.cloned.1.call-done = bf16[1024,768]{1,0:T(8,128)(2,1)} async-done(((bf16[512,768]{1,0:T(8,128)(2,1)}), bf16[1024,768]{1,0:T(8,128)(2,1)}) %all-gather.30.cloned.1.call-update) | async-done | bytes 1572880 | tf_op jit(solution)/shard_map/all_gather | solution.py:199
  604.2 7.7 convert_reduce_fusion
  617.3 15.1 %reduce-scatter.20.cloned.1.call-done = bf16[512,768]{1,0:T(8,128)(2,1)} async-done(((bf16[1024,768]{1,0:T(8,128)(2,1)}), bf16[512,768]{1,0:T(8,128)(2,1)}) %reduce-scatter.20.cloned.1.call-update) | async-done | bytes 786448 | tf_op jit(solution)/shard_map/reduce_scatter | solution.py:203
  635.6 25.2 %reduce-scatter.24.cloned.1.call-done = bf16[512,768]{1,0:T(8,128)(2,1)} async-done(((bf16[1024,768]{1,0:T(8,128)(2,1)}), bf16[512,768]{1,0:T(8,128)(2,1)}) %reduce-scatter.24.cloned.1.call-update) | async-done | bytes 786448 | tf_op jit(solution)/shard_map/reduce_scatter | solution.py:203
  671.5 22.6 %all-gather.28.cloned.1.call-done = bf16[1024,768]{1,0:T(8,128)(2,1)} async-done(((bf16[512,768]{1,0:T(8,128)(2,1)}), bf16[1024,768]{1,0:T(8,128)(2,1)}) %all-gather.28.cloned.1.call-update) | async-done | bytes 1572880 | tf_op jit(solution)/shard_map/all_gather | solution.py:199
  699.8 75.5 %while.66 = (s32[]{:T(128)}, f32[1024,384]{0,1:T(8,128)S(1)}, f32[1024,384]{0,1:T(8,128)}, bf16[1024,384]{1,0:T(8,128)(2,1)}, bf16[1024,384]{0,1:T(8,128)(2,1)},...) while((s32[]{:T(128)}, f32[1024,384]{0,1:T(8,128)S(1)}, ...), condition=%wide.region_27.28_spmd, body=%wide.region_25.27_spmd.sunk | while | flops 1373894656 | bytes 97054008 | solution.py:163
  701.8 4.6 fusion.267
  709.3 5.4 multiply_reduce_fusion.20
  726.9 4.6 fusion.267
  734.4 5.4 multiply_reduce_fusion.20
  752.1 4.6 fusion.267
  759.6 5.4 multiply_reduce_fusion.20
  787.7 74.4 %while.67 = (s32[]{:T(128)}, f32[1024,384]{0,1:T(8,128)}, f32[1024,384]{0,1:T(8,128)}, bf16[1024,384]{1,0:T(8,128)(2,1)S(1)}, bf16[1024,384]{0,1:T(8,128)(2,1)},...) while((s32[]{:T(128)}, f32[1024,384]{0,1:T(8,128)}, ...), condition=%wide.region_36.37_spmd, body=%wide.region_34.36_spmd.sunk | while | flops 1373894656 | bytes 97054008 | solution.py:163
  790.1 4.6 fusion.279
  797.6 5.4 multiply_reduce_fusion.21
  814.7 4.6 fusion.279
  822.2 5.4 multiply_reduce_fusion.21
  839.4 4.6 fusion.279
  846.9 5.4 multiply_reduce_fusion.21
  868.6 11.7 add_convert_fusion.7
  894.4 5.7 bitcast_convert_fusion.1
  908.1 5.5 bitcast_convert_fusion
  931.1 4.9 fusion.144
  936.0 4.4 convolution_add_fusion
  946.6 4.5 convolution_add_fusion.1
  955.4 6.0 all-to-all-start.1
  968.2 42.0 %all-to-all-done.1 = bf16[2,1,512,768]{3,0,1,2:T(2,128)(2,1)} async-done(((bf16[2,1,512,768]{3,0,1,2:T(2,128)(2,1)}), bf16[2,1,512,768]{3,0,1,2:T(2,128)(2,1)}, u32[]{:S(2)}, u32[]{:S(2)}) %all-to-all-start.1) | async-done | bytes 1572896 | tf_op jit(solution)/shard_map/all_to_all | solution.py:354
  1010.2 8.1 all-to-all-start.3
  1023.8 64.2 %all-reduce.1 = (f32[3,768]{1,0:T(4,128)}, f32[768]{0:T(1024)}, f32[768]{0:T(1024)}, f32[768]{0:T(1024)}, f32[3072]{0:T(1024)}, /*index=5*/f32[768]{0:T(1024)}, f32[768]{0:T(1024)}, f32[768]{0:T(1024)}) all-reduce(f32[3,768]{1,0:T(4,128)S(1)} %add_dynamic-update-slice_fusion.3, ...), channel_id=1, replica_groups=mesh['dp'=16,'tensor'=2] {'dp','tensor'}, use_global_device_ids=true, to_apply=%region_41.42 | all-reduce | flops 9984 | bytes 79872 | tf_op jit(solution)/shard_map/psum | solution.py:371
  1088.0 43.3 %all-reduce.4.cloned.1.call-done = f32[3,768,384]{2,0,1:T(4,128)} async-done(((f32[3,768,384]{2,0,1:T(4,128)}), f32[3,768,384]{2,0,1:T(4,128)}) %all-reduce.4.cloned.1.call-update) | async-done | bytes 3538960
  1134.4 59.1 %reduce-scatter.28.cloned.1.call-done = f32[384,48]{0,1:T(8,128)} async-done(((f32[384,768]{0,1:T(8,128)}), f32[384,48]{0,1:T(8,128)}) %reduce-scatter.28.cloned.1.call-update) | async-done | bytes 73744 | tf_op jit(solution)/shard_map/reduce_scatter | solution.py:361
  1193.5 79.0 %reduce-scatter.32.cloned.1.call-done = f32[1536,48]{0,1:T(8,128)} async-done(((f32[1536,768]{0,1:T(8,128)}), f32[1536,48]{0,1:T(8,128)}) %reduce-scatter.32.cloned.1.call-update) | async-done | bytes 294928 | tf_op jit(solution)/shard_map/reduce_scatter | solution.py:363
  1272.5 79.3 %reduce-scatter.30.cloned.1.call-done = f32[48,1536]{1,0:T(8,128)} async-done(((f32[768,1536]{1,0:T(8,128)}), f32[48,1536]{1,0:T(8,128)}) %reduce-scatter.30.cloned.1.call-update) | async-done | bytes 294928 | tf_op jit(solution)/shard_map/reduce_scatter | solution.py:362
  (506 shorter events, 315.9 us)
Async XLA Ops:
  7.2 57.5 %copy-start = (s32[1024]{0:T(1024)S(1)}, s32[1024]{0:T(1024)}, u32[]{:S(2)}) copy-start(s32[1024]{0:T(1024)} %param.27) | copy-start | bytes 12292
  7.2 88.5 %all-gather.12.cloned.1.call-start = ((), (), s32[]{:S(2)}) async-start(), calls=%async_computation.15 | async-start | bytes 1880064 | tf_op jit(solution)/shard_map/all_gather | solution.py:168
  7.9 87.8 %all-gather.22.cloned.1.call-start = ((), (), s32[]{:S(2)}) async-start(), calls=%async_computation.22 | async-start | bytes 2359296 | tf_op jit(solution)/shard_map/all_gather | solution.py:191
  64.6 56.5 %all-gather.14.cloned.1.call-start = ((), (), s32[]{:S(2)}) async-start(), calls=%async_computation.16 | async-start | bytes 2359296 | tf_op jit(solution)/shard_map/all_gather | solution.py:191
  64.7 7.2 copy-start.54
  64.7 31.0 %copy-start.83 = (f32[3,384]{1,0:T(4,128)S(1)}, f32[3,384]{1,0:T(4,128)}, u32[]{:S(2)}) copy-start(f32[3,384]{1,0:T(4,128)} %param.29) | copy-start | bytes 13828
  71.1 67.3 %copy-start.42 = (f32[1024,32]{0,1:T(8,128)}, f32[1024,32]{0,1:T(8,128)S(1)}, u32[]{:S(2)}) copy-start(f32[1024,32]{0,1:T(8,128)S(1)} %get-tuple-element.931) | copy-start | bytes 393220
  71.1 67.3 %copy-start.44 = (f32[1024,32]{0,1:T(8,128)}, f32[1024,32]{0,1:T(8,128)S(1)}, u32[]{:S(2)}) copy-start(f32[1024,32]{0,1:T(8,128)S(1)} %get-tuple-element.932) | copy-start | bytes 393220
  71.2 181.2 %reduce-scatter.16.cloned.1.call-start = ((), (), s32[]{:S(2)}) async-start(), calls=%async_computation.23 | async-start | bytes 4718592 | tf_op jit(solution)/shard_map/reduce_scatter | solution.py:195
  100.2 21.0 %copy-start.76 = (bf16[3,768,384]{2,1,0:T(8,128)(2,1)S(1)}, bf16[3,768,384]{2,1,0:T(8,128)(2,1)}, u32[]{:S(2)}) copy-start(bf16[3,768,384]{2,1,0:T(8,128)(2,1)} %all-gather.12.cloned.1.call-done) | copy-start | bytes 5308420
  201.8 93.5 %reduce-scatter.12.cloned.1.call-start = ((), (), s32[]{:S(2)}) async-start(), calls=%async_computation.17 | async-start | bytes 4718592 | tf_op jit(solution)/shard_map/reduce_scatter | solution.py:195
  208.4 38.9 %copy-start.16 = (bf16[384,768]{0,1:T(8,128)(2,1)S(1)}, bf16[384,768]{0,1:T(8,128)(2,1)}, u32[]{:S(2)}) copy-start(bf16[384,768]{0,1:T(8,128)(2,1)} %all_gather.50) | copy-start | bytes 1769476
  251.7 43.6 %copy-start.71 = (f32[768]{0:T(1024)S(1)}, f32[768]{0:T(1024)}, u32[]{:S(2)}) copy-start(f32[768]{0:T(1024)} %param.31) | copy-start | bytes 9220
  251.8 88.0 %all-gather.18.cloned.1.call-start = ((), (), s32[]{:S(2)}) async-start(), calls=%async_computation.19 | async-start | bytes 2506752 | tf_op jit(solution)/shard_map/all_gather | solution.py:172
  252.3 115.5 %all-gather.24.cloned.1.call-start = ((), (), s32[]{:S(2)}) async-start(), calls=%async_computation.24 | async-start | bytes 2359296 | tf_op jit(solution)/shard_map/all_gather | solution.py:191
  300.5 96.6 %all-gather.16.cloned.1.call-start = ((), (), s32[]{:S(2)}) async-start(), calls=%async_computation.18 | async-start | bytes 2359296 | tf_op jit(solution)/shard_map/all_gather | solution.py:191
  301.3 140.5 %all-gather.20.cloned.1.call-start = ((), (), s32[]{:S(2)}) async-start(), calls=%async_computation.20 | async-start | bytes 2506752 | tf_op jit(solution)/shard_map/all_gather | solution.py:173
  302.0 95.1 %copy-start.82 = (f32[1536]{0:T(1024)S(1)}, f32[1536]{0:T(1024)}, u32[]{:S(2)}) copy-start(f32[1536]{0:T(1024)} %param.35) | copy-start | bytes 18436
  302.0 195.8 %reduce-scatter.14.cloned.1.call-start = ((), (), s32[]{:S(2)}) async-start(), calls=%async_computation.21 | async-start | bytes 4718592 | tf_op jit(solution)/shard_map/reduce_scatter | solution.py:195
  448.8 88.1 %reduce-scatter.18.cloned.1.call-start = ((), (), s32[]{:S(2)}) async-start(), calls=%async_computation.25 | async-start | bytes 4718592 | tf_op jit(solution)/shard_map/reduce_scatter | solution.py:195
  458.5 36.4 %copy-start.53 = (f32[768]{0:T(1024)S(1)}, f32[768]{0:T(1024)}, u32[]{:S(2)}) copy-start(f32[768]{0:T(1024)} %param.38) | copy-start | bytes 9220
  458.5 36.4 %all-to-all-start.2 = ((bf16[2,16,32,768]{3,2,0,1:T(8,128)(2,1)}), bf16[2,16,32,768]{3,2,0,1:T(8,128)(2,1)}, u32[]{:S(2)}, u32[]{:S(2)}) async-start(bf16[2,16,32,768]{3,2,0,1:T(8,128)(2,1)} %copy.101), calls=%async_computation.6 | async-start | bytes 3145728 | tf_op jit(solution)/shard_map/all_to_all | solution.py:244
  463.1 73.8 %copy-start.72 = (f32[768]{0:T(1024)S(1)}, f32[768]{0:T(1024)}, u32[]{:S(2)}) copy-start(f32[768]{0:T(1024)} %param.37) | copy-start | bytes 9220
  463.1 112.3 %all-gather.26.cloned.1.call-start = ((), (), s32[]{:S(2)}) async-start(), calls=%async_computation.26 | async-start | bytes 2359296 | tf_op jit(solution)/shard_map/all_gather | solution.py:199
  548.1 56.1 %all-gather.30.cloned.1.call-start = ((), (), s32[]{:S(2)}) async-start(), calls=%async_computation.30 | async-start | bytes 2359296 | tf_op jit(solution)/shard_map/all_gather | solution.py:199
  548.9 83.6 %reduce-scatter.20.cloned.1.call-start = ((), (), s32[]{:S(2)}) async-start(), calls=%async_computation.27 | async-start | bytes 2359296 | tf_op jit(solution)/shard_map/reduce_scatter | solution.py:203
  575.4 9.4 copy-start.74
  588.6 72.1 %reduce-scatter.24.cloned.1.call-start = ((), (), s32[]{:S(2)}) async-start(), calls=%async_computation.31 | async-start | bytes 2359296 | tf_op jit(solution)/shard_map/reduce_scatter | solution.py:203
  604.2 9.4 copy-start.75
  617.3 76.8 %all-gather.28.cloned.1.call-start = ((), (), s32[]{:S(2)}) async-start(), calls=%async_computation.28 | async-start | bytes 2359296 | tf_op jit(solution)/shard_map/all_gather | solution.py:199
  666.7 115.0 %all-gather.32.cloned.1.call-start = ((), (), s32[]{:S(2)}) async-start(), calls=%async_computation.32 | async-start | bytes 2359296 | tf_op jit(solution)/shard_map/all_gather | solution.py:199
  669.3 24.7 %copy-start.17 = (bf16[384,768]{0,1:T(8,128)(2,1)S(1)}, bf16[384,768]{0,1:T(8,128)(2,1)}, u32[]{:S(2)}) copy-start(bf16[384,768]{0,1:T(8,128)(2,1)} %all_gather.50) | copy-start | bytes 1769476
  671.5 290.0 %reduce-scatter.22.cloned.1.call-start = ((), (), s32[]{:S(2)}) async-start(), calls=%async_computation.29 | async-start | bytes 2359296 | tf_op jit(solution)/shard_map/reduce_scatter | solution.py:203
  709.3 5.9 slice-start.1
  734.4 5.4 slice-start
  734.4 5.9 slice-start.1
  759.6 5.9 slice-start.1
  797.6 5.4 slice-start.2
  797.6 5.9 slice-start.3
  822.2 5.9 slice-start.3
  846.9 5.9 slice-start.3
  880.3 7.9 copy-start.22
  880.3 7.9 copy-start.23
  894.4 5.8 copy-start.20
  894.4 5.8 copy-start.21
  900.1 63.7 %reduce-scatter.26.cloned.1.call-start = ((), (), s32[]{:S(2)}) async-start(), calls=%async_computation.33 | async-start | bytes 2359296 | tf_op jit(solution)/shard_map/reduce_scatter | solution.py:203
  908.1 5.5 copy-start.31
  908.1 5.6 copy-start.24
  908.1 5.6 copy-start.26
  913.7 217.6 %all-reduce.4.cloned.1.call-start = ((), (), s32[]{:S(2)}) async-start(), calls=%async_computation.37 | async-start | bytes 9437184
  924.1 269.3 %reduce-scatter.28.cloned.1.call-start = ((), (), s32[]{:S(2)}) async-start(), calls=%async_computation.34 | async-start | bytes 1253376 | tf_op jit(solution)/shard_map/reduce_scatter | solution.py:361
  931.1 341.4 %reduce-scatter.32.cloned.1.call-start = ((), (), s32[]{:S(2)}) async-start(), calls=%async_computation.36 | async-start | bytes 5013504 | tf_op jit(solution)/shard_map/reduce_scatter | solution.py:363
  940.5 411.3 %reduce-scatter.30.cloned.1.call-start = ((), (), s32[]{:S(2)}) async-start(), calls=%async_computation.35 | async-start | bytes 5013504 | tf_op jit(solution)/shard_map/reduce_scatter | solution.py:362
  955.4 6.0 copy-start.13
  955.4 54.8 %all-to-all-start.1 = ((bf16[2,1,512,768]{3,0,1,2:T(2,128)(2,1)}), bf16[2,1,512,768]{3,0,1,2:T(2,128)(2,1)}, u32[]{:S(2)}, u32[]{:S(2)}) async-start(bf16[2,1,512,768]{3,0,1,2:T(2,128)(2,1)} %copy.99), calls=%async_computation.5 | async-start | bytes 3145728 | tf_op jit(solution)/shard_map/all_to_all | solution.py:354
  968.2 50.3 %copy-start.84 = (u32[32]{0:T(128)S(1)}, u32[32]{0:T(128)}, u32[]{:S(2)}) copy-start(u32[32]{0:T(128)} %constant.499) | copy-start | bytes 388
  968.2 51.5 %copy-start.56 = (f32[768]{0:T(1024)S(1)}, f32[768]{0:T(1024)}, u32[]{:S(2)}) copy-start(f32[768]{0:T(1024)} %get-tuple-element.768) | copy-start | bytes 9220
  968.2 51.5 %copy-start.57 = (f32[768]{0:T(1024)S(1)}, f32[768]{0:T(1024)}, u32[]{:S(2)}) copy-start(f32[768]{0:T(1024)} %get-tuple-element.769) | copy-start | bytes 9220
  968.2 51.6 %copy-start.62 = (f32[768]{0:T(1024)S(1)}, f32[768]{0:T(1024)}, u32[]{:S(2)}) copy-start(f32[768]{0:T(1024)} %get-tuple-element.758) | copy-start | bytes 9220
  968.2 51.6 %copy-start.63 = (f32[768]{0:T(1024)S(1)}, f32[768]{0:T(1024)}, u32[]{:S(2)}) copy-start(f32[768]{0:T(1024)} %get-tuple-element.765) | copy-start | bytes 9220
  968.2 51.6 %copy-start.68 = (f32[1536]{0:T(1024)S(1)}, f32[1536]{0:T(1024)}, u32[]{:S(2)}) copy-start(f32[1536]{0:T(1024)} %get-tuple-element.943) | copy-start | bytes 18436
  968.2 51.6 %copy-start.69 = (f32[1536]{0:T(1024)S(1)}, f32[1536]{0:T(1024)}, u32[]{:S(2)}) copy-start(f32[1536]{0:T(1024)} %get-tuple-element.945) | copy-start | bytes 18436
  1010.2 122.8 %all-to-all-start.3 = ((bf16[2,1,512,768]{3,0,1,2:T(2,128)(2,1)}), bf16[2,1,512,768]{3,0,1,2:T(2,128)(2,1)S(1)}, u32[]{:S(2)}, u32[]{:S(2)}) async-start(bf16[2,1,512,768]{3,0,1,2:T(2,128)(2,1)} %copy.110), calls=%async_computation.11 | async-start | bytes 3145728 | tf_op jit(solution)/shard_map/all_to_all | solution.py:355
  1023.4 328.3 %copy-start.1 = (s32[1024]{0:T(1024)S(1)}, s32[1024]{0:T(1024)}, u32[]{:S(2)}) copy-start(s32[1024]{0:T(1024)} %param.27) | copy-start | bytes 12292
  (66 other events, 233.7 us)
Sparse Core Ops, SparseCore 0:
  10.3 49.4 all-gather.11
  64.7 27.5 all-gather.21
  93.9 27.1 all-gather.13
  201.9 43.4 reduce-scatter.15
  251.8 43.4 reduce-scatter.11
  297.4 42.3 all-gather.17
  341.9 25.8 all-gather.23
  369.9 27.1 all-gather.15
  399.5 42.3 all-gather.19
  449.0 42.1 reduce-scatter.13
  493.4 43.4 reduce-scatter.17
  548.2 27.1 all-gather.25
  577.0 27.1 all-gather.29
  606.3 26.1 reduce-scatter.19
  634.5 26.1 reduce-scatter.23
  666.8 27.1 all-gather.27
  695.4 27.1 all-gather.31
  900.2 26.1 reduce-scatter.21
  928.6 26.1 reduce-scatter.25
  958.3 172.9 all-reduce.3
  1135.5 57.9 reduce-scatter.27
  1197.9 74.5 reduce-scatter.31
  1276.9 74.7 reduce-scatter.29
where the time goes:
time: 1370 us; the launch traced here: 1360 us
  waiting for transfers between devices  638 us (47%)
  matrix products  270 us (20%)
  local copies, waits for them, and re-layouts  156 us (11%)
  blocking collectives  142 us (10%)
  other arithmetic  115 us (8%)
  starting transfers between devices  20.2 us (1%)
  between operations  16.3 us (1%)
    reduce_scatter x4, waiting for transfers between devices, collect_forward(): return lax.psum_scatter(terms, 'tensor', scatter_dimension=0, tiled=True)  82 us
    reduce_scatter x1, waiting for transfers between devices, body(): lax.psum_scatter(grad_wu, 'dp', scatter_dimension=0, tiled=True)  79.3 us
    reduce_scatter x1, waiting for transfers between devices, body(): lax.psum_scatter(grad_wd, 'dp', scatter_dimension=1, tiled=True)  79 us
    all_gather x4, waiting for transfers between devices, spread_forward(): return lax.all_gather(rows_val, 'tensor', axis=0, tiled=True)  69 us
    all_gather x4, waiting for transfers between devices, spread_backward(): return lax.all_gather(rows_val, 'tensor', axis=0, tiled=True)  64.6 us
    psum x1, blocking collectives, body(): lax.psum((bias_q_full, grad_bo, grad_gain_one, grad_shift_one, bias_u_ful...  64.2 us
    reduce_scatter x1, waiting for transfers between devices, body(): lax.psum_scatter(grad_wo, 'dp', scatter_dimension=1, tiled=True)  59.1 us
    all_to_all x1, blocking collectives, body(): lax.all_to_all(tokens.reshape(batches, dp_size, stripe, features), 'dp',...  53.8 us
  transfers between devices with their start and end apart: 26, of which 18 were waited for; matrix products, arithmetic and copies ran while one was open for 22% of the time, Pallas kernels for 0%

commit v1 on v0

v1 whole, which is shorter than its diff:
```python
import functools

import jax
import jax.numpy as jnp
from jax import lax
from jax.experimental import pallas as pl
from jax.experimental.pallas import tpu as pltpu
from jax.sharding import PartitionSpec as P

HD = 64
LANES = 128
NORM_EPS = 1e-12
ROPE_BASE = 10000.0
MASK_FILL = -1e30
SCORE_SCALE = 0.125
INV_ROOT_TWO = 0.7071067811865476
INV_ROOT_TAU = 0.3989422804014327
AXES = ("dp", "tensor")
BF = jnp.bfloat16
F32 = jnp.float32
VMEM_BYTES = 60 * 1024 * 1024


def dot(a, b, dims):
    return lax.dot_general(a, b, (dims, ((), ())), preferred_element_type=F32)


NN = ((1,), (0,))
NT = ((1,), (1,))
TN = ((0,), (0,))


def rope_tables(positions):
    steps = (jnp.arange(LANES) % HD // 2).astype(F32)
    inverse = jnp.power(ROPE_BASE, -2.0 * steps / HD)
    angles = positions.astype(F32)[:, None] * inverse[None, :]
    return jnp.cos(angles), jnp.sin(angles)


def turn(values, cos_table, sine_table):
    lane = lax.broadcasted_iota(jnp.int32, values.shape, 1)
    swapped = jnp.where(
        lane % 2 == 0, -pltpu.roll(values, LANES - 1, 1), pltpu.roll(values, 1, 1)
    )
    return values * cos_table + swapped * sine_table


def project_kernel(x_ref, w_ref, b_ref, cos_ref, sine_ref, out_ref):
    kind = pl.program_id(0)
    raw = dot(x_ref[...], w_ref[0], NN) + b_ref[0]

    @pl.when(kind < 2)
    def _():
        for part in range(raw.shape[1] // LANES):
            cols = slice(part * LANES, (part + 1) * LANES)
            out_ref[0, :, cols] = turn(raw[:, cols], cos_ref[...], sine_ref[...]).astype(BF)

    @pl.when(kind == 2)
    def _():
        out_ref[0] = raw.astype(BF)


def project(x, w, b, cos_table, sine_table):
    rows, features = x.shape
    block = 256
    return pl.pallas_call(
        project_kernel,
        grid=(3, features // block),
        in_specs=[
            pl.BlockSpec((rows, features), lambda p, c: (0, 0)),
            pl.BlockSpec((1, features, block), lambda p, c: (p, 0, c)),
            pl.BlockSpec((1, 1, block), lambda p, c: (p, 0, c)),
            pl.BlockSpec((rows, LANES), lambda p, c: (0, 0)),
            pl.BlockSpec((rows, LANES), lambda p, c: (0, 0)),
        ],
        out_specs=pl.BlockSpec((1, rows, block), lambda p, c: (p, 0, c)),
        out_shape=jax.ShapeDtypeStruct((3, rows, features), BF),
        compiler_params=pltpu.CompilerParams(vmem_limit_bytes=VMEM_BYTES),
        name="project",
    )(x, w, b, cos_table, sine_table)


def head_masks(rows):
    lane = lax.broadcasted_iota(jnp.int32, (rows, LANES), 1)
    return lane


def pair_operands(q, k, bias, lane, head):
    inside = lane // HD == head
    spare = lane == (1 - head) * HD
    zero = jnp.zeros_like(q)
    q_head = jnp.where(inside, q, jnp.where(spare, jnp.ones_like(q), zero))
    k_head = jnp.where(inside, k, jnp.where(spare, bias, zero))
    return q_head, k_head


def attend_kernel(q_ref, k_ref, v_ref, bias_ref, ctx_ref, lse_ref, *, chunk):
    rows = q_ref.shape[1]
    lane = lax.broadcasted_iota(jnp.int32, (rows, LANES), 1)
    q = q_ref[0] * jnp.asarray(SCORE_SCALE, BF)
    k = k_ref[0]
    v_turned = v_ref[0].T
    bias = bias_ref[...]
    for part in range(rows // chunk):
        span = slice(part * chunk, (part + 1) * chunk)
        outs = []
        for head in range(2):
            q_head, k_head = pair_operands(q, k, bias, lane, head)
            scores = dot(k_head, q_head[span], NT)
            top = jnp.max(scores, axis=0, keepdims=True)
            expo = jnp.exp(scores - top)
            total = jnp.sum(expo, axis=0, keepdims=True)
            mixed = dot(v_turned[head * HD : (head + 1) * HD], expo.astype(BF), NN)
            outs.append(mixed / total)
            lse_ref[0, head : head + 1, span] = top + jnp.log(total)
        ctx_ref[span, :] = jnp.concatenate(outs, axis=0).T.astype(BF)


def attend(qkv, bias):
    _, rows, features = qkv.shape
    pairs = features // LANES
    chunk = 256

    def spec(which):
        return pl.BlockSpec((1, rows, LANES), lambda h: (which, 0, h))

    return pl.pallas_call(
        functools.partial(attend_kernel, chunk=chunk),
        grid=(pairs,),
        in_specs=[spec(0), spec(1), spec(2), pl.BlockSpec((rows, LANES), lambda h: (0, 0))],
        out_specs=[
            pl.BlockSpec((rows, LANES), lambda h: (0, h)),
            pl.BlockSpec((1, 2, rows), lambda h: (h, 0, 0)),
        ],
        out_shape=[
            jax.ShapeDtypeStruct((rows, features), BF),
            jax.ShapeDtypeStruct((pairs, 2, rows), F32),
        ],
        compiler_params=pltpu.CompilerParams(vmem_limit_bytes=VMEM_BYTES),
        name="attend",
    )(qkv, qkv, qkv, bias)


def attend_back_kernel(
    q_ref, k_ref, v_ref, bias_ref, ctx_ref, grad_ref, lse_ref, cos_ref, sine_ref, out_ref,
    dk_ref, dv_ref, *, chunk
):
    rows = q_ref.shape[1]
    lane = lax.broadcasted_iota(jnp.int32, (rows, LANES), 1)
    q = q_ref[0] * jnp.asarray(SCORE_SCALE, BF)
    k = k_ref[0]
    v = v_ref[0]
    grad = grad_ref[...]
    bias = bias_ref[...]
    k_turned = k.T
    zero = jnp.zeros_like(grad)
    dots = (grad.astype(F32) * ctx_ref[...].astype(F32)).T
    for part in range(rows // chunk):
        span = slice(part * chunk, (part + 1) * chunk)
        dq_parts = []
        dk_sum = None
        dv_sum = None
        for head in range(2):
            q_head, k_head = pair_operands(q, k, bias, lane, head)
            inside = lane // HD == head
            g_head = jnp.where(inside, grad, zero)[span]
            q_only = jnp.where(inside, q, zero)[span]
            scores = dot(k_head, q_head[span], NT)
            prob = jnp.exp(scores - lse_ref[0, head : head + 1, span])
            g_prob = dot(v, g_head, NT)
            inner = jnp.sum(dots[head * HD : (head + 1) * HD, span], axis=0, keepdims=True)
            g_score = (prob * (g_prob - inner)).astype(BF)
            dv = dot(prob.astype(BF), g_head, NN)
            dk = dot(g_score, q_only, NN)
            dq_parts.append(dot(k_turned[head * HD : (head + 1) * HD], g_score, NN))
            dk_sum = dk if dk_sum is None else dk_sum + dk
            dv_sum = dv if dv_sum is None else dv_sum + dv
        dq = jnp.concatenate(dq_parts, axis=0).T * SCORE_SCALE
        out_ref[0, span, :] = turn(dq, cos_ref[span, :], -sine_ref[span, :]).astype(BF)
        if part == 0:
            dk_ref[...] = dk_sum
            dv_ref[...] = dv_sum
        else:
            dk_ref[...] += dk_sum
            dv_ref[...] += dv_sum
    out_ref[1] = turn(dk_ref[...], cos_ref[...], -sine_ref[...]).astype(BF)
    out_ref[2] = dv_ref[...].astype(BF)


def attend_back(qkv, bias, context, grad_ctx, lse, cos_table, sine_table):
    _, rows, features = qkv.shape
    pairs = features // LANES
    chunk = 256

    def spec(which):
        return pl.BlockSpec((1, rows, LANES), lambda h: (which, 0, h))

    fixed = pl.BlockSpec((rows, LANES), lambda h: (0, 0))
    cols = pl.BlockSpec((rows, LANES), lambda h: (0, h))
    return pl.pallas_call(
        functools.partial(attend_back_kernel, chunk=chunk),
        grid=(pairs,),
        in_specs=[
            spec(0), spec(1), spec(2), fixed, cols, cols,
            pl.BlockSpec((1, 2, rows), lambda h: (h, 0, 0)), fixed, fixed,
        ],
        out_specs=pl.BlockSpec((3, rows, LANES), lambda h: (0, 0, h)),
        out_shape=jax.ShapeDtypeStruct((3, rows, features), BF),
        scratch_shapes=[pltpu.VMEM((rows, LANES), F32), pltpu.VMEM((rows, LANES), F32)],
        compiler_params=pltpu.CompilerParams(vmem_limit_bytes=VMEM_BYTES),
        name="attend_back",
    )(qkv, qkv, qkv, bias, context, grad_ctx, lse, cos_table, sine_table)


def normalize(hidden, gain_vec, shift_vec):
    row_mean = jnp.mean(hidden, axis=-1, keepdims=True)
    centred = hidden - row_mean
    row_var = jnp.mean(centred * centred, axis=-1, keepdims=True)
    inv_std = lax.rsqrt(row_var + NORM_EPS)
    normed = centred * inv_std
    return (normed * gain_vec + shift_vec, normed, inv_std)


def normalize_back(grad_unit, normed, inv_std):
    first_mean = jnp.mean(grad_unit, axis=-1, keepdims=True)
    second_mean = jnp.mean(grad_unit * normed, axis=-1, keepdims=True)
    return inv_std * (grad_unit - first_mean - normed * second_mean)


def gelu_slope(up_proj):
    return (
        0.5 * (1.0 + lax.erf(up_proj * INV_ROOT_TWO))
        + up_proj * jnp.exp(-0.5 * up_proj * up_proj) * INV_ROOT_TAU
    )


def layer(rows, cotangent, place, length, cos_table, sine_table, params):
    (w_qkv, b_qkv, w_out_t, b_out, gain_one, shift_one, w_up, b_up, w_down_t, b_down,
     gain_two, shift_two) = params
    live = place < length
    bias = jnp.broadcast_to(jnp.where(live, 0.0, MASK_FILL).astype(BF)[:, None], (rows.shape[0], LANES))
    qkv = project(rows, w_qkv, b_qkv[:, None, :], cos_table, sine_table)
    context, lse = attend(qkv, bias)
    first_sum = rows.astype(F32) + dot(context, w_out_t, NT) + b_out
    normed_one, unit_one, inv_one = normalize(first_sum, gain_one, shift_one)
    mid = normed_one.astype(BF)
    up_proj = dot(mid, w_up, NN) + b_up
    activated = jax.nn.gelu(up_proj, approximate=False).astype(BF)
    second_sum = normed_one + dot(activated, w_down_t, NT) + b_down
    result, unit_two, inv_two = normalize(second_sum, gain_two, shift_two)
    result = result.astype(BF)

    grad_out = jnp.where(live[:, None], cotangent.astype(F32), 0.0)
    g_gain_two = jnp.sum(grad_out * unit_two, axis=0)
    g_shift_two = jnp.sum(grad_out, axis=0)
    grad_second = normalize_back(grad_out * gain_two, unit_two, inv_two)
    g_b_down = jnp.sum(grad_second, axis=0)
    grad_down = grad_second.astype(BF)
    g_w_down_t = dot(grad_down, activated, TN)
    grad_up = (dot(grad_down, w_down_t, NN) * gelu_slope(up_proj)).astype(BF)
    g_b_up = jnp.sum(grad_up.astype(F32), axis=0)
    g_w_up = dot(mid, grad_up, TN)
    grad_mid = grad_second + dot(grad_up, w_up, NT)
    g_gain_one = jnp.sum(grad_mid * unit_one, axis=0)
    g_shift_one = jnp.sum(grad_mid, axis=0)
    grad_first = normalize_back(grad_mid * gain_one, unit_one, inv_one)
    g_b_out = jnp.sum(grad_first, axis=0)
    grad_attn = grad_first.astype(BF)
    g_w_out_t = dot(grad_attn, context, TN)
    grad_ctx = dot(grad_attn, w_out_t, NN).astype(BF)
    grad_raw = attend_back(qkv, bias, context, grad_ctx, lse, cos_table, sine_table)
    g_b_qkv = jnp.sum(grad_raw.astype(F32), axis=1)
    g_w_qkv = [dot(rows, grad_raw[i], TN) for i in range(3)]
    in_sum = sum(dot(grad_raw[i], w_qkv[i], NT) for i in range(3))
    grad_rows = (grad_first + in_sum).astype(BF)
    weights = (g_w_qkv, g_w_out_t, g_w_up, g_w_down_t)
    small = (g_b_qkv, g_b_out, g_gain_one, g_shift_one, g_b_up, g_b_down, g_gain_two, g_shift_two)
    return result, grad_rows, weights, small


def body(
    tokens, out_grad, lengths, order, w_qkv, b_qkv, w_out, b_out, norm1_gain, norm1_bias,
    w_up, b_up, w_down, b_down, norm2_gain, norm2_bias,
):
    dp_size = lax.axis_size("dp")
    tp_size = lax.axis_size("tensor")
    devices = dp_size * tp_size
    me = lax.axis_index(AXES)
    stored, stripe, features = tokens.shape
    batches = stored // devices
    slot = devices * stripe
    depth = w_qkv.shape[1]
    cols = w_qkv.shape[2]
    units = w_up.shape[1]

    def deal(rows_val):
        return lax.all_to_all(
            rows_val.reshape(batches, devices, stripe, features), AXES,
            split_axis=1, concat_axis=2, tiled=True,
        ).reshape(batches, slot, features)

    def give_back(rows_val):
        return lax.all_to_all(
            rows_val.reshape(batches, 1, slot, features), AXES,
            split_axis=2, concat_axis=1, tiled=True,
        ).reshape(stored, stripe, features)

    inputs = deal(tokens)
    attn_shard = jnp.concatenate([w_qkv.reshape(3 * depth, cols), w_out.T], axis=0)
    attn_all = lax.all_gather(attn_shard, AXES, axis=0, tiled=False)
    attn_all = attn_all.reshape(dp_size, tp_size, 4, depth, cols)
    attn_all = attn_all.transpose(2, 0, 3, 1, 4).reshape(4, features, features)
    ffn_shard = jnp.stack([w_up, w_down.T], axis=0)
    ffn_all = lax.all_gather(ffn_shard, AXES, axis=0, tiled=False)
    ffn_all = ffn_all.reshape(dp_size, tp_size, 2, depth, units)
    ffn_all = ffn_all.transpose(2, 0, 3, 1, 4).reshape(2, features, tp_size * units)
    b_qkv_all = lax.all_gather(b_qkv, "tensor", axis=1, tiled=True)
    b_up_all = lax.all_gather(b_up, "tensor", axis=0, tiled=True)
    cotangents = deal(out_grad)
    cos_table, sine_table = rope_tables(order)
    params = (attn_all[:3], b_qkv_all, attn_all[3], b_out, norm1_gain, norm1_bias,
              ffn_all[0], b_up_all, ffn_all[1], b_down, norm2_gain, norm2_bias)
    results, input_grads, weights, small = [], [], None, None
    for micro in range(batches):
        length = lax.dynamic_index_in_dim(lengths, micro * devices + me, 0, keepdims=False)
        result, grad_rows, weights_one, small_one = layer(
            inputs[micro], cotangents[micro], order, length, cos_table, sine_table, params
        )
        results.append(result)
        input_grads.append(grad_rows)
        if weights is None:
            weights, small = weights_one, small_one
        else:
            weights, small = jax.tree.map(jnp.add, (weights, small), (weights_one, small_one))
    mixed = give_back(jnp.stack(results, axis=0))
    grad_tokens = give_back(jnp.stack(input_grads, axis=0))

    def scatter(parts):
        laid = [
            p.astype(BF).reshape(dp_size, depth, tp_size, -1).transpose(0, 2, 1, 3) for p in parts
        ]
        laid = jnp.stack(laid, axis=2).reshape(devices, len(parts), depth, -1)
        return lax.psum_scatter(laid, AXES, scatter_dimension=0, tiled=False).astype(F32)

    g_qkv, g_out_t, g_up, g_down_t = weights
    ffn_sum = scatter([g_up, g_down_t])
    attn_sum = scatter(list(g_qkv) + [g_out_t])
    sizes = [s.size for s in small]
    packed = jnp.concatenate([s.reshape(-1) for s in small]).reshape(-1, LANES)
    summed = jnp.sum(lax.all_gather(packed, AXES, axis=0, tiled=False), axis=0).reshape(-1)
    small_sums, start = [], 0
    for s, size in zip(small, sizes):
        small_sums.append(summed[start : start + size].reshape(s.shape))
        start += size
    return (
        mixed, grad_tokens, attn_sum[:3], small_sums[0], attn_sum[3].T, small_sums[1],
        small_sums[2], small_sums[3], ffn_sum[0], small_sums[4], ffn_sum[1].T, small_sums[5],
        small_sums[6], small_sums[7],
    )


def solution(mesh):
    rows = P(None, AXES, None)
    in_specs = (
        rows, rows, P(), P(), P(None, "dp", "tensor"), P(None, "tensor"), P("tensor", "dp"), P(),
        P(), P(), P("dp", "tensor"), P("tensor"), P("tensor", "dp"), P(), P(), P(),
    )
    out_specs = (
        rows, rows, P(None, "dp", "tensor"), P(), P("tensor", "dp"), P(), P(), P(),
        P("dp", "tensor"), P(), P("tensor", "dp"), P(), P(), P(),
    )
    return jax.shard_map(body, mesh=mesh, in_specs=in_specs, out_specs=out_specs, check_vma=False)
```

time: 1370 us -> 743 us (0.54)
  waiting for transfers between devices: 638 us -> 226 us
  matrix products: 270 us -> 109 us
  Pallas kernels: 0 us -> 86.1 us
  blocking collectives: 142 us -> 74.6 us
  other arithmetic: 115 us -> 55.8 us
    reduce_scatter x11 -> x1, waiting for transfers between devices: 340 us -> 118 us  [scatter(): lax.psum_scatter(laid, AXES, scatter_dimension=0, tiled=False).astype(F32)]
    dot_general x66 -> x15, matrix products: 270 us -> 109 us  [dot(): return lax.dot_general(a, b, (dims, ((), ())), preferred_element_type=F32)]
    all_gather x11 -> x3, waiting for transfers between devices: 183 us -> 64.7 us  [the longest x1 58.7 us: body(): lax.all_gather(packed, AXES, axis=0, tiled=False)]
    pallas_call x0 -> x3, Pallas kernels: none -> 86.1 us  [the longest x1 37.1 us: attend(): pl.pallas_call(functools.partial(attend_kernel, chunk=chunk), grid=(pairs...]
    psum x1 -> x0, blocking collectives: 64.2 us -> none  [body(): lax.psum((bias_q_full, grad_bo, grad_gain_one, grad_shift_one, bias_u_ful...]
    all_to_all x3, waiting for transfers between devices: 68.5 us -> 30.3 us  [the longest x2 30.3 us: give_back(): lax.all_to_all(rows_val.reshape(batches, 1, slot, features), AXES, split_...]
    unnamed x24 -> x6, waiting for transfers between devices: 46.9 us -> 12.3 us
    another operation x10 -> x3, other arithmetic: 46.1 us -> 12.6 us  [the longest x2 10.8 us: scatter(): laid = jnp.stack(laid, axis=2).reshape(devices, len(parts), depth, -1)]
  transfers between devices with their start and end apart: 26 -> 8, of which waited for: 18 -> 6; matrix products, arithmetic and copies ran while one was open for 22% -> 24% of each run, Pallas kernels for 0% -> 7%
where the time goes in v1:
time: 743 us; the launch traced here: 733 us
  waiting for transfers between devices  226 us (30%)
  local copies, waits for them, and re-layouts  154 us (21%)
  matrix products  109 us (15%)
  Pallas kernels  86.1 us (12%)
  blocking collectives  74.6 us (10%)
  other arithmetic  55.8 us (8%)
  between operations  14.7 us (2%)
  starting transfers between devices  13 us (2%)
    reduce_scatter x1, waiting for transfers between devices, scatter(): lax.psum_scatter(laid, AXES, scatter_dimension=0, tiled=False).astype(F32)  118 us
    dot_general x15, matrix products, dot(): return lax.dot_general(a, b, (dims, ((), ())), preferred_element_type=F32)  109 us
    all_gather x1, waiting for transfers between devices, body(): lax.all_gather(packed, AXES, axis=0, tiled=False)  58.7 us
    all_to_all x1, blocking collectives, deal(): lax.all_to_all(rows_val.reshape(batches, devices, stripe, features), AXES...  54.3 us
    unnamed x99, local copies, waits for them, and re-layouts  42.3 us
    pallas_call x1, Pallas kernels, attend(): pl.pallas_call(functools.partial(attend_kernel, chunk=chunk), grid=(pairs...  37.1 us
    pallas_call x1, Pallas kernels, attend_back(): pl.pallas_call(functools.partial(attend_back_kernel, chunk=chunk), grid=(...  36.3 us
    all_to_all x2, waiting for transfers between devices, give_back(): lax.all_to_all(rows_val.reshape(batches, 1, slot, features), AXES, split_...  30.3 us
  transfers between devices with their start and end apart: 8, of which 6 were waited for; matrix products, arithmetic and copies ran while one was open for 24% of the time, Pallas kernels for 7%

profile of v1, /device:TPU:0, one launch (start us, length us, event | category | flops | bytes accessed | tf_op | source)
XLA Modules:
  0.0 733.0 jit_solution(12019444553586394049)
XLA Ops:
  7.2 1.6 pad_maximum_fusion.3
  8.9 1.7 pad_maximum_fusion.2
  10.7 54.3 %all_to_all.16 = bf16[1,32,32,768]{3,2,0,1:T(8,128)(2,1)S(1)} all-to-all(bf16[1,32,32,768]{3,2,0,1:T(8,128)(2,1)} %bitcast.180), channel_id=1, replica_groups=mesh['dp'=16,'tensor'=2] {'dp','tensor'}, dimensions={1} | all-to-all | bytes 3145728 | tf_op jit(solution)/shard_map/all_to_all | solution.py:297
  65.0 3.7 all-to-all-start
  68.7 16.0 %all_gather.23 = f32[3,768]{1,0:T(4,128)S(1)} all-gather(f32[3,384]{1,0:T(4,128)S(1)} %copy-done.26), channel_id=1, replica_groups=mesh['dp'=16,'tensor'=2] {'tensor'}, dimensions={1}, use_global_device_ids=true | all-gather | bytes 13824 | tf_op jit(solution)/shard_map/all_gather | solution.py:317
  86.7 4.4 all-gather.2
  91.1 3.1 multiply_sine_fusion
  95.6 2.8 all-gather.9.cloned.1.call-done
  98.4 2.4 slice.140
  100.8 4.6 copy.80
  105.4 8.9 %slice.110.w_ref = bf16[3,768,768]{2,1,0:T(8,128)(2,1)} reshape(bf16[3,16,48,2,384]{4,3,2,1,0:T(2,128)(2,1)} %copy.80) | data formatting | bytes 7077888 | tf_op jit(solution)/shard_map/slice | solution.py:321
  114.3 4.3 fusion.36
  122.0 12.6 %project.1.q_ref.k_ref.v_ref = bf16[3,1024,768]{2,1,0:T(8,128)(2,1)} custom-call(bf16[1024,768]{1,0:T(8,128)(2,1)} %bitcast.158, bf16[3,768,768]{2,1,0:T(8,128)(2,1)} %slice.110.w_ref, f32[3,1,768]{2,1,0:T(1,128)} %broadcast_in_dim.26.b_ref, f32[1024,128]{1,0:T(8,128)} %get-tuple-element.48.cos_ref, f32[1024,128]{1,0:T(8,128)} %get-tuple-element.47.sine_ref), custom_call_target="tpu_custom_call" | custom-call | tf_op jit(solution)/shard_map/project/pallas_call | solution.py:66
  135.5 37.1 %attend.1 = (bf16[1024,768]{1,0:T(8,128)(2,1)}, f32[6,2,1024]{2,1,0:T(2,128)}) custom-call(bf16[3,1024,768]{2,1,0:T(8,128)(2,1)} %project.1.q_ref.k_ref.v_ref, bf16[3,1024,768]{2,1,0:T(8,128)(2,1)} %project.1.q_ref.k_ref.v_ref, bf16[3,1024,768]{2,1,0:T(8,128)(2,1)} %project.1.q_ref.k_ref.v_ref, bf16[1024,128]{1,0:T(8,128)(2,1)} %broadcast_in_dim.33.bias_ref), custom_call_target="tpu_custom_call" | custom-call | tf_op jit(solution)/shard_map/attend/pallas_call | solution.py:127
  172.6 3.3 fusion.37
  176.0 1.6 copy-done.1
  178.1 3.2 all-gather.11.cloned.1.call-done
  181.3 16.4 %copy.112 = bf16[16,2,2,48,1536]{4,1,3,0,2:T(2,128)(2,1)S(1)} copy(bf16[16,2,2,48,1536]{4,3,2,1,0:T(8,128)(2,1)} %bitcast.157) | data formatting | bytes 18874368 | tf_op jit(solution)/shard_map/reshape | solution.py:315
  197.8 11.3 %fusion.35 = (bf16[1,16,48,2,1536]{4,3,2,1,0:T(2,128)(2,1)S(1)}, bf16[1,16,48,2,1536]{4,3,2,1,0:T(2,128)(2,1)S(1)}) fusion(bf16[2,16,48,2,1536]{4,3,2,1,0:T(2,128)(2,1)S(1)} %bitcast.142), kind=kLoop, calls=%fused_computation.118 | loop fusion | bytes 18874368 | tf_op jit(solution)/shard_map/slice | solution.py:322
  210.3 3.4 copy.105
  213.8 35.5 %fusion.2 = (bf16[1024,3072]{1,0:T(8,128)(2,1)}, f32[1024,3072]{1,0:T(8,128)}) fusion(f32[3072]{0:T(1024)S(1)} %bitcast.193, bf16[768,3072]{1,0:T(8,128)(2,1)S(1)} %bitcast.167, f32[1024,768]{1,0:T(8,128)S(1)} %copy-done.2, f32[768]{0:T(1024)S(1)} %copy-done.34, f32[768]{0:T(1024)S(1)} %copy-done.28, f32[1024]{0:T(1024)S(1)} %add_rsqrt_fusion.1, ...), kind=kOutput, calls=%fused_computation.4 | convolution fusion | flops 5043388416 | bytes 26765312 | tf_op jit(solution)/shard_map/dot_general | solution.py:25
  249.3 7.6 %fusion.38 = (f32[1024]{0:T(1024)S(1)}, f32[1024,768]{1,0:T(8,128)S(1)}) fusion(f32[768]{0:T(1024)S(1)} %copy-done.33, bf16[1024,3072]{1,0:T(8,128)(2,1)} %get-tuple-element.51, bf16[768,3072]{1,0:T(8,128)(2,1)S(1)} %bitcast.169, f32[768]{0:T(1024)S(1)} %copy-done.34, f32[768]{0:T(1024)S(1)} %copy-done.28, f32[1024]{0:T(1024)S(1)} %add_rsqrt_fusion.1, ...), kind=kOutput, calls=%fused_computation.121 | convolution fusion | flops 4837342208 | bytes 17323008 | tf_op jit(solution)/shard_map/dot_general | solution.py:25
  257.5 1.6 multiply_reduce_fusion
  259.1 2.5 fusion.33
  261.6 14.8 %convert_reduce_fusion = (f32[3072]{0:T(1024)}, bf16[1024,3072]{1,0:T(8,128)(2,1)}) fusion(f32[1024,3072]{1,0:T(8,128)} %get-tuple-element.52, f32[3072]{0:T(1024)S(1)} %bitcast.194, bf16[768,3072]{1,0:T(8,128)(2,1)S(1)} %bitcast.170, f32[1024,768]{1,0:T(8,128)S(1)} %get-tuple-element.27), kind=kOutput, calls=%fused_computation.11 | convolution fusion | flops 4873516032 | bytes 26763264 | tf_op jit(solution)/shard_map/dot_general | solution.py:25
  276.4 9.0 %multiply_reduce_fusion.1 = (f32[768]{0:T(1024)}, f32[1024]{0:T(1024)S(1)}, f32[1024]{0:T(1024)S(1)}, f32[768]{0:T(1024)}, f32[1024,768]{1,0:T(8,128)S(1)}) fusion(f32[1024,768]{1,0:T(8,128)S(1)} %copy-done.2, f32[1024]{0:T(1024)S(1)} %add_rsqrt_fusion.1, f32[1024]{0:T(1024)S(1)} %broadcast_multiply_fusion.5, f32[768]{0:T(1024)S(1)} %copy-done.28, ...), kind=kOutput, calls=%fused_computation.35 | convolution fusion | flops 4839698432 | bytes 20472832 | tf_op jit(solution)/shard_map/dot_general | solution.py:25
  285.5 1.7 fusion.34
  287.2 2.6 convolution_convert_fusion.2.grad_ref
  289.8 2.5 convolution_convert_fusion.3
  292.3 36.3 %attend_back.1 = bf16[3,1024,768]{2,1,0:T(8,128)(2,1)} custom-call(bf16[3,1024,768]{2,1,0:T(8,128)(2,1)} %project.1.q_ref.k_ref.v_ref, bf16[3,1024,768]{2,1,0:T(8,128)(2,1)} %project.1.q_ref.k_ref.v_ref, bf16[3,1024,768]{2,1,0:T(8,128)(2,1)} %project.1.q_ref.k_ref.v_ref, bf16[1024,128]{1,0:T(8,128)(2,1)} %broadcast_in_dim.33.bias_ref, ...), custom_call_target="tpu_custom_call" | custom-call | tf_op jit(solution)/shard_map/attend_back/pallas_call | solution.py:200
  328.7 4.0 fusion.21
  332.7 2.5 fusion.22
  335.1 2.5 fusion.23
  340.3 1.6 copy.91
  343.0 1.4 copy.92
  344.5 2.4 copy.93
  346.9 3.6 reshape.255
  351.8 2.5 pad_maximum_fusion.1
  354.6 3.2 convert_reduce_fusion.1
  358.7 10.3 %convolution_convert_fusion.1 = bf16[768,3072]{1,0:T(8,128)(2,1)} fusion(bf16[1024,3072]{1,0:T(8,128)(2,1)} %get-tuple-element.57, f32[1024,768]{1,0:T(8,128)S(1)} %copy-done.3, f32[768]{0:T(1024)S(1)} %copy-done.35, f32[768]{0:T(1024)S(1)} %copy-done.29, f32[1024]{0:T(1024)S(1)} %add_rsqrt_fusion.1, f32[1024]{0:T(1024)S(1)} %broadcast_multiply_fusion.5), kind=kOutput, calls=%fused_computation.31 | convolution fusion | flops 4838129664 | bytes 14170112 | tf_op jit(solution)/shard_map/dot_general | solution.py:25
  369.0 11.7 %reshape.259 = bf16[16,48,2,1536]{3,2,1,0:T(2,128)(2,1)} reshape(bf16[768,3072]{1,0:T(8,128)(2,1)} %convolution_convert_fusion.1) | data formatting | bytes 9437184 | tf_op jit(solution)/shard_map/reshape | solution.py:340
  380.6 5.8 copy.96
  386.4 9.6 %convolution_convert_fusion = bf16[768,3072]{1,0:T(8,128)(2,1)} fusion(bf16[1024,3072]{1,0:T(8,128)(2,1)} %get-tuple-element.51, f32[1024,768]{1,0:T(8,128)S(1)} %copy-done.14), kind=kOutput, calls=%fused_computation.30 | convolution fusion | flops 4834983936 | bytes 14155776 | tf_op jit(solution)/shard_map/dot_general | solution.py:25
  396.1 11.8 %reshape.260 = bf16[16,48,2,1536]{3,2,1,0:T(2,128)(2,1)} reshape(bf16[768,3072]{1,0:T(8,128)(2,1)} %convolution_convert_fusion) | data formatting | bytes 9437184 | tf_op jit(solution)/shard_map/reshape | solution.py:340
  407.9 5.6 copy.97
  413.5 8.3 %pad_maximum_fusion = bf16[32,2,48,1536]{3,2,1,0:T(8,128)(2,1)} fusion(bf16[32,1,48,1536]{3,2,1,0:T(8,128)(2,1)} %bitcast.150, bf16[32,1,48,1536]{3,2,1,0:T(8,128)(2,1)} %bitcast.147), kind=kLoop, calls=%fused_computation.27 | loop fusion | flops 4718592 | bytes 18874368 | tf_op jit(solution)/shard_map/stack | solution.py:342
  421.8 1.6 copy-done.11
  427.0 1.4 fusion.25
  428.4 1.4 fusion.24
  430.3 1.5 fusion.20
  431.8 2.4 copy.113
  434.8 11.6 %reduce.6 = bf16[1024,768]{1,0:T(8,128)(2,1)} reduce(bf16[1024,1,1,768]{3,2,1,0:T(2,128)(2,1)S(1)} %bitcast.153, bf16[]{:T(256)} %broadcast.197), dimensions={1,2}, to_apply=%bitcast.140.reduce_sub_computation | reduce | bytes 3145730
  446.4 4.6 reshape.272
  451.0 4.3 all-to-all-start.3
  455.3 3.8 copy.114
  459.1 11.6 %reduce.5 = bf16[1024,768]{1,0:T(8,128)(2,1)} reduce(bf16[1024,1,1,768]{3,2,1,0:T(2,128)(2,1)S(1)} %bitcast.154, bf16[]{:T(256)} %broadcast.197), dimensions={1,2}, to_apply=%bitcast.141.reduce_sub_computation | reduce | bytes 3145730
  470.7 4.6 reshape.270
  475.3 30.3 %all-to-all-done.3 = bf16[32,2,12288]{2,1,0:T(2,128)(2,1)} async-done(((bf16[32,2,12288]{2,1,0:T(2,128)(2,1)}), bf16[32,2,12288]{2,1,0:T(2,128)(2,1)}, u32[]{:S(2)}, u32[]{:S(2)}) %all-to-all-start.3) | async-done | bytes 1572896 | tf_op jit(solution)/shard_map/all_to_all | solution.py:303
  505.6 4.8 all-to-all-start.1
  510.4 12.2 %all-reduce.3.cloned.1.call-done = bf16[32,4,48,384]{3,2,0,1:T(8,128)(2,1)} async-done(((bf16[32,4,48,384]{3,2,0,1:T(8,128)(2,1)}), bf16[32,4,48,384]{3,2,0,1:T(8,128)(2,1)}) %all-reduce.3.cloned.1.call-update) | async-done | bytes 4718608
  524.9 58.7 %all-gather.7.cloned.1.call-done = f32[32,78,128]{2,1,0:T(8,128)} async-done(((f32[1,78,128]{2,1,0:T(8,128)}), f32[32,78,128]{2,1,0:T(8,128)}) %all-gather.7.cloned.1.call-update) | async-done | bytes 1277968 | tf_op jit(solution)/shard_map/all_gather | solution.py:350
  586.8 8.2 %reshape.273 = bf16[1024,1,1,768]{3,2,1,0:T(2,128)(2,1)S(1)} reshape(bf16[32,2,12288]{2,1,0:T(2,128)(2,1)} %all-to-all-done.3) | data formatting | bytes 3145728
  596.4 8.3 %reshape.271 = bf16[1024,1,1,768]{3,2,1,0:T(2,128)(2,1)S(1)} reshape(bf16[32,2,12288]{2,1,0:T(2,128)(2,1)} %all-to-all-done.1) | data formatting | bytes 3145728
  606.1 118.4 %reduce-scatter.5.cloned.1.call-done = bf16[1,2,48,1536]{3,2,1,0:T(8,128)(2,1)} async-done(((bf16[32,2,48,1536]{3,2,1,0:T(8,128)(2,1)}), bf16[1,2,48,1536]{3,2,1,0:T(8,128)(2,1)}) %reduce-scatter.5.cloned.1.call-update) | async-done | bytes 294928 | tf_op jit(solution)/shard_map/reduce_scatter | solution.py:343
  (147 shorter events, 30.8 us)
Async XLA Ops:
  7.2 91.2 %all-gather.9.cloned.1.call-start = ((), (), s32[]{:S(2)}) async-start(), calls=%async_computation.7 | async-start | bytes 4866048 | tf_op jit(solution)/shard_map/all_gather | solution.py:310
  8.8 172.5 %all-gather.11.cloned.1.call-start = ((), (), s32[]{:S(2)}) async-start(), calls=%async_computation.8 | async-start | bytes 9732096 | tf_op jit(solution)/shard_map/all_gather | solution.py:314
  10.6 58.1 %copy-start.23 = (s32[1024]{0:T(1024)S(1)}, s32[1024]{0:T(1024)}, u32[]{:S(2)}) copy-start(s32[1024]{0:T(1024)} %param.19) | copy-start | bytes 12292
  10.7 58.1 %copy-start.26 = (f32[3,384]{1,0:T(4,128)S(1)}, f32[3,384]{1,0:T(4,128)}, u32[]{:S(2)}) copy-start(f32[3,384]{1,0:T(4,128)} %param.21) | copy-start | bytes 13828
  10.7 74.7 %copy-start.25 = (f32[1536]{0:T(1024)S(1)}, f32[1536]{0:T(1024)}, u32[]{:S(2)}) copy-start(f32[1536]{0:T(1024)} %param.27) | copy-start | bytes 18436
  10.7 74.6 %copy-start.36 = (s32[32]{0:T(128)S(1)}, s32[32]{0:T(128)}, u32[]{:S(2)}) copy-start(s32[32]{0:T(128)} %param.18) | copy-start | bytes 388
  10.7 83.4 %copy-start.20 = (f32[768]{0:T(1024)S(1)}, f32[768]{0:T(1024)}, u32[]{:S(2)}) copy-start(f32[768]{0:T(1024)} %param.30) | copy-start | bytes 9220
  65.0 55.9 %all-to-all-start = ((bf16[1,32,32,768]{3,2,0,1:T(8,128)(2,1)}), bf16[1,32,32,768]{3,2,0,1:T(8,128)(2,1)S(1)}, u32[]{:S(2)}, u32[]{:S(2)}) async-start(bf16[1,32,32,768]{3,2,0,1:T(8,128)(2,1)} %bitcast.181), calls=%async_computation | async-start | bytes 3145728 | tf_op jit(solution)/shard_map/all_to_all | solution.py:297
  68.6 454.0 %all-reduce.3.cloned.1.call-start = ((), (), s32[]{:S(2)}) async-start(), calls=%async_computation.9 | async-start | bytes 9437184
  120.8 1.1 copy-start.6
  135.5 37.1 %copy-start.7 = (bf16[1,32,32,768]{3,2,0,1:T(8,128)(2,1)S(1)}, bf16[1,32,32,768]{3,2,0,1:T(8,128)(2,1)}, u32[]{:S(2)}) copy-start(bf16[1,32,32,768]{3,2,0,1:T(8,128)(2,1)} %copy-done.6) | copy-start | bytes 4718596
  135.5 37.1 %copy-start.32 = (f32[768]{0:T(1024)S(1)}, f32[768]{0:T(1024)}, u32[]{:S(2)}) copy-start(f32[768]{0:T(1024)} %param.23) | copy-start | bytes 9220
  176.0 1.6 copy-start.1
  210.3 3.4 copy-start.2
  210.3 3.4 copy-start.28
  210.3 3.4 copy-start.34
  213.7 35.5 %copy-start.12 = (bf16[96,8,2,1536]{3,1,2,0:T(8,128)(2,1)S(1)}, bf16[96,8,2,1536]{3,1,2,0:T(8,128)(2,1)}, u32[]{:S(2)}) copy-start(bf16[96,8,2,1536]{3,1,2,0:T(8,128)(2,1)} %copy.105) | copy-start | bytes 14155780
  213.7 35.5 %copy-start.33 = (f32[768]{0:T(1024)S(1)}, f32[768]{0:T(1024)}, u32[]{:S(2)}) copy-start(f32[768]{0:T(1024)} %param.29) | copy-start | bytes 9220
  257.5 1.6 copy-start.27
  261.6 14.8 %copy-start.13 = (f32[1024,768]{1,0:T(8,128)}, f32[1024,768]{1,0:T(8,128)S(1)}, u32[]{:S(2)}) copy-start(f32[1024,768]{1,0:T(8,128)S(1)} %get-tuple-element.27) | copy-start | bytes 9437188
  285.5 1.7 copy-start.16
  287.2 2.6 copy-start.4
  287.2 2.6 copy-start.15
  292.3 36.3 %copy-start.8 = (bf16[1,32,32,768]{3,2,0,1:T(8,128)(2,1)S(1)}, bf16[1,32,32,768]{3,2,0,1:T(8,128)(2,1)}, u32[]{:S(2)}) copy-start(bf16[1,32,32,768]{3,2,0,1:T(8,128)(2,1)} %copy-done.6) | copy-start | bytes 4718596
  328.7 4.0 copy-start
  335.1 2.5 copy-start.17
  337.9 1.3 copy-start.18
  354.4 3.4 copy-start.22
  354.4 3.4 copy-start.31
  354.4 3.4 copy-start.30
  354.4 3.4 copy-start.24
  354.5 3.4 copy-start.21
  354.5 4.2 copy-start.3
  354.5 4.2 copy-start.29
  354.5 4.1 copy-start.35
  354.5 229.1 %all-gather.7.cloned.1.call-start = ((), (), s32[]{:S(2)}) async-start(), calls=%async_computation.5 | async-start | bytes 1351680 | tf_op jit(solution)/shard_map/all_gather | solution.py:350
  357.9 0.6 copy-start.19
  358.6 365.9 %reduce-scatter.5.cloned.1.call-start = ((), (), s32[]{:S(2)}) async-start(), calls=%async_computation.6 | async-start | bytes 9732096 | tf_op jit(solution)/shard_map/reduce_scatter | solution.py:343
  380.6 5.8 copy-start.14
  421.8 1.6 copy-start.11
  421.8 5.1 slice-start
  421.8 2.8 copy-start.10
  424.3 1.4 copy-start.9
  424.4 2.6 slice-start.1
  428.4 1.9 copy-start.5
  451.0 54.6 %all-to-all-start.3 = ((bf16[32,2,12288]{2,1,0:T(2,128)(2,1)}), bf16[32,2,12288]{2,1,0:T(2,128)(2,1)}, u32[]{:S(2)}, u32[]{:S(2)}) async-start(bf16[32,2,12288]{2,1,0:T(2,128)(2,1)} %reshape.272), calls=%async_computation.3 | async-start | bytes 3145728 | tf_op jit(solution)/shard_map/all_to_all | solution.py:303
  505.6 90.8 %all-to-all-start.1 = ((bf16[32,2,12288]{2,1,0:T(2,128)(2,1)}), bf16[32,2,12288]{2,1,0:T(2,128)(2,1)}, u32[]{:S(2)}, u32[]{:S(2)}) async-start(bf16[32,2,12288]{2,1,0:T(2,128)(2,1)} %reshape.270), calls=%async_computation.1 | async-start | bytes 3145728 | tf_op jit(solution)/shard_map/all_to_all | solution.py:303
Sparse Core Ops, SparseCore 0:
  11.5 86.8 all-gather.8
  101.9 79.3 all-gather.10
  354.5 168.0 all-reduce.2
  525.9 57.6 all-gather.6
  589.3 135.0 reduce-scatter.4

commit v2 on v1

--- a/solution.py
+++ b/solution.py
@@ -45,9 +45,15 @@
     return values * cos_table + swapped * sine_table
 
 
+def block_rows(w_ref, member, part, depth, cols=slice(None)):
+    taken = w_ref[:, member, part * depth : (part + 1) * depth, cols]
+    return taken.reshape(taken.shape[0] * depth, taken.shape[2])
+
+
 def project_kernel(x_ref, w_ref, b_ref, cos_ref, sine_ref, out_ref):
     kind = pl.program_id(0)
-    raw = dot(x_ref[...], w_ref[0], NN) + b_ref[0]
+    depth = w_ref.shape[2]
+    raw = dot(x_ref[...], block_rows(w_ref, 0, 0, depth), NN) + b_ref[0]
 
     @pl.when(kind < 2)
     def _():
@@ -60,29 +66,25 @@
         out_ref[0] = raw.astype(BF)
 
 
-def project(x, w, b, cos_table, sine_table):
+def project(x, attn_w, b, cos_table, sine_table):
     rows, features = x.shape
-    block = 256
+    groups, members, depth4, cols = attn_w.shape
+    depth = depth4 // 4
     return pl.pallas_call(
         project_kernel,
-        grid=(3, features // block),
+        grid=(3, members),
         in_specs=[
             pl.BlockSpec((rows, features), lambda p, c: (0, 0)),
-            pl.BlockSpec((1, features, block), lambda p, c: (p, 0, c)),
-            pl.BlockSpec((1, 1, block), lambda p, c: (p, 0, c)),
+            pl.BlockSpec((groups, 1, depth, cols), lambda p, c: (0, c, p, 0)),
+            pl.BlockSpec((1, 1, cols), lambda p, c: (p, 0, c)),
             pl.BlockSpec((rows, LANES), lambda p, c: (0, 0)),
             pl.BlockSpec((rows, LANES), lambda p, c: (0, 0)),
         ],
-        out_specs=pl.BlockSpec((1, rows, block), lambda p, c: (p, 0, c)),
+        out_specs=pl.BlockSpec((1, rows, cols), lambda p, c: (p, 0, c)),
         out_shape=jax.ShapeDtypeStruct((3, rows, features), BF),
         compiler_params=pltpu.CompilerParams(vmem_limit_bytes=VMEM_BYTES),
         name="project",
-    )(x, w, b, cos_table, sine_table)
-
-
-def head_masks(rows):
-    lane = lax.broadcasted_iota(jnp.int32, (rows, LANES), 1)
-    return lane
+    )(x, attn_w, b, cos_table, sine_table)
 
 
 def pair_operands(q, k, bias, lane, head):
@@ -227,55 +229,497 @@
     return inv_std * (grad_unit - first_mean - normed * second_mean)
 
 
-def gelu_slope(up_proj):
-    return (
-        0.5 * (1.0 + lax.erf(up_proj * INV_ROOT_TWO))
-        + up_proj * jnp.exp(-0.5 * up_proj * up_proj) * INV_ROOT_TAU
-    )
-
-
-def layer(rows, cotangent, place, length, cos_table, sine_table, params):
-    (w_qkv, b_qkv, w_out_t, b_out, gain_one, shift_one, w_up, b_up, w_down_t, b_down,
-     gain_two, shift_two) = params
+def column_sum(values):
+    return jnp.sum(values, axis=0, keepdims=True)
+
+
+def middle_kernel(
+    x_ref, ctx_ref, cot_ref, live_ref, attn_ref, ffn_ref, vec_ref, b_up_ref,
+    mixed_ref, act_ref, g_up_ref, mid_ref, g_down_ref, g_attn_ref, g_first_ref, g_ctx_ref,
+    small_ref, small_up_ref, slope_ref, *, chunk
+):
+    members, depth, cols = attn_ref.shape[1], attn_ref.shape[2], attn_ref.shape[3]
+    ffn_depth, units = ffn_ref.shape[2] // 2, ffn_ref.shape[3]
+    b_out, gain_one, shift_one = vec_ref[0:1], vec_ref[1:2], vec_ref[2:3]
+    b_down, gain_two, shift_two = vec_ref[3:4], vec_ref[4:5], vec_ref[5:6]
+
+    @pl.when(pl.program_id(0) == 0)
+    def _():
+        small_ref[...] = jnp.zeros_like(small_ref)
+        small_up_ref[...] = jnp.zeros_like(small_up_ref)
+
+    first_sum = x_ref[...].astype(F32) + b_out
+    for t in range(members):
+        first_sum += dot(ctx_ref[:, t * cols : (t + 1) * cols], block_rows(attn_ref, t, 0, depth), NT)
+    normed_one, unit_one, inv_one = normalize(first_sum, gain_one, shift_one)
+    mid = normed_one.astype(BF)
+    mid_ref[...] = mid
+    second_sum = normed_one + b_down
+    for t in range(members):
+        for start in range(0, units, chunk):
+            here = slice(t * units + start, t * units + start + chunk)
+            span = slice(start, start + chunk)
+            up_proj = dot(mid, block_rows(ffn_ref, t, 0, ffn_depth, span), NN) + b_up_ref[:, here]
+            phi = 0.5 * (1.0 + lax.erf(up_proj * INV_ROOT_TWO))
+            act_ref[:, here] = (up_proj * phi).astype(BF)
+            slope_ref[:, here] = phi + up_proj * jnp.exp(-0.5 * up_proj * up_proj) * INV_ROOT_TAU
+        half = slice(t * units, (t + 1) * units)
+        second_sum += dot(act_ref[:, half], block_rows(ffn_ref, t, 1, ffn_depth), NT)
+    result, unit_two, inv_two = normalize(second_sum, gain_two, shift_two)
+    mixed_ref[...] = result.astype(BF)
+
+    grad_out = jnp.where(live_ref[...] > 0.0, cot_ref[...].astype(F32), 0.0)
+    grad_second = normalize_back(grad_out * gain_two, unit_two, inv_two)
+    small_ref[5:6] += column_sum(grad_out * unit_two)
+    small_ref[6:7] += column_sum(grad_out)
+    small_ref[4:5] += column_sum(grad_second)
+    grad_down = grad_second.astype(BF)
+    g_down_ref[...] = grad_down
+    grad_mid = grad_second
+    for t in range(members):
+        for start in range(0, units, chunk):
+            here = slice(t * units + start, t * units + start + chunk)
+            span = slice(start, start + chunk)
+            grad_act = dot(grad_down, block_rows(ffn_ref, t, 1, ffn_depth, span), NN)
+            grad_up = (grad_act * slope_ref[:, here]).astype(BF)
+            g_up_ref[:, here] = grad_up
+            small_up_ref[:, here] += column_sum(grad_up.astype(F32))
+        half = slice(t * units, (t + 1) * units)
+        grad_mid += dot(g_up_ref[:, half], block_rows(ffn_ref, t, 0, ffn_depth), NT)
+    small_ref[2:3] += column_sum(grad_mid * unit_one)
+    small_ref[3:4] += column_sum(grad_mid)
+    grad_first = normalize_back(grad_mid * gain_one, unit_one, inv_one)
+    small_ref[1:2] += column_sum(grad_first)
+    g_first_ref[...] = grad_first
+    grad_attn = grad_first.astype(BF)
+    g_attn_ref[...] = grad_attn
+    for t in range(members):
+        g_ctx_ref[:, t * cols : (t + 1) * cols] = dot(
+            grad_attn, block_rows(attn_ref, t, 0, depth), NN
+        ).astype(BF)
+
+
+def middle(x, context, cotangent, live, attn_w, ffn_w, vectors, b_up):
+    rows, features = x.shape
+    groups, members, depth4, cols = attn_w.shape
+    ffn_rows, units = ffn_w.shape[2], ffn_w.shape[3]
+    width = members * units
+    tile = 256
+
+    def row(n):
+        return pl.BlockSpec((tile, n), lambda i: (i, 0))
+
+    def fixed(shape, index):
+        return pl.BlockSpec(shape, lambda i: index, pipeline_mode=pl.Buffered(1))
+
+    def out(n, dtype):
+        return jax.ShapeDtypeStruct((rows, n), dtype)
+
+    return pl.pallas_call(
+        functools.partial(middle_kernel, chunk=512),
+        grid=(rows // tile,),
+        in_specs=[
+            row(features), row(features), row(features), row(1),
+            fixed((groups, members, depth4 // 4, cols), (0, 0, 3, 0)),
+            fixed((groups, members, ffn_rows, units), (0, 0, 0, 0)),
+            fixed((8, features), (0, 0)), fixed((1, width), (0, 0)),
+        ],
+        out_specs=[
+            row(features), row(width), row(width), row(features), row(features), row(features),
+            row(features), row(features),
+            pl.BlockSpec((8, features), lambda i: (0, 0)), pl.BlockSpec((1, width), lambda i: (0, 0)),
+        ],
+        out_shape=[
+            out(features, BF), out(width, BF), out(width, BF), out(features, BF), out(features, BF),
+            out(features, BF), out(features, F32), out(features, BF),
+            jax.ShapeDtypeStruct((8, features), F32), jax.ShapeDtypeStruct((1, width), F32),
+        ],
+        scratch_shapes=[pltpu.VMEM((tile, width), F32)],
+        compiler_params=pltpu.CompilerParams(vmem_limit_bytes=VMEM_BYTES),
+        name="middle",
+    )(x, context, cotangent, live, attn_w, ffn_w, vectors, b_up)
+
+
+def ffn_weights_kernel(mid_ref, g_down_ref, act_ref, g_up_ref, out_ref, mid_t_ref, down_t_ref):
+    groups, _, depth2, width = out_ref.shape
+    depth = depth2 // 2
+
+    @pl.when((pl.program_id(0) == 0) & (pl.program_id(1) == 0))
+    def _():
+        mid_t_ref[...] = mid_ref[...].T
+        down_t_ref[...] = g_down_ref[...].T
+
+    out_ref[:, 0, :depth] = dot(mid_t_ref[...], g_up_ref[...], NN).astype(BF).reshape(groups, depth, width)
+    out_ref[:, 0, depth:] = dot(down_t_ref[...], act_ref[...], NN).astype(BF).reshape(groups, depth, width)
+
+
+def ffn_weights(mid, grad_down, act, grad_up, groups, members):
+    rows, features = mid.shape
+    units = act.shape[1] // members
+    chunk = 512
+    per = units // chunk
+    fixed = pl.BlockSpec((rows, features), lambda t, j: (0, 0), pipeline_mode=pl.Buffered(1))
+    part = pl.BlockSpec((rows, chunk), lambda t, j: (0, t * per + j))
+    depth2 = 2 * features // groups
+    return pl.pallas_call(
+        ffn_weights_kernel,
+        grid=(members, per),
+        in_specs=[fixed, fixed, part, part],
+        out_specs=pl.BlockSpec((groups, 1, depth2, chunk), lambda t, j: (0, t, 0, j)),
+        out_shape=jax.ShapeDtypeStruct((groups, members, depth2, units), BF),
+        scratch_shapes=[pltpu.VMEM((features, rows), BF), pltpu.VMEM((features, rows), BF)],
+        compiler_params=pltpu.CompilerParams(vmem_limit_bytes=VMEM_BYTES),
+        name="ffn_weights",
+    )(mid, grad_down, act, grad_up)
+
+
+def attn_weights_kernel(
+    x_ref, g_attn_ref, ctx_ref, raw_ref, w_ref, g_first_ref, out_ref, rows_ref, bias_ref,
+    x_t_ref, attn_t_ref, sum_ref
+):
+    groups, _, depth4, cols = out_ref.shape
+    depth = depth4 // 4
+    step = pl.program_id(0)
+
+    @pl.when(step == 0)
+    def _():
+        x_t_ref[...] = x_ref[...].T
+        attn_t_ref[...] = g_attn_ref[...].T
+        sum_ref[...] = g_first_ref[...]
+        bias_ref[...] = jnp.zeros_like(bias_ref)
+
+    total = sum_ref[...]
+    for p in range(3):
+        out_ref[:, 0, p * depth : (p + 1) * depth] = dot(x_t_ref[...], raw_ref[p], NN).astype(BF).reshape(
+            groups, depth, cols
+        )
+        total += dot(raw_ref[p], block_rows(w_ref, 0, p, depth), NT)
+        bias_ref[p : p + 1] = column_sum(raw_ref[p].astype(F32))
+    out_ref[:, 0, 3 * depth :] = dot(attn_t_ref[...], ctx_ref[...], NN).astype(BF).reshape(
+        groups, depth, cols
+    )
+    sum_ref[...] = total
+
+    @pl.when(step == pl.num_programs(0) - 1)
+    def _():
+        rows_ref[...] = sum_ref[...].astype(BF)
+
+
+def attn_weights(x, grad_attn, context, grad_raw, attn_w, grad_first):
+    rows, features = x.shape
+    groups, members, depth4, cols = attn_w.shape
+
+    def fixed(n):
+        return pl.BlockSpec((rows, n), lambda t: (0, 0), pipeline_mode=pl.Buffered(1))
+
+    return pl.pallas_call(
+        attn_weights_kernel,
+        grid=(members,),
+        in_specs=[
+            fixed(features), fixed(features), pl.BlockSpec((rows, cols), lambda t: (0, t)),
+            pl.BlockSpec((3, rows, cols), lambda t: (0, 0, t)),
+            pl.BlockSpec((groups, 1, depth4, cols), lambda t: (0, t, 0, 0)), fixed(features),
+        ],
+        out_specs=[
+            pl.BlockSpec((groups, 1, depth4, cols), lambda t: (0, t, 0, 0)),
+            pl.BlockSpec((rows, features), lambda t: (0, 0)),
+            pl.BlockSpec((8, cols), lambda t: (0, t)),
+        ],
+        out_shape=[
+            jax.ShapeDtypeStruct((groups, members, depth4, cols), BF),
+            jax.ShapeDtypeStruct((rows, features), BF),
+            jax.ShapeDtypeStruct((8, features), F32),
+        ],
+        scratch_shapes=[
+            pltpu.VMEM((features, rows), BF), pltpu.VMEM((features, rows), BF),
+            pltpu.VMEM((rows, features), F32),
+        ],
+        compiler_params=pltpu.CompilerParams(vmem_limit_bytes=VMEM_BYTES),
+        name="attn_weights",
+    )(x, grad_attn, context, grad_raw, attn_w, grad_first)
+
+
+def merge_groups(w, parts):
+    groups, members, rows, cols = w.shape
+    depth = rows // parts
+    if depth % 16 == 0:
+        return w
+    w = w.reshape(groups, members, parts, depth, cols).transpose(1, 2, 0, 3, 4)
+    return w.reshape(1, members, parts * groups * depth, cols)
+
+
+def split_groups(w, parts, groups):
+    have, members, rows, cols = w.shape
+    if have == groups:
+        return w
+    w = w.reshape(members, parts, groups, rows // parts // groups, cols).transpose(2, 0, 1, 3, 4)
+    return w.reshape(groups, members, rows // groups, cols)
+
+
+def layer(rows, cotangent, place, length, cos_table, sine_table, attn_w, ffn_w, b_qkv, b_up, vectors):
     live = place < length
     bias = jnp.broadcast_to(jnp.where(live, 0.0, MASK_FILL).astype(BF)[:, None], (rows.shape[0], LANES))
-    qkv = project(rows, w_qkv, b_qkv[:, None, :], cos_table, sine_table)
+    qkv = project(rows, attn_w, b_qkv[:, None, :], cos_table, sine_table)
     context, lse = attend(qkv, bias)
-    first_sum = rows.astype(F32) + dot(context, w_out_t, NT) + b_out
-    normed_one, unit_one, inv_one = normalize(first_sum, gain_one, shift_one)
-    mid = normed_one.astype(BF)
-    up_proj = dot(mid, w_up, NN) + b_up
-    activated = jax.nn.gelu(up_proj, approximate=False).astype(BF)
-    second_sum = normed_one + dot(activated, w_down_t, NT) + b_down
-    result, unit_two, inv_two = normalize(second_sum, gain_two, shift_two)
-    result = result.astype(BF)
-
-    grad_out = jnp.where(live[:, None], cotangent.astype(F32), 0.0)
-    g_gain_two = jnp.sum(grad_out * unit_two, axis=0)
-    g_shift_two = jnp.sum(grad_out, axis=0)
-    grad_second = normalize_back(grad_out * gain_two, unit_two, inv_two)
-    g_b_down = jnp.sum(grad_second, axis=0)
-    grad_down = grad_second.astype(BF)
-    g_w_down_t = dot(grad_down, activated, TN)
-    grad_up = (dot(grad_down, w_down_t, NN) * gelu_slope(up_proj)).astype(BF)
-    g_b_up = jnp.sum(grad_up.astype(F32), axis=0)
-    g_w_up = dot(mid, grad_up, TN)
-    grad_mid = grad_second + dot(grad_up, w_up, NT)
-    g_gain_one = jnp.sum(grad_mid * unit_one, axis=0)
-    g_shift_one = jnp.sum(grad_mid, axis=0)
-    grad_first = normalize_back(grad_mid * gain_one, unit_one, inv_one)
-    g_b_out = jnp.sum(grad_first, axis=0)
-    grad_attn = grad_first.astype(BF)
-    g_w_out_t = dot(grad_attn, context, TN)
-    grad_ctx = dot(grad_attn, w_out_t, NN).astype(BF)
-    grad_raw = attend_back(qkv, bias, context, grad_ctx, lse, cos_table, sine_table)
-    g_b_qkv = jnp.sum(grad_raw.astype(F32), axis=1)
-    g_w_qkv = [dot(rows, grad_raw[i], TN) for i in range(3)]
-    in_sum = sum(dot(grad_raw[i], w_qkv[i], NT) for i in range(3))
-    grad_rows = (grad_first + in_sum).astype(BF)
-    weights = (g_w_qkv, g_w_out_t, g_w_up, g_w_down_t)
-    small = (g_b_qkv, g_b_out, g_gain_one, g_shift_one, g_b_up, g_b_down, g_gain_two, g_shift_two)
-    return result, grad_rows, weights, small
+    mixed, act, g_up, mid, g_down, g_attn, g_first, g_ctx, small, small_up = middle(
+        rows, context, cotangent, live.astype(F32)[:, None], attn_w, ffn_w, vectors, b_up
+    )
+    g_ffn = ffn_weights(mid, g_down, act, g_up, ffn_w.shape[0], ffn_w.shape[1])
+    g_raw = attend_back(qkv, bias, context, g_ctx, lse, cos_table, sine_table)
+    g_attn_w, grad_rows, small_qkv = attn_weights(rows, g_attn, context, g_raw, attn_w, g_first)
+    packed = jnp.concatenate([small_qkv[:3], small[1:7], small_up.reshape(-1, small.shape[1])], axis=0)
+    return mixed, grad_rows, g_attn_w, g_ffn, packed
+
+
+MESH = pl.DeviceIdType.MESH
+
+
+def axis_orders(bits, rows):
+    core = bits - 2
+    rest = [d for d in range(bits) if d != core]
+    if bits != 5 or rows % 192:
+        return [(0, rows, tuple(rest) + (core,))]
+    far, near, y, _, x = range(5)
+    unit = rows // 12
+    return [
+        (0, 5 * unit, (far, near, x, y, core)),
+        (5 * unit, 5 * unit, (far, near, y, x, core)),
+        (10 * unit, 2 * unit, (x, y, near, far, core)),
+    ]
+
+
+class Place:
+    def __init__(self, devices, members):
+        self.devices, self.members = devices, members
+        self.bits = devices.bit_length() - 1
+        self.me = lax.axis_index("dp") * members + lax.axis_index("tensor")
+        self.bit = [self.me // self.stride(d) % 2 for d in range(self.bits)]
+
+    def stride(self, dim):
+        return 1 << (self.bits - 1 - dim)
+
+    def ident(self, number):
+        return (number // self.members, number % self.members)
+
+    def partner(self, dim):
+        return self.ident(self.me + (1 - 2 * self.bit[dim]) * self.stride(dim))
+
+    def meet_all(self):
+        barrier = pltpu.get_barrier_semaphore()
+
+        def greet(offset, carry):
+            pl.semaphore_signal(
+                barrier, inc=1, device_id=self.ident((self.me + offset) % self.devices),
+                device_id_type=MESH,
+            )
+            return carry
+
+        lax.fori_loop(1, self.devices, greet, 0)
+        pl.semaphore_wait(barrier, self.devices - 1)
+
+    def swap(self, src, dst, send_sem, recv_sem, offset):
+        target = (self.me + offset) % self.devices
+        return pltpu.make_async_remote_copy(
+            src_ref=src.at[target], dst_ref=dst.at[self.me], send_sem=send_sem.at[offset],
+            recv_sem=recv_sem.at[offset], device_id=self.ident(target), device_id_type=MESH,
+        )
+
+    def for_others(self, action):
+        def one(offset, carry):
+            action(offset)
+            return carry
+
+        lax.fori_loop(1, self.devices, one, 0)
+
+
+def head_kernel(
+    rows_ref, shard_ref, bias_ref, seq_ref, attn_ref, biases_ref, held_ref,
+    send_sem, recv_sem, w_send, w_recv, b_sem, local_sem, *, devices, members
+):
+    here = Place(devices, members)
+    bits = here.bits
+    colours = axis_orders(bits, shard_ref.shape[0])
+    mine = pltpu.make_async_copy(rows_ref.at[here.me], held_ref, local_sem.at[0])
+    mine.start()
+    own = pltpu.make_async_copy(shard_ref, attn_ref.at[tuple(here.bit)], local_sem.at[1])
+    own.start()
+    own_bias = pltpu.make_async_copy(bias_ref, biases_ref.at[here.me % members], local_sem.at[2])
+    own_bias.start()
+    here.meet_all()
+
+    def spread(colour, step):
+        start, count, order = colours[colour]
+        done = set(order[:step])
+        span = pl.ds(start, count)
+        place = tuple(slice(None) if d in done else here.bit[d] for d in range(bits))
+        there = attn_ref.at[place + (span, slice(None))]
+        return pltpu.make_async_remote_copy(
+            src_ref=shard_ref.at[span] if step == 0 else there, dst_ref=there,
+            send_sem=w_send.at[colour, step], recv_sem=w_recv.at[colour, step],
+            device_id=here.partner(order[step]), device_id_type=MESH,
+        )
+
+    to_member = pltpu.make_async_remote_copy(
+        src_ref=bias_ref, dst_ref=biases_ref.at[here.me % members], send_sem=b_sem.at[0],
+        recv_sem=b_sem.at[1], device_id=here.partner(bits - 1), device_id_type=MESH,
+    )
+    moving = [spread(c, 0) for c in range(len(colours))]
+    for copy in moving:
+        copy.start()
+    to_member.start()
+    here.for_others(lambda o: here.swap(rows_ref, seq_ref, send_sem, recv_sem, o).start())
+    mine.wait()
+    back = pltpu.make_async_copy(held_ref, seq_ref.at[here.me], local_sem.at[0])
+    back.start()
+    own.wait()
+    own_bias.wait()
+    for step in range(bits):
+        for c in range(len(colours)):
+            moving[c].wait()
+            if step + 1 < bits:
+                moving[c] = spread(c, step + 1)
+                moving[c].start()
+    to_member.wait()
+    back.wait()
+    here.for_others(lambda o: here.swap(rows_ref, seq_ref, send_sem, recv_sem, o).wait())
+
+
+def head(tokens, attn_shard, biases, members):
+    devices, stripe, features = tokens.shape
+    bits = devices.bit_length() - 1
+    colours = len(axis_orders(bits, attn_shard.shape[0]))
+    anywhere = pl.BlockSpec(memory_space=pl.ANY)
+    onchip = pl.BlockSpec(memory_space=pltpu.VMEM)
+    sems = pltpu.SemaphoreType.DMA
+    seq, attn, both = pl.pallas_call(
+        functools.partial(head_kernel, devices=devices, members=members),
+        in_specs=[anywhere, onchip, onchip],
+        out_specs=[anywhere, anywhere, anywhere],
+        out_shape=[
+            jax.ShapeDtypeStruct(tokens.shape, BF),
+            jax.ShapeDtypeStruct((2,) * bits + attn_shard.shape, BF),
+            jax.ShapeDtypeStruct((members,) + biases.shape, F32),
+        ],
+        scratch_shapes=[
+            pltpu.VMEM((stripe, features), BF), sems((devices,)), sems((devices,)),
+            sems((colours, bits)), sems((colours, bits)), sems((2,)), sems((3,)),
+        ],
+        compiler_params=pltpu.CompilerParams(collective_id=0, has_side_effects=True),
+        name="head",
+    )(tokens, attn_shard, biases)
+    return seq, attn.reshape((devices,) + attn_shard.shape), both
+
+
+def tail_kernel(
+    rows_ref, grad_ref, small_ref, back_ref, sum_ref, total_ref, held_ref, *rest, devices, members
+):
+    here = Place(devices, members)
+    bits = here.bits
+    colours = axis_orders(bits, grad_ref.shape[-2])
+    count = len(colours)
+    got = [rest[c * bits : (c + 1) * bits] for c in range(count)]
+    kept = [rest[(count + c) * bits : (count + c + 1) * bits] for c in range(count)]
+    small_got, small_kept = rest[2 * count * bits : 2 * count * bits + 2]
+    send_sem, recv_sem, w_send, w_recv, s_send, s_recv, local_sem = rest[2 * count * bits + 2 :]
+    mine = pltpu.make_async_copy(rows_ref.at[here.me], held_ref, local_sem.at[0])
+    mine.start()
+    here.meet_all()
+
+    def current(colour, step):
+        start, size, _ = colours[colour]
+        if step == 0:
+            return grad_ref, (pl.ds(start, size), slice(None))
+        return kept[colour][step - 1], (slice(None), slice(None))
+
+    def place(colour, step, side):
+        order = colours[colour][2][::-1]
+        left = [d for d in range(bits) if d not in order[:step]]
+        return tuple(
+            (here.bit[d] if side else 1 - here.bit[d]) if d == order[step] else slice(None)
+            for d in left
+        )
+
+    def hand_over(colour, step):
+        ref, inner = current(colour, step)
+        return pltpu.make_async_remote_copy(
+            src_ref=ref.at[place(colour, step, False) + inner], dst_ref=got[colour][step],
+            send_sem=w_send.at[colour, step], recv_sem=w_recv.at[colour, step],
+            device_id=here.partner(colours[colour][2][::-1][step]), device_id_type=MESH,
+        )
+
+    def hand_small(step):
+        return pltpu.make_async_remote_copy(
+            src_ref=small_ref if step == 0 else small_kept.at[step - 1], dst_ref=small_got.at[step],
+            send_sem=s_send.at[step], recv_sem=s_recv.at[step],
+            device_id=here.partner(bits - 1 - step), device_id_type=MESH,
+        )
+
+    moving = [hand_over(c, 0) for c in range(count)]
+    for copy in moving:
+        copy.start()
+    small = hand_small(0)
+    small.start()
+    here.for_others(lambda o: here.swap(rows_ref, back_ref, send_sem, recv_sem, o).start())
+    mine.wait()
+    back = pltpu.make_async_copy(held_ref, back_ref.at[here.me], local_sem.at[0])
+    back.start()
+    for step in range(bits):
+        for c in range(count):
+            moving[c].wait()
+            ref, inner = current(c, step)
+            added = ref[place(c, step, True) + inner] + got[c][step][...]
+            if step + 1 < bits:
+                kept[c][step][...] = added
+                moving[c] = hand_over(c, step + 1)
+                moving[c].start()
+            else:
+                start, size, _ = colours[c]
+                sum_ref[start : start + size] = added.astype(F32)
+        small.wait()
+        before = small_ref[...] if step == 0 else small_kept[step - 1]
+        after = before + small_got[step]
+        if step + 1 < bits:
+            small_kept[step] = after
+            small = hand_small(step + 1)
+            small.start()
+        else:
+            total_ref[...] = after
+    back.wait()
+    here.for_others(lambda o: here.swap(rows_ref, back_ref, send_sem, recv_sem, o).wait())
+
+
+def tail(grad_rows, grad_w, small, members):
+    devices, stripe, features = grad_rows.shape
+    bits = devices.bit_length() - 1
+    rows, cols = grad_w.shape[1:]
+    colours = axis_orders(bits, rows)
+    anywhere = pl.BlockSpec(memory_space=pl.ANY)
+    onchip = pl.BlockSpec(memory_space=pltpu.VMEM)
+    sems = pltpu.SemaphoreType.DMA
+    levels = [
+        pltpu.VMEM((2,) * (bits - 1 - step) + (size, cols), BF)
+        for _, size, _ in colours
+        for step in range(bits)
+    ]
+    return pl.pallas_call(
+        functools.partial(tail_kernel, devices=devices, members=members),
+        in_specs=[anywhere, onchip, onchip],
+        out_specs=[anywhere, onchip, onchip],
+        out_shape=[
+            jax.ShapeDtypeStruct(grad_rows.shape, BF),
+            jax.ShapeDtypeStruct((rows, cols), F32),
+            jax.ShapeDtypeStruct(small.shape, F32),
+        ],
+        scratch_shapes=[pltpu.VMEM((stripe, features), BF)] + levels + levels + [
+            pltpu.VMEM((bits,) + small.shape, F32), pltpu.VMEM((bits,) + small.shape, F32),
+            sems((devices,)), sems((devices,)), sems((len(colours), bits)), sems((len(colours), bits)),
+            sems((bits,)), sems((bits,)), sems((1,)),
+        ],
+        compiler_params=pltpu.CompilerParams(
+            collective_id=1, has_side_effects=True, vmem_limit_bytes=VMEM_BYTES
+        ),
+        name="tail",
+    )(grad_rows, grad_w.reshape((2,) * bits + (rows, cols)), small)
 
 
 def body(
@@ -287,75 +731,47 @@
     devices = dp_size * tp_size
     me = lax.axis_index(AXES)
     stored, stripe, features = tokens.shape
-    batches = stored // devices
     slot = devices * stripe
     depth = w_qkv.shape[1]
     cols = w_qkv.shape[2]
     units = w_up.shape[1]
 
     def deal(rows_val):
-        return lax.all_to_all(
-            rows_val.reshape(batches, devices, stripe, features), AXES,
-            split_axis=1, concat_axis=2, tiled=True,
-        ).reshape(batches, slot, features)
-
-    def give_back(rows_val):
-        return lax.all_to_all(
-            rows_val.reshape(batches, 1, slot, features), AXES,
-            split_axis=2, concat_axis=1, tiled=True,
-        ).reshape(stored, stripe, features)
-
-    inputs = deal(tokens)
+        return lax.all_to_all(rows_val, AXES, split_axis=0, concat_axis=0, tiled=True)
+
+    ffn_shard = jnp.concatenate([w_up, w_down.T], axis=0)
+    ffn_all = lax.all_gather(ffn_shard, AXES, axis=0, tiled=True)
+    ffn_w = merge_groups(ffn_all.reshape(dp_size, tp_size, 2 * depth, units), 2)
     attn_shard = jnp.concatenate([w_qkv.reshape(3 * depth, cols), w_out.T], axis=0)
-    attn_all = lax.all_gather(attn_shard, AXES, axis=0, tiled=False)
-    attn_all = attn_all.reshape(dp_size, tp_size, 4, depth, cols)
-    attn_all = attn_all.transpose(2, 0, 3, 1, 4).reshape(4, features, features)
-    ffn_shard = jnp.stack([w_up, w_down.T], axis=0)
-    ffn_all = lax.all_gather(ffn_shard, AXES, axis=0, tiled=False)
-    ffn_all = ffn_all.reshape(dp_size, tp_size, 2, depth, units)
-    ffn_all = ffn_all.transpose(2, 0, 3, 1, 4).reshape(2, features, tp_size * units)
-    b_qkv_all = lax.all_gather(b_qkv, "tensor", axis=1, tiled=True)
-    b_up_all = lax.all_gather(b_up, "tensor", axis=0, tiled=True)
-    cotangents = deal(out_grad)
+    biases = jnp.concatenate([b_qkv.reshape(-1), b_up]).reshape(-1, LANES)
+    rows, attn_all, biases = head(tokens, attn_shard, biases, tp_size)
+    rows = rows.reshape(slot, features)
+    attn_w = merge_groups(attn_all.reshape(dp_size, tp_size, 4 * depth, cols), 4)
+    biases = biases.reshape(tp_size, -1)
+    b_qkv_all = biases[:, : 3 * cols].reshape(tp_size, 3, cols).transpose(1, 0, 2).reshape(3, features)
+    b_up_all = biases[:, 3 * cols :].reshape(1, tp_size * units)
+    cotangent = deal(out_grad).reshape(slot, features)
     cos_table, sine_table = rope_tables(order)
-    params = (attn_all[:3], b_qkv_all, attn_all[3], b_out, norm1_gain, norm1_bias,
-              ffn_all[0], b_up_all, ffn_all[1], b_down, norm2_gain, norm2_bias)
-    results, input_grads, weights, small = [], [], None, None
-    for micro in range(batches):
-        length = lax.dynamic_index_in_dim(lengths, micro * devices + me, 0, keepdims=False)
-        result, grad_rows, weights_one, small_one = layer(
-            inputs[micro], cotangents[micro], order, length, cos_table, sine_table, params
-        )
-        results.append(result)
-        input_grads.append(grad_rows)
-        if weights is None:
-            weights, small = weights_one, small_one
-        else:
-            weights, small = jax.tree.map(jnp.add, (weights, small), (weights_one, small_one))
-    mixed = give_back(jnp.stack(results, axis=0))
-    grad_tokens = give_back(jnp.stack(input_grads, axis=0))
-
-    def scatter(parts):
-        laid = [
-            p.astype(BF).reshape(dp_size, depth, tp_size, -1).transpose(0, 2, 1, 3) for p in parts
-        ]
-        laid = jnp.stack(laid, axis=2).reshape(devices, len(parts), depth, -1)
-        return lax.psum_scatter(laid, AXES, scatter_dimension=0, tiled=False).astype(F32)
-
-    g_qkv, g_out_t, g_up, g_down_t = weights
-    ffn_sum = scatter([g_up, g_down_t])
-    attn_sum = scatter(list(g_qkv) + [g_out_t])
-    sizes = [s.size for s in small]
-    packed = jnp.concatenate([s.reshape(-1) for s in small]).reshape(-1, LANES)
-    summed = jnp.sum(lax.all_gather(packed, AXES, axis=0, tiled=False), axis=0).reshape(-1)
-    small_sums, start = [], 0
-    for s, size in zip(small, sizes):
-        small_sums.append(summed[start : start + size].reshape(s.shape))
-        start += size
+    none = jnp.zeros_like(b_out)
+    vectors = jnp.stack(
+        [b_out, norm1_gain, norm1_bias, b_down, norm2_gain, norm2_bias, none, none], axis=0
+    )
+    length = lax.dynamic_index_in_dim(lengths, me, 0, keepdims=False)
+    result, grad_rows, g_attn_w, g_ffn, packed = layer(
+        rows, cotangent, order, length, cos_table, sine_table, attn_w, ffn_w, b_qkv_all, b_up_all, vectors
+    )
+    mixed = deal(result.reshape(devices, stripe, features))
+    laid = split_groups(g_ffn, 2, dp_size).reshape(devices * 2 * depth, units)
+    ffn_sum = lax.psum_scatter(laid, AXES, scatter_dimension=0, tiled=True).astype(F32)
+    laid = split_groups(g_attn_w, 4, dp_size).reshape(devices, 4 * depth, cols)
+    packed = jnp.pad(packed, ((0, -packed.shape[0] % 8), (0, 0)))
+    grad_tokens, attn_sum, summed = tail(
+        grad_rows.reshape(devices, stripe, features), laid, packed, tp_size
+    )
     return (
-        mixed, grad_tokens, attn_sum[:3], small_sums[0], attn_sum[3].T, small_sums[1],
-        small_sums[2], small_sums[3], ffn_sum[0], small_sums[4], ffn_sum[1].T, small_sums[5],
-        small_sums[6], small_sums[7],
+        mixed, grad_tokens, attn_sum[: 3 * depth].reshape(3, depth, cols), summed[:3],
+        attn_sum[3 * depth :].T, summed[3], summed[4], summed[5], ffn_sum[:depth],
+        summed[9:13].reshape(-1), ffn_sum[depth:].T, summed[6], summed[7], summed[8],
     )
 
 

time: 743 us -> 446 us (0.60); the launches traced: 733 us -> 445 us
  Pallas kernels: 86.1 us -> 374 us
  waiting for transfers between devices: 226 us -> 11.7 us
  local copies, waits for them, and re-layouts: 154 us -> 19.7 us
  matrix products: 109 us -> 0 us
  blocking collectives: 74.6 us -> 0 us
  other arithmetic: 55.8 us -> 9.14 us
    pallas_call x1 -> x6, Pallas kernels: 12.6 us -> 302 us  [the longest x1 126 us: head(): pl.pallas_call(functools.partial(head_kernel, devices=devices, members=me...]
    dot_general x15 -> x0, matrix products: 109 us -> none  [dot(): return lax.dot_general(a, b, (dims, ((), ())), preferred_element_type=F32)]
    reduce_scatter x1, waiting for transfers between devices: 118 us -> 11.7 us  [body(): lax.psum_scatter(laid, AXES, scatter_dimension=0, tiled=True).astype(F32)]
    all_gather x3 -> x1, waiting for transfers between devices: 64.7 us -> 0.01 us  [body(): ffn_all = lax.all_gather(ffn_shard, AXES, axis=0, tiled=True)]
    all_to_all x1 -> x0, blocking collectives: 54.3 us -> none  [deal(): lax.all_to_all(rows_val.reshape(batches, devices, stripe, features), AXES...]
    reshape x9 -> x4, local copies, waits for them, and re-layouts: 45.9 us -> 0.65 us  [the longest x1 0.61 us: body(): summed[9:13].reshape(-1)]
    unnamed x99 -> x39, local copies, waits for them, and re-layouts: 42.3 us -> 5.71 us
    slice x13 -> x8, local copies, waits for them, and re-layouts: 37.1 us -> 6.78 us  [the longest x1 1.63 us: body(): attn_sum[:3 * depth].reshape(3, depth, cols)]
  transfers between devices with their start and end apart: 8 -> 4, of which waited for: 6 -> 1; matrix products, arithmetic and copies ran while one was open for 24% -> 5% of each run, Pallas kernels for 7% -> 72%
where the time goes in v2:
time: 446 us; the launch traced here: 445 us
  Pallas kernels  374 us (84%)
  local copies, waits for them, and re-layouts  19.7 us (4%)
  starting transfers between devices  15.5 us (3%)
  between operations  14.4 us (3%)
  waiting for transfers between devices  11.7 us (3%)
  other arithmetic  9.14 us (2%)
    pallas_call x1, Pallas kernels, head(): pl.pallas_call(functools.partial(head_kernel, devices=devices, members=me...  126 us
    pallas_call x1, Pallas kernels, tail(): pl.pallas_call(functools.partial(tail_kernel, devices=devices, members=me...  88.8 us
    pallas_call x1, Pallas kernels, middle(): pl.pallas_call(functools.partial(middle_kernel, chunk=512), grid=(rows //...  37.5 us
    pallas_call x1, Pallas kernels, attend(): pl.pallas_call(functools.partial(attend_kernel, chunk=chunk), grid=(pairs...  36.7 us
    pallas_call x1, Pallas kernels, attend_back(): pl.pallas_call(functools.partial(attend_back_kernel, chunk=chunk), grid=(...  36.1 us
    pallas_call x1, Pallas kernels, attn_weights(): pl.pallas_call(attn_weights_kernel, grid=(members,), in_specs=[fixed(feat...  19.5 us
    pallas_call x1, Pallas kernels, ffn_weights(): pl.pallas_call(ffn_weights_kernel, grid=(members, per), in_specs=[fixed,...  16.3 us
    all_to_all x2, starting transfers between devices, deal(): lax.all_to_all(rows_val, AXES, split_axis=0, concat_axis=0, tiled=True)  15.4 us
  transfers between devices with their start and end apart: 4, of which 1 were waited for; matrix products, arithmetic and copies ran while one was open for 5% of the time, Pallas kernels for 72%

profile of v2, /device:TPU:0, one launch (start us, length us, event | category | flops | bytes accessed | tf_op | source)
XLA Modules:
  0.0 444.7 jit_solution(17581017423788044646)
XLA Ops:
  7.2 0.0 all-gather.2.cloned.1.call-start
  7.2 1.7 pad_maximum_fusion
  8.9 0.0 all-gather.2.cloned.1.call-update
  9.0 0.0 copy-start.9
  9.0 0.0 copy-start.8
  9.0 0.0 copy-start.3
  9.0 0.0 copy-start.4
  9.0 7.3 %all-to-all-start = ((bf16[32,32,768]{2,1,0:T(8,128)(2,1)}), bf16[32,32,768]{2,1,0:T(8,128)(2,1)S(1)}, u32[]{:S(2)}, u32[]{:S(2)}) async-start(bf16[32,32,768]{2,1,0:T(8,128)(2,1)} %param.17), calls=%async_computation | async-start | bytes 3145728 | tf_op jit(solution)/shard_map/all_to_all | solution.py:740
  16.4 0.0 copy-start.6
  16.4 0.0 copy-start.16
  16.4 0.0 copy-start.10
  16.4 0.0 copy-start.11
  16.4 0.0 copy-start.12
  16.4 0.0 copy-start.13
  16.4 0.0 copy-start.14
  16.4 0.0 copy-start.15
  16.4 0.0 reduce-scatter.2.cloned.1.call-start
  16.5 0.0 copy-done.8
  16.5 0.6 maximum_bitcast_fusion.bias_ref
  17.1 0.0 copy-done.4
  17.1 0.7 pad_maximum_fusion.1.shard_ref
  17.8 126.5 %head.1 = (bf16[32,32,768]{2,1,0:T(8,128)(2,1)}, bf16[2,2,2,2,2,192,384]{6,5,4,3,2,1,0:T(8,128)(2,1)}, f32[2,21,128]{2,1,0:T(8,128)}) custom-call(bf16[32,32,768]{2,1,0:T(8,128)(2,1)} %rows_ref.1, bf16[192,384]{1,0:T(8,128)(2,1)} %pad_maximum_fusion.1.shard_ref, f32[21,128]{1,0:T(8,128)} %maximum_bitcast_fusion.bias_ref), custom_call_target="tpu_custom_call" | custom-call | tf_op jit(solution)/shard_map/head/pallas_call | solution.py:594
  144.3 0.8 copy.36
  145.1 0.6 broadcast_in_dim_reshape.3.b_ref
  145.7 0.6 dynamic_slice.4
  146.3 0.6 fusion
  147.0 1.0 copy.32.live_ref
  148.0 0.6 copy.34
  148.7 0.0 copy-done.13
  148.7 3.1 multiply_sine_fusion
  151.8 12.9 %project.1.q_ref.k_ref.v_ref = bf16[3,1024,768]{2,1,0:T(8,128)(2,1)} custom-call(bf16[1024,768]{1,0:T(8,128)(2,1)} %bitcast.33, bf16[16,2,192,384]{3,2,1,0:T(8,128)(2,1)} %bitcast.29, f32[3,1,768]{2,1,0:T(1,128)} %broadcast_in_dim_reshape.3.b_ref, f32[1024,128]{1,0:T(8,128)} %get-tuple-element.65.cos_ref, f32[1024,128]{1,0:T(8,128)} %get-tuple-element.64.sine_ref), custom_call_target="tpu_custom_call" | custom-call | tf_op jit(solution)/shard_map/project/pallas_call | solution.py:73
  164.7 0.9 broadcast_in_dim.23.bias_ref
  165.6 36.7 %attend.1 = (bf16[1024,768]{1,0:T(8,128)(2,1)}, f32[6,2,1024]{2,1,0:T(2,128)}) custom-call(bf16[3,1024,768]{2,1,0:T(8,128)(2,1)} %project.1.q_ref.k_ref.v_ref, bf16[3,1024,768]{2,1,0:T(8,128)(2,1)} %project.1.q_ref.k_ref.v_ref, bf16[3,1024,768]{2,1,0:T(8,128)(2,1)} %project.1.q_ref.k_ref.v_ref, bf16[1024,128]{1,0:T(8,128)(2,1)} %broadcast_in_dim.23.bias_ref), custom_call_target="tpu_custom_call" | custom-call | tf_op jit(solution)/shard_map/attend/pallas_call | solution.py:129
  202.3 0.6 stack.31.vec_ref
  203.0 0.0 all-to-all-done
  203.0 1.1 copy-done
  204.1 37.5 %middle.1 = (bf16[1024,768]{1,0:T(8,128)(2,1)}, bf16[1024,3072]{1,0:T(8,128)(2,1)}, bf16[1024,3072]{1,0:T(8,128)(2,1)}, bf16[1024,768]{1,0:T(8,128)(2,1)}, bf16[...) custom-call(bf16[1024,768]{1,0:T(8,128)(2,1)} %bitcast.34, ...), custom_call_target="tpu_custom_call" | custom-call | tf_op jit(solution)/shard_map/middle/pallas_call | solution.py:318
  241.7 16.3 %ffn_weights.1 = bf16[16,2,96,1536]{3,2,1,0:T(8,128)(2,1)} custom-call(bf16[1024,768]{1,0:T(8,128)(2,1)} %get-tuple-element.52.mid_ref, bf16[1024,768]{1,0:T(8,128)(2,1)} %get-tuple-element.53.g_down_ref, bf16[1024,3072]{1,0:T(8,128)(2,1)} %get-tuple-element.54.act_ref, bf16[1024,3072]{1,0:T(8,128)(2,1)} %get-tuple-element.55.g_up_ref), custom_call_target="tpu_custom_call" | custom-call | tf_op jit(solution)/shard_map/ffn_weights/pallas_call | solution.py:364
  258.0 0.0 reduce-scatter.2.cloned.1.call-update
  258.0 8.1 %all-to-all-start.1 = ((bf16[32,32,768]{2,1,0:T(8,128)(2,1)}), bf16[32,32,768]{2,1,0:T(8,128)(2,1)S(1)}, u32[]{:S(2)}, u32[]{:S(2)}) async-start(bf16[32,32,768]{2,1,0:T(8,128)(2,1)} %bitcast.11), calls=%async_computation.1 | async-start | bytes 3145728 | tf_op jit(solution)/shard_map/all_to_all | solution.py:740
  266.1 36.1 %attend_back.1.raw_ref = bf16[3,1024,768]{2,1,0:T(8,128)(2,1)} custom-call(bf16[3,1024,768]{2,1,0:T(8,128)(2,1)} %project.1.q_ref.k_ref.v_ref, bf16[3,1024,768]{2,1,0:T(8,128)(2,1)} %project.1.q_ref.k_ref.v_ref, bf16[3,1024,768]{2,1,0:T(8,128)(2,1)} %project.1.q_ref.k_ref.v_ref, bf16[1024,128]{1,0:T(8,128)(2,1)} %broadcast_in_dim.23.bias_ref, ...), custom_call_target="tpu_custom_call" | custom-call | tf_op jit(solution)/shard_map/attend_back/pallas_call | solution.py:202
  302.2 19.5 %attn_weights.1 = (bf16[16,2,192,384]{3,2,1,0:T(8,128)(2,1)}, bf16[1024,768]{1,0:T(8,128)(2,1)}, f32[8,768]{1,0:T(8,128)}) custom-call(bf16[1024,768]{1,0:T(8,128)(2,1)} %bitcast.35, bf16[1024,768]{1,0:T(8,128)(2,1)} %get-tuple-element.40.g_attn_ref, bf16[1024,768]{1,0:T(8,128)(2,1)} %get-tuple-element.38.ctx_ref, bf16[3,1024,768]{2,1,0:T(8,128)(2,1)} %attend_back.1.raw_ref, ...), custom_call_target="tpu_custom_call" | custom-call | tf_op jit(solution)/shard_map/attn_weights/pallas_call | solution.py:415
  321.7 0.7 slice.50
  322.4 0.5 broadcast.83
  323.0 0.0 copy-done.7
  323.0 0.7 reduce.15
  323.7 0.0 copy-done.5
  323.7 0.6 select_maximum_fusion.small_ref
  324.3 88.8 %tail.1 = (bf16[32,32,768]{2,1,0:T(8,128)(2,1)}, f32[192,384]{1,0:T(8,128)}, f32[16,768]{1,0:T(8,128)}) custom-call(bf16[32,32,768]{2,1,0:T(8,128)(2,1)} %bitcast.39, bf16[2,2,2,2,2,192,384]{6,5,4,3,2,1,0:T(8,128)(2,1)} %bitcast.38, f32[16,768]{1,0:T(8,128)} %select_maximum_fusion.small_ref), custom_call_target="tpu_custom_call" | custom-call | tf_op jit(solution)/shard_map/tail/pallas_call | solution.py:704
  413.1 0.7 slice.59
  413.9 1.3 slice.53
  415.2 1.6 slice.52
  416.8 0.6 reshape.116
  417.4 1.6 slice_reduce_fusion
  419.0 1.5 slice_bitcast_fusion.1
  420.5 0.0 all-to-all-done.1
  420.5 11.7 %reduce-scatter.2.cloned.1.call-done = bf16[96,1536]{1,0:T(8,128)(2,1)} async-done(((bf16[3072,1536]{1,0:T(8,128)(2,1)}), bf16[96,1536]{1,0:T(8,128)(2,1)}) %reduce-scatter.2.cloned.1.call-update) | async-done | bytes 294928 | tf_op jit(solution)/shard_map/reduce_scatter | solution.py:765
  432.2 1.1 convert_element_type.22
  433.3 0.7 slice_bitcast_fusion
  434.0 0.0 copy-done.2
  434.0 0.7 slice.66
  434.8 1.1 copy.39
  435.9 0.8 copy-done.1
  436.7 1.1 copy.40
  (32 shorter events, 0.1 us)
Async XLA Ops:
  7.2 195.8 %all-gather.2.cloned.1.call-start = ((), (), s32[]{:S(2)}) async-start(), calls=%async_computation.3 | async-start | bytes 9732096 | tf_op jit(solution)/shard_map/all_gather | solution.py:743
  9.0 7.5 %copy-start.9 = (f32[3,384]{1,0:T(4,128)S(1)}, f32[3,384]{1,0:T(4,128)}, u32[]{:S(2)}) copy-start(f32[3,384]{1,0:T(4,128)} %param.21) | copy-start | bytes 13828
  9.0 7.6 %copy-start.8 = (f32[1536]{0:T(1024)S(1)}, f32[1536]{0:T(1024)}, u32[]{:S(2)}) copy-start(f32[1536]{0:T(1024)} %param.27) | copy-start | bytes 18436
  9.0 8.2 %copy-start.3 = (bf16[3,48,384]{2,1,0:T(8,128)(2,1)S(1)}, bf16[3,48,384]{2,1,0:T(8,128)(2,1)}, u32[]{:S(2)}) copy-start(bf16[3,48,384]{2,1,0:T(8,128)(2,1)} %param.20) | copy-start | bytes 331780
  9.0 8.1 %copy-start.4 = (bf16[384,48]{0,1:T(8,128)(2,1)S(1)}, bf16[384,48]{0,1:T(8,128)(2,1)}, u32[]{:S(2)}) copy-start(bf16[384,48]{0,1:T(8,128)(2,1)} %param.22) | copy-start | bytes 110596
  9.0 193.9 %all-to-all-start = ((bf16[32,32,768]{2,1,0:T(8,128)(2,1)}), bf16[32,32,768]{2,1,0:T(8,128)(2,1)S(1)}, u32[]{:S(2)}, u32[]{:S(2)}) async-start(bf16[32,32,768]{2,1,0:T(8,128)(2,1)} %param.17), calls=%async_computation | async-start | bytes 3145728 | tf_op jit(solution)/shard_map/all_to_all | solution.py:740
  16.4 129.4 %copy-start.6 = (s32[1024]{0:T(1024)S(1)}, s32[1024]{0:T(1024)}, u32[]{:S(2)}) copy-start(s32[1024]{0:T(1024)} %param.19) | copy-start | bytes 12292
  16.4 129.4 %copy-start.16 = (s32[32]{0:T(128)S(1)}, s32[32]{0:T(128)}, u32[]{:S(2)}) copy-start(s32[32]{0:T(128)} %param.18) | copy-start | bytes 388
  16.4 132.2 %copy-start.10 = (f32[768]{0:T(1024)S(1)}, f32[768]{0:T(1024)}, u32[]{:S(2)}) copy-start(f32[768]{0:T(1024)} %param.23) | copy-start | bytes 9220
  16.4 132.2 %copy-start.11 = (f32[768]{0:T(1024)S(1)}, f32[768]{0:T(1024)}, u32[]{:S(2)}) copy-start(f32[768]{0:T(1024)} %param.24) | copy-start | bytes 9220
  16.4 132.2 %copy-start.12 = (f32[768]{0:T(1024)S(1)}, f32[768]{0:T(1024)}, u32[]{:S(2)}) copy-start(f32[768]{0:T(1024)} %param.25) | copy-start | bytes 9220
  16.4 132.2 %copy-start.13 = (f32[768]{0:T(1024)S(1)}, f32[768]{0:T(1024)}, u32[]{:S(2)}) copy-start(f32[768]{0:T(1024)} %param.29) | copy-start | bytes 9220
  16.4 132.3 %copy-start.14 = (f32[768]{0:T(1024)S(1)}, f32[768]{0:T(1024)}, u32[]{:S(2)}) copy-start(f32[768]{0:T(1024)} %param.30) | copy-start | bytes 9220
  16.4 132.3 %copy-start.15 = (f32[768]{0:T(1024)S(1)}, f32[768]{0:T(1024)}, u32[]{:S(2)}) copy-start(f32[768]{0:T(1024)} %param.31) | copy-start | bytes 9220
  16.4 415.7 %reduce-scatter.2.cloned.1.call-start = ((), (), s32[]{:S(2)}) async-start(), calls=%async_computation.4 | async-start | bytes 9732096 | tf_op jit(solution)/shard_map/reduce_scatter | solution.py:765
  203.0 1.1 copy-start
  258.0 162.6 %all-to-all-start.1 = ((bf16[32,32,768]{2,1,0:T(8,128)(2,1)}), bf16[32,32,768]{2,1,0:T(8,128)(2,1)S(1)}, u32[]{:S(2)}, u32[]{:S(2)}) async-start(bf16[32,32,768]{2,1,0:T(8,128)(2,1)} %bitcast.11), calls=%async_computation.1 | async-start | bytes 3145728 | tf_op jit(solution)/shard_map/all_to_all | solution.py:740
  302.2 20.8 %copy-start.7 = (f32[1,3072]{1,0:T(1,128)S(1)}, f32[1,3072]{1,0:T(1,128)}, u32[]{:S(2)}) copy-start(f32[1,3072]{1,0:T(1,128)} %get-tuple-element.48) | copy-start | bytes 36868
  302.2 21.5 %copy-start.5 = (f32[8,768]{1,0:T(8,128)S(1)}, f32[8,768]{1,0:T(8,128)}, u32[]{:S(2)}) copy-start(f32[8,768]{1,0:T(8,128)} %get-tuple-element.47) | copy-start | bytes 73732
  432.2 1.8 copy-start.2
  434.8 2.0 copy-start.1
Sparse Core Ops, SparseCore 0:
  11.5 133.4 all-gather.1
  258.1 174.0 reduce-scatter.1

commit v3 on v2

--- a/solution.py
+++ b/solution.py
@@ -30,11 +30,9 @@
 TN = ((0,), (0,))
 
 
-def rope_tables(positions):
+def inverse_steps():
     steps = (jnp.arange(LANES) % HD // 2).astype(F32)
-    inverse = jnp.power(ROPE_BASE, -2.0 * steps / HD)
-    angles = positions.astype(F32)[:, None] * inverse[None, :]
-    return jnp.cos(angles), jnp.sin(angles)
+    return jnp.power(ROPE_BASE, -2.0 * steps / HD)[None, :]
 
 
 def turn(values, cos_table, sine_table):
@@ -53,7 +51,8 @@
 def project_kernel(x_ref, w_ref, b_ref, cos_ref, sine_ref, out_ref):
     kind = pl.program_id(0)
     depth = w_ref.shape[2]
-    raw = dot(x_ref[...], block_rows(w_ref, 0, 0, depth), NN) + b_ref[0]
+    weight = [block_rows(w_ref, t, 0, depth) for t in range(w_ref.shape[1])]
+    raw = dot(x_ref[...], jnp.concatenate(weight, axis=1), NN) + b_ref[0]
 
     @pl.when(kind < 2)
     def _():
@@ -70,17 +69,18 @@
     rows, features = x.shape
     groups, members, depth4, cols = attn_w.shape
     depth = depth4 // 4
+    tile = rows // 2
     return pl.pallas_call(
         project_kernel,
-        grid=(3, members),
+        grid=(3, rows // tile),
         in_specs=[
-            pl.BlockSpec((rows, features), lambda p, c: (0, 0)),
-            pl.BlockSpec((groups, 1, depth, cols), lambda p, c: (0, c, p, 0)),
-            pl.BlockSpec((1, 1, cols), lambda p, c: (p, 0, c)),
-            pl.BlockSpec((rows, LANES), lambda p, c: (0, 0)),
-            pl.BlockSpec((rows, LANES), lambda p, c: (0, 0)),
-        ],
-        out_specs=pl.BlockSpec((1, rows, cols), lambda p, c: (p, 0, c)),
+            pl.BlockSpec((tile, features), lambda p, r: (r, 0)),
+            pl.BlockSpec((groups, members, depth, cols), lambda p, r: (0, 0, p, 0)),
+            pl.BlockSpec((1, 1, features), lambda p, r: (p, 0, 0)),
+            pl.BlockSpec((tile, LANES), lambda p, r: (r, 0)),
+            pl.BlockSpec((tile, LANES), lambda p, r: (r, 0)),
+        ],
+        out_specs=pl.BlockSpec((1, tile, features), lambda p, r: (p, r, 0)),
         out_shape=jax.ShapeDtypeStruct((3, rows, features), BF),
         compiler_params=pltpu.CompilerParams(vmem_limit_bytes=VMEM_BYTES),
         name="project",
@@ -102,6 +102,10 @@
     q = q_ref[0] * jnp.asarray(SCORE_SCALE, BF)
     k = k_ref[0]
     v_turned = v_ref[0].T
+    ones = jnp.ones((16, rows), BF)
+    v_heads = [
+        jnp.concatenate([v_turned[head * HD : (head + 1) * HD], ones], axis=0) for head in range(2)
+    ]
     bias = bias_ref[...]
     for part in range(rows // chunk):
         span = slice(part * chunk, (part + 1) * chunk)
@@ -109,11 +113,12 @@
         for head in range(2):
             q_head, k_head = pair_operands(q, k, bias, lane, head)
             scores = dot(k_head, q_head[span], NT)
-            top = jnp.max(scores, axis=0, keepdims=True)
+            tops = jnp.max(scores.reshape(16, rows // 16, chunk), axis=0)
+            top = jnp.max(tops, axis=0, keepdims=True)
             expo = jnp.exp(scores - top)
-            total = jnp.sum(expo, axis=0, keepdims=True)
-            mixed = dot(v_turned[head * HD : (head + 1) * HD], expo.astype(BF), NN)
-            outs.append(mixed / total)
+            mixed = dot(v_heads[head], expo.astype(BF), NN)
+            total = mixed[HD : HD + 1]
+            outs.append(mixed[:HD] / total)
             lse_ref[0, head : head + 1, span] = top + jnp.log(total)
         ctx_ref[span, :] = jnp.concatenate(outs, axis=0).T.astype(BF)
 
@@ -121,7 +126,7 @@
 def attend(qkv, bias):
     _, rows, features = qkv.shape
     pairs = features // LANES
-    chunk = 256
+    chunk = rows
 
     def spec(which):
         return pl.BlockSpec((1, rows, LANES), lambda h: (which, 0, h))
@@ -230,7 +235,9 @@
 
 
 def column_sum(values):
-    return jnp.sum(values, axis=0, keepdims=True)
+    rows = values.shape[0]
+    grouped = jnp.sum(values.reshape(rows // 32, 32, values.shape[1]), axis=0)
+    return jnp.sum(grouped, axis=0, keepdims=True)
 
 
 def middle_kernel(
@@ -268,7 +275,7 @@
     result, unit_two, inv_two = normalize(second_sum, gain_two, shift_two)
     mixed_ref[...] = result.astype(BF)
 
-    grad_out = jnp.where(live_ref[...] > 0.0, cot_ref[...].astype(F32), 0.0)
+    grad_out = jnp.where(live_ref[:, 0:1].astype(F32) == 0.0, cot_ref[...].astype(F32), 0.0)
     grad_second = normalize_back(grad_out * gain_two, unit_two, inv_two)
     small_ref[5:6] += column_sum(grad_out * unit_two)
     small_ref[6:7] += column_sum(grad_out)
@@ -319,7 +326,7 @@
         functools.partial(middle_kernel, chunk=512),
         grid=(rows // tile,),
         in_specs=[
-            row(features), row(features), row(features), row(1),
+            row(features), row(features), row(features), row(LANES),
             fixed((groups, members, depth4 // 4, cols), (0, 0, 3, 0)),
             fixed((groups, members, ffn_rows, units), (0, 0, 0, 0)),
             fixed((8, features), (0, 0)), fixed((1, width), (0, 0)),
@@ -456,13 +463,11 @@
     return w.reshape(groups, members, rows // groups, cols)
 
 
-def layer(rows, cotangent, place, length, cos_table, sine_table, attn_w, ffn_w, b_qkv, b_up, vectors):
-    live = place < length
-    bias = jnp.broadcast_to(jnp.where(live, 0.0, MASK_FILL).astype(BF)[:, None], (rows.shape[0], LANES))
+def layer(rows, cotangent, bias, cos_table, sine_table, attn_w, ffn_w, b_qkv, b_up, vectors):
     qkv = project(rows, attn_w, b_qkv[:, None, :], cos_table, sine_table)
     context, lse = attend(qkv, bias)
     mixed, act, g_up, mid, g_down, g_attn, g_first, g_ctx, small, small_up = middle(
-        rows, context, cotangent, live.astype(F32)[:, None], attn_w, ffn_w, vectors, b_up
+        rows, context, cotangent, bias, attn_w, ffn_w, vectors, b_up
     )
     g_ffn = ffn_weights(mid, g_down, act, g_up, ffn_w.shape[0], ffn_w.shape[1])
     g_raw = attend_back(qkv, bias, context, g_ctx, lse, cos_table, sine_table)
@@ -518,23 +523,34 @@
         pl.semaphore_wait(barrier, self.devices - 1)
 
     def swap(self, src, dst, send_sem, recv_sem, offset):
-        target = (self.me + offset) % self.devices
+        target = self.other(offset)
         return pltpu.make_async_remote_copy(
             src_ref=src.at[target], dst_ref=dst.at[self.me], send_sem=send_sem.at[offset],
             recv_sem=recv_sem.at[offset], device_id=self.ident(target), device_id_type=MESH,
         )
 
-    def for_others(self, action):
+    def other(self, offset):
+        planes = self.devices // 8
+        return (self.me // 8 + offset // 8) % planes * 8 + (self.me + offset) % 8
+
+    def for_others(self, action, first=1, last=None):
         def one(offset, carry):
             action(offset)
             return carry
 
-        lax.fori_loop(1, self.devices, one, 0)
+        lax.fori_loop(first, self.devices if last is None else last, one, 0)
+
+    def share(self, step, near_first):
+        cuts = [1, 4, 8, 18, 28, 32] if near_first else [32, 24, 14, 8, 4, 1]
+        if self.devices != 32:
+            cuts = [1 + (self.devices - 1) * s // self.bits for s in range(self.bits + 1)]
+        first, last = cuts[step], cuts[step + 1]
+        return min(first, last), max(first, last)
 
 
 def head_kernel(
-    rows_ref, shard_ref, bias_ref, seq_ref, attn_ref, biases_ref, held_ref,
-    send_sem, recv_sem, w_send, w_recv, b_sem, local_sem, *, devices, members
+    rows_ref, shard_ref, bias_ref, place_ref, length_ref, inverse_ref,
+    seq_ref, attn_ref, biases_ref, cos_ref, sine_ref, mask_ref, held_ref, send_sem, recv_sem, w_send, w_recv, b_sem, local_sem, *, devices, members
 ):
     here = Place(devices, members)
     bits = here.bits
@@ -567,10 +583,17 @@
     for copy in moving:
         copy.start()
     to_member.start()
-    here.for_others(lambda o: here.swap(rows_ref, seq_ref, send_sem, recv_sem, o).start())
+    here.for_others(lambda o: here.swap(rows_ref, seq_ref, send_sem, recv_sem, o).start(), *here.share(0, True))
     mine.wait()
     back = pltpu.make_async_copy(held_ref, seq_ref.at[here.me], local_sem.at[0])
     back.start()
+    place = place_ref[...]
+    angles = place.astype(F32) * inverse_ref[...]
+    cos_ref[...] = jnp.cos(angles)
+    sine_ref[...] = jnp.sin(angles)
+    mask_ref[...] = jnp.where(
+        jnp.broadcast_to(place, mask_ref.shape) < length_ref[...], 0.0, MASK_FILL
+    ).astype(BF)
     own.wait()
     own_bias.wait()
     for step in range(bits):
@@ -579,26 +602,35 @@
             if step + 1 < bits:
                 moving[c] = spread(c, step + 1)
                 moving[c].start()
+        if step + 1 < bits:
+            here.for_others(
+                lambda o: here.swap(rows_ref, seq_ref, send_sem, recv_sem, o).start(),
+                *here.share(step + 1, True),
+            )
     to_member.wait()
     back.wait()
     here.for_others(lambda o: here.swap(rows_ref, seq_ref, send_sem, recv_sem, o).wait())
 
 
-def head(tokens, attn_shard, biases, members):
+def head(tokens, attn_shard, biases, order, length, members):
     devices, stripe, features = tokens.shape
     bits = devices.bit_length() - 1
     colours = len(axis_orders(bits, attn_shard.shape[0]))
     anywhere = pl.BlockSpec(memory_space=pl.ANY)
     onchip = pl.BlockSpec(memory_space=pltpu.VMEM)
     sems = pltpu.SemaphoreType.DMA
-    seq, attn, both = pl.pallas_call(
+    slot = order.shape[0]
+    seq, attn, both, cos_table, sine_table, mask = pl.pallas_call(
         functools.partial(head_kernel, devices=devices, members=members),
-        in_specs=[anywhere, onchip, onchip],
-        out_specs=[anywhere, anywhere, anywhere],
+        in_specs=[anywhere] + [onchip] * 5,
+        out_specs=[anywhere] * 3 + [onchip] * 3,
         out_shape=[
             jax.ShapeDtypeStruct(tokens.shape, BF),
             jax.ShapeDtypeStruct((2,) * bits + attn_shard.shape, BF),
             jax.ShapeDtypeStruct((members,) + biases.shape, F32),
+            jax.ShapeDtypeStruct((slot, LANES), F32),
+            jax.ShapeDtypeStruct((slot, LANES), F32),
+            jax.ShapeDtypeStruct((slot, LANES), BF),
         ],
         scratch_shapes=[
             pltpu.VMEM((stripe, features), BF), sems((devices,)), sems((devices,)),
@@ -606,8 +638,8 @@
         ],
         compiler_params=pltpu.CompilerParams(collective_id=0, has_side_effects=True),
         name="head",
-    )(tokens, attn_shard, biases)
-    return seq, attn.reshape((devices,) + attn_shard.shape), both
+    )(tokens, attn_shard, biases, order[:, None], length.reshape(1, 1), inverse_steps())
+    return seq, attn.reshape((devices,) + attn_shard.shape), both, cos_table, sine_table, mask
 
 
 def tail_kernel(
@@ -659,7 +691,7 @@
         copy.start()
     small = hand_small(0)
     small.start()
-    here.for_others(lambda o: here.swap(rows_ref, back_ref, send_sem, recv_sem, o).start())
+    here.for_others(lambda o: here.swap(rows_ref, back_ref, send_sem, recv_sem, o).start(), *here.share(0, False))
     mine.wait()
     back = pltpu.make_async_copy(held_ref, back_ref.at[here.me], local_sem.at[0])
     back.start()
@@ -675,6 +707,11 @@
             else:
                 start, size, _ = colours[c]
                 sum_ref[start : start + size] = added.astype(F32)
+        if step + 1 < bits:
+            here.for_others(
+                lambda o: here.swap(rows_ref, back_ref, send_sem, recv_sem, o).start(),
+                *here.share(step + 1, False),
+            )
         small.wait()
         before = small_ref[...] if step == 0 else small_kept[step - 1]
         after = before + small_got[step]
@@ -744,21 +781,23 @@
     ffn_w = merge_groups(ffn_all.reshape(dp_size, tp_size, 2 * depth, units), 2)
     attn_shard = jnp.concatenate([w_qkv.reshape(3 * depth, cols), w_out.T], axis=0)
     biases = jnp.concatenate([b_qkv.reshape(-1), b_up]).reshape(-1, LANES)
-    rows, attn_all, biases = head(tokens, attn_shard, biases, tp_size)
+    length = lax.dynamic_index_in_dim(lengths, me, 0, keepdims=False)
+    rows, attn_all, biases, cos_table, sine_table, mask = head(
+        tokens, attn_shard, biases, order, length, tp_size
+    )
     rows = rows.reshape(slot, features)
     attn_w = merge_groups(attn_all.reshape(dp_size, tp_size, 4 * depth, cols), 4)
     biases = biases.reshape(tp_size, -1)
     b_qkv_all = biases[:, : 3 * cols].reshape(tp_size, 3, cols).transpose(1, 0, 2).reshape(3, features)
     b_up_all = biases[:, 3 * cols :].reshape(1, tp_size * units)
+    rows, out_grad = lax.optimization_barrier((rows, out_grad))
     cotangent = deal(out_grad).reshape(slot, features)
-    cos_table, sine_table = rope_tables(order)
     none = jnp.zeros_like(b_out)
     vectors = jnp.stack(
         [b_out, norm1_gain, norm1_bias, b_down, norm2_gain, norm2_bias, none, none], axis=0
     )
-    length = lax.dynamic_index_in_dim(lengths, me, 0, keepdims=False)
     result, grad_rows, g_attn_w, g_ffn, packed = layer(
-        rows, cotangent, order, length, cos_table, sine_table, attn_w, ffn_w, b_qkv_all, b_up_all, vectors
+        rows, cotangent, mask, cos_table, sine_table, attn_w, ffn_w, b_qkv_all, b_up_all, vectors
     )
     mixed = deal(result.reshape(devices, stripe, features))
     laid = split_groups(g_ffn, 2, dp_size).reshape(devices * 2 * depth, units)

time: 446 us -> 396 us (0.89)
  Pallas kernels: 374 us -> 321 us
    pallas_call x1, Pallas kernels: 126 us -> 90.3 us  [head(): pl.pallas_call(functools.partial(head_kernel, devices=devices, members=me...]
    pallas_call x1, Pallas kernels: 36.7 us -> 21.7 us  [attend(): pl.pallas_call(functools.partial(attend_kernel, chunk=chunk), grid=(pairs...]
  transfers between devices with their start and end apart: 4 -> 4, of which waited for: 1 -> 2; matrix products, arithmetic and copies ran while one was open for 5% -> 5% of each run, Pallas kernels for 72% -> 68%
where the time goes in v3:
time: 396 us; the launch traced here: 395 us
  Pallas kernels  321 us (81%)
  local copies, waits for them, and re-layouts  20.1 us (5%)
  starting transfers between devices  17.8 us (4%)
  waiting for transfers between devices  14.4 us (4%)
  between operations  14.3 us (4%)
  other arithmetic  7.53 us (2%)
    pallas_call x1, Pallas kernels, head(): pl.pallas_call(functools.partial(head_kernel, devices=devices, members=me...  90.3 us
    pallas_call x1, Pallas kernels, tail(): pl.pallas_call(functools.partial(tail_kernel, devices=devices, members=me...  87.3 us
    pallas_call x1, Pallas kernels, middle(): pl.pallas_call(functools.partial(middle_kernel, chunk=512), grid=(rows //...  37.6 us
    pallas_call x1, Pallas kernels, attend_back(): pl.pallas_call(functools.partial(attend_back_kernel, chunk=chunk), grid=(...  36.1 us
    pallas_call x1, Pallas kernels, attend(): pl.pallas_call(functools.partial(attend_kernel, chunk=chunk), grid=(pairs...  21.7 us
    pallas_call x1, Pallas kernels, attn_weights(): pl.pallas_call(attn_weights_kernel, grid=(members,), in_specs=[fixed(feat...  19.5 us
    all_to_all x2, starting transfers between devices, deal(): lax.all_to_all(rows_val, AXES, split_axis=0, concat_axis=0, tiled=True)  17.6 us
    pallas_call x1, Pallas kernels, ffn_weights(): pl.pallas_call(ffn_weights_kernel, grid=(members, per), in_specs=[fixed,...  16.3 us
  transfers between devices with their start and end apart: 4, of which 2 were waited for; matrix products, arithmetic and copies ran while one was open for 5% of the time, Pallas kernels for 68%

profile of v3, /device:TPU:0, one launch (start us, length us, event | category | flops | bytes accessed | tf_op | source)
XLA Modules:
  0.0 395.0 jit_solution(221371030378746554)
XLA Ops:
  7.2 0.0 all-gather.2.cloned.1.call-start
  7.2 1.7 pad_maximum_fusion
  8.9 0.0 all-gather.2.cloned.1.call-update
  9.0 1.7 copy.31.place_ref
  10.7 0.7 reshape.154
  11.4 1.2 dynamic_slice.4
  12.6 0.5 multiply_power_fusion.inverse_ref
  13.1 1.3 maximum_bitcast_fusion.bias_ref
  14.4 1.6 pad_maximum_fusion.1.shard_ref
  16.0 90.3 %head.1 = (bf16[32,32,768]{2,1,0:T(8,128)(2,1)}, bf16[2,2,2,2,2,192,384]{6,5,4,3,2,1,0:T(8,128)(2,1)}, f32[2,21,128]{2,1,0:T(8,128)}, f32[1024,128]{1,0:T(8,128)...) custom-call(bf16[32,32,768]{2,1,0:T(8,128)(2,1)} %rows_ref.1, bf16[192,384]{1,0:T(8,128)(2,1)} %pad_maximum_fusion.1.shard_ref, ...), custom_call_target="tpu_custom_call" | custom-call | tf_op jit(solution)/shard_map/head/pallas_call | solution.py:623
  106.3 0.0 copy-start.4
  106.4 0.0 copy-start.6
  106.4 0.0 copy-start.7
  106.4 0.0 copy-start.8
  106.4 0.0 copy-start.9
  106.4 0.0 copy-start.10
  106.4 0.0 copy-start.11
  106.4 14.1 %all-to-all-start = ((bf16[32,32,768]{2,1,0:T(8,128)(2,1)}), bf16[32,32,768]{2,1,0:T(8,128)(2,1)S(1)}, u32[]{:S(2)}, u32[]{:S(2)}) async-start(bf16[32,32,768]{2,1,0:T(8,128)(2,1)} %param.17), calls=%async_computation | async-start | bytes 3145728 | tf_op jit(solution)/shard_map/all_to_all | solution.py:777
  120.6 0.2 reduce-scatter.2.cloned.1.call-start
  120.8 0.0 copy-done.4
  120.9 0.6 broadcast_in_dim_reshape.3.b_ref
  121.5 0.6 copy.34
  122.1 0.0 copy-done.6
  122.1 0.0 copy-done.7
  122.1 0.0 copy-done.8
  122.2 0.0 copy-done.9
  122.2 0.0 copy-done.10
  122.2 0.0 copy-done.11
  122.2 12.1 %project.1.q_ref.k_ref.v_ref = bf16[3,1024,768]{2,1,0:T(8,128)(2,1)} custom-call(bf16[1024,768]{1,0:T(8,128)(2,1)} %bitcast.33, bf16[16,2,192,384]{3,2,1,0:T(8,128)(2,1)} %bitcast.29, f32[3,1,768]{2,1,0:T(1,128)} %broadcast_in_dim_reshape.3.b_ref, f32[1024,128]{1,0:T(8,128)} %get-tuple-element.44.cos_ref, f32[1024,128]{1,0:T(8,128)} %get-tuple-element.45.sine_ref), custom_call_target="tpu_custom_call" | custom-call | tf_op jit(solution)/shard_map/project/pallas_call | solution.py:73
  134.3 21.7 %attend.1 = (bf16[1024,768]{1,0:T(8,128)(2,1)}, f32[6,2,1024]{2,1,0:T(2,128)}) custom-call(bf16[3,1024,768]{2,1,0:T(8,128)(2,1)} %project.1.q_ref.k_ref.v_ref, bf16[3,1024,768]{2,1,0:T(8,128)(2,1)} %project.1.q_ref.k_ref.v_ref, bf16[3,1024,768]{2,1,0:T(8,128)(2,1)} %project.1.q_ref.k_ref.v_ref, bf16[1024,128]{1,0:T(8,128)(2,1)} %get-tuple-element.46.bias_ref.live_ref), custom_call_target="tpu_custom_call" | custom-call | tf_op jit(solution)/shard_map/attend/pallas_call | solution.py:134
  156.0 0.6 stack.31.vec_ref
  156.7 2.7 all-to-all-done
  159.4 0.0 copy-start
  159.4 0.0 all-gather.2.cloned.1.call-done
  159.4 1.1 copy-done
  160.5 37.6 %middle.1 = (bf16[1024,768]{1,0:T(8,128)(2,1)}, bf16[1024,3072]{1,0:T(8,128)(2,1)}, bf16[1024,3072]{1,0:T(8,128)(2,1)}, bf16[1024,768]{1,0:T(8,128)(2,1)}, bf16[...) custom-call(bf16[1024,768]{1,0:T(8,128)(2,1)} %bitcast.34, ...), custom_call_target="tpu_custom_call" | custom-call | tf_op jit(solution)/shard_map/middle/pallas_call | solution.py:325
  198.1 16.3 %ffn_weights.1 = bf16[16,2,96,1536]{3,2,1,0:T(8,128)(2,1)} custom-call(bf16[1024,768]{1,0:T(8,128)(2,1)} %get-tuple-element.62.mid_ref, bf16[1024,768]{1,0:T(8,128)(2,1)} %get-tuple-element.63.g_down_ref, bf16[1024,3072]{1,0:T(8,128)(2,1)} %get-tuple-element.64.act_ref, bf16[1024,3072]{1,0:T(8,128)(2,1)} %get-tuple-element.65.g_up_ref), custom_call_target="tpu_custom_call" | custom-call | tf_op jit(solution)/shard_map/ffn_weights/pallas_call | solution.py:371
  214.4 0.0 reduce-scatter.2.cloned.1.call-update
  214.4 3.4 all-to-all-start.1
  217.9 36.1 %attend_back.1.raw_ref = bf16[3,1024,768]{2,1,0:T(8,128)(2,1)} custom-call(bf16[3,1024,768]{2,1,0:T(8,128)(2,1)} %project.1.q_ref.k_ref.v_ref, bf16[3,1024,768]{2,1,0:T(8,128)(2,1)} %project.1.q_ref.k_ref.v_ref, bf16[3,1024,768]{2,1,0:T(8,128)(2,1)} %project.1.q_ref.k_ref.v_ref, bf16[1024,128]{1,0:T(8,128)(2,1)} %get-tuple-element.46.bias_ref.live_ref, ...), custom_call_target="tpu_custom_call" | custom-call | tf_op jit(solution)/shard_map/attend_back/pallas_call | solution.py:207
  254.0 0.0 copy-start.5
  254.0 19.5 %attn_weights.1 = (bf16[16,2,192,384]{3,2,1,0:T(8,128)(2,1)}, bf16[1024,768]{1,0:T(8,128)(2,1)}, f32[8,768]{1,0:T(8,128)}) custom-call(bf16[1024,768]{1,0:T(8,128)(2,1)} %bitcast.35, bf16[1024,768]{1,0:T(8,128)(2,1)} %get-tuple-element.50.g_attn_ref, bf16[1024,768]{1,0:T(8,128)(2,1)} %get-tuple-element.47.ctx_ref, bf16[3,1024,768]{2,1,0:T(8,128)(2,1)} %attend_back.1.raw_ref, ...), custom_call_target="tpu_custom_call" | custom-call | tf_op jit(solution)/shard_map/attn_weights/pallas_call | solution.py:422
  273.6 0.7 slice.50
  274.3 0.5 broadcast.117
  274.8 0.0 copy-done.5
  274.8 0.7 reduce.15
  275.5 0.0 copy-done.3
  275.5 0.6 select_maximum_fusion.small_ref
  276.2 87.3 %tail.1 = (bf16[32,32,768]{2,1,0:T(8,128)(2,1)}, f32[192,384]{1,0:T(8,128)}, f32[16,768]{1,0:T(8,128)}) custom-call(bf16[32,32,768]{2,1,0:T(8,128)(2,1)} %bitcast.39, bf16[2,2,2,2,2,192,384]{6,5,4,3,2,1,0:T(8,128)(2,1)} %bitcast.38, f32[16,768]{1,0:T(8,128)} %select_maximum_fusion.small_ref), custom_call_target="tpu_custom_call" | custom-call | tf_op jit(solution)/shard_map/tail/pallas_call | solution.py:741
  363.5 0.7 slice.59
  364.2 1.3 slice.53
  365.5 1.6 slice.52
  367.2 0.6 reshape.168
  367.8 1.6 slice_reduce_fusion
  369.4 1.5 slice_bitcast_fusion.1
  370.9 0.0 all-to-all-done.1
  370.9 11.6 %reduce-scatter.2.cloned.1.call-done = bf16[96,1536]{1,0:T(8,128)(2,1)} async-done(((bf16[3072,1536]{1,0:T(8,128)(2,1)}), bf16[96,1536]{1,0:T(8,128)(2,1)}) %reduce-scatter.2.cloned.1.call-update) | async-done | bytes 294928 | tf_op jit(solution)/shard_map/reduce_scatter | solution.py:804
  382.5 1.1 convert_element_type.16
  383.6 0.7 slice_bitcast_fusion
  384.3 0.0 copy-done.2
  384.3 0.7 slice.66
  385.1 1.1 copy.39
  386.2 0.8 copy-done.1
  387.0 1.1 copy.40
  (17 shorter events, 0.1 us)
Async XLA Ops:
  7.2 152.2 %all-gather.2.cloned.1.call-start = ((), (), s32[]{:S(2)}) async-start(), calls=%async_computation.3 | async-start | bytes 9732096 | tf_op jit(solution)/shard_map/all_gather | solution.py:780
  106.3 14.5 %copy-start.4 = (f32[2,21,128]{2,1,0:T(8,128)S(1)}, f32[2,21,128]{2,1,0:T(8,128)}, u32[]{:S(2)}) copy-start(f32[2,21,128]{2,1,0:T(8,128)} %get-tuple-element.43) | copy-start | bytes 64516
  106.4 15.8 %copy-start.6 = (f32[768]{0:T(1024)S(1)}, f32[768]{0:T(1024)}, u32[]{:S(2)}) copy-start(f32[768]{0:T(1024)} %param.23) | copy-start | bytes 9220
  106.4 15.8 %copy-start.7 = (f32[768]{0:T(1024)S(1)}, f32[768]{0:T(1024)}, u32[]{:S(2)}) copy-start(f32[768]{0:T(1024)} %param.24) | copy-start | bytes 9220
  106.4 15.8 %copy-start.8 = (f32[768]{0:T(1024)S(1)}, f32[768]{0:T(1024)}, u32[]{:S(2)}) copy-start(f32[768]{0:T(1024)} %param.25) | copy-start | bytes 9220
  106.4 15.8 %copy-start.9 = (f32[768]{0:T(1024)S(1)}, f32[768]{0:T(1024)}, u32[]{:S(2)}) copy-start(f32[768]{0:T(1024)} %param.29) | copy-start | bytes 9220
  106.4 15.8 %copy-start.10 = (f32[768]{0:T(1024)S(1)}, f32[768]{0:T(1024)}, u32[]{:S(2)}) copy-start(f32[768]{0:T(1024)} %param.30) | copy-start | bytes 9220
  106.4 15.8 %copy-start.11 = (f32[768]{0:T(1024)S(1)}, f32[768]{0:T(1024)}, u32[]{:S(2)}) copy-start(f32[768]{0:T(1024)} %param.31) | copy-start | bytes 9220
  106.4 53.0 %all-to-all-start = ((bf16[32,32,768]{2,1,0:T(8,128)(2,1)}), bf16[32,32,768]{2,1,0:T(8,128)(2,1)S(1)}, u32[]{:S(2)}, u32[]{:S(2)}) async-start(bf16[32,32,768]{2,1,0:T(8,128)(2,1)} %param.17), calls=%async_computation | async-start | bytes 3145728 | tf_op jit(solution)/shard_map/all_to_all | solution.py:777
  120.6 261.9 %reduce-scatter.2.cloned.1.call-start = ((), (), s32[]{:S(2)}) async-start(), calls=%async_computation.4 | async-start | bytes 9732096 | tf_op jit(solution)/shard_map/reduce_scatter | solution.py:804
  159.4 1.1 copy-start
  214.4 156.5 %all-to-all-start.1 = ((bf16[32,32,768]{2,1,0:T(8,128)(2,1)}), bf16[32,32,768]{2,1,0:T(8,128)(2,1)S(1)}, u32[]{:S(2)}, u32[]{:S(2)}) async-start(bf16[32,32,768]{2,1,0:T(8,128)(2,1)} %bitcast.11), calls=%async_computation.1 | async-start | bytes 3145728 | tf_op jit(solution)/shard_map/all_to_all | solution.py:777
  254.0 20.8 %copy-start.5 = (f32[1,3072]{1,0:T(1,128)S(1)}, f32[1,3072]{1,0:T(1,128)}, u32[]{:S(2)}) copy-start(f32[1,3072]{1,0:T(1,128)} %get-tuple-element.58) | copy-start | bytes 36868
  254.0 21.5 %copy-start.3 = (f32[8,768]{1,0:T(8,128)S(1)}, f32[8,768]{1,0:T(8,128)}, u32[]{:S(2)}) copy-start(f32[8,768]{1,0:T(8,128)} %get-tuple-element.57) | copy-start | bytes 73732
  382.5 1.8 copy-start.2
  385.1 2.0 copy-start.1
Sparse Core Ops, SparseCore 0:
  11.5 117.4 all-gather.1
  214.6 167.9 reduce-scatter.1

commit v4 on v3

--- a/solution.py
+++ b/solution.py
@@ -19,6 +19,7 @@
 BF = jnp.bfloat16
 F32 = jnp.float32
 VMEM_BYTES = 60 * 1024 * 1024
+VMEM_LESS = 32 * 1024 * 1024
 
 
 def dot(a, b, dims):
@@ -69,7 +70,7 @@
     rows, features = x.shape
     groups, members, depth4, cols = attn_w.shape
     depth = depth4 // 4
-    tile = rows // 2
+    tile = rows
     return pl.pallas_call(
         project_kernel,
         grid=(3, rows // tile),
@@ -82,7 +83,7 @@
         ],
         out_specs=pl.BlockSpec((1, tile, features), lambda p, r: (p, r, 0)),
         out_shape=jax.ShapeDtypeStruct((3, rows, features), BF),
-        compiler_params=pltpu.CompilerParams(vmem_limit_bytes=VMEM_BYTES),
+        compiler_params=pltpu.CompilerParams(vmem_limit_bytes=VMEM_LESS),
         name="project",
     )(x, attn_w, b, cos_table, sine_table)
 
@@ -143,7 +144,7 @@
             jax.ShapeDtypeStruct((rows, features), BF),
             jax.ShapeDtypeStruct((pairs, 2, rows), F32),
         ],
-        compiler_params=pltpu.CompilerParams(vmem_limit_bytes=VMEM_BYTES),
+        compiler_params=pltpu.CompilerParams(vmem_limit_bytes=VMEM_LESS),
         name="attend",
     )(qkv, qkv, qkv, bias)
 
@@ -363,7 +364,7 @@
 def ffn_weights(mid, grad_down, act, grad_up, groups, members):
     rows, features = mid.shape
     units = act.shape[1] // members
-    chunk = 512
+    chunk = 768
     per = units // chunk
     fixed = pl.BlockSpec((rows, features), lambda t, j: (0, 0), pipeline_mode=pl.Buffered(1))
     part = pl.BlockSpec((rows, chunk), lambda t, j: (0, t * per + j))
@@ -587,13 +588,14 @@
     mine.wait()
     back = pltpu.make_async_copy(held_ref, seq_ref.at[here.me], local_sem.at[0])
     back.start()
-    place = place_ref[...]
-    angles = place.astype(F32) * inverse_ref[...]
+    place = jnp.broadcast_to(place_ref[...].astype(F32), (LANES, place_ref.shape[1])).T
+    angles = place * inverse_ref[...]
     cos_ref[...] = jnp.cos(angles)
     sine_ref[...] = jnp.sin(angles)
-    mask_ref[...] = jnp.where(
-        jnp.broadcast_to(place, mask_ref.shape) < length_ref[...], 0.0, MASK_FILL
-    ).astype(BF)
+    lengths = length_ref[...].astype(F32)
+    ours = lax.broadcasted_iota(jnp.int32, lengths.shape, 1) == here.me
+    length = jnp.sum(jnp.where(ours, lengths, 0.0), axis=1, keepdims=True)
+    mask_ref[...] = jnp.where(place < length, 0.0, MASK_FILL).astype(BF)
     own.wait()
     own_bias.wait()
     for step in range(bits):
@@ -612,7 +614,7 @@
     here.for_others(lambda o: here.swap(rows_ref, seq_ref, send_sem, recv_sem, o).wait())
 
 
-def head(tokens, attn_shard, biases, order, length, members):
+def head(tokens, attn_shard, biases, order, lengths, members):
     devices, stripe, features = tokens.shape
     bits = devices.bit_length() - 1
     colours = len(axis_orders(bits, attn_shard.shape[0]))
@@ -638,7 +640,7 @@
         ],
         compiler_params=pltpu.CompilerParams(collective_id=0, has_side_effects=True),
         name="head",
-    )(tokens, attn_shard, biases, order[:, None], length.reshape(1, 1), inverse_steps())
+    )(tokens, attn_shard, biases, order[None, :], lengths[None, :], inverse_steps())
     return seq, attn.reshape((devices,) + attn_shard.shape), both, cos_table, sine_table, mask
 
 
@@ -766,7 +768,6 @@
     dp_size = lax.axis_size("dp")
     tp_size = lax.axis_size("tensor")
     devices = dp_size * tp_size
-    me = lax.axis_index(AXES)
     stored, stripe, features = tokens.shape
     slot = devices * stripe
     depth = w_qkv.shape[1]
@@ -781,9 +782,8 @@
     ffn_w = merge_groups(ffn_all.reshape(dp_size, tp_size, 2 * depth, units), 2)
     attn_shard = jnp.concatenate([w_qkv.reshape(3 * depth, cols), w_out.T], axis=0)
     biases = jnp.concatenate([b_qkv.reshape(-1), b_up]).reshape(-1, LANES)
-    length = lax.dynamic_index_in_dim(lengths, me, 0, keepdims=False)
     rows, attn_all, biases, cos_table, sine_table, mask = head(
-        tokens, attn_shard, biases, order, length, tp_size
+        tokens, attn_shard, biases, order, lengths, tp_size
     )
     rows = rows.reshape(slot, features)
     attn_w = merge_groups(attn_all.reshape(dp_size, tp_size, 4 * depth, cols), 4)

time: 396 us -> 390 us (0.985)
  Pallas kernels: 321 us -> 306 us
  waiting for transfers between devices: 14.4 us -> 27.8 us
  starting transfers between devices: 17.8 us -> 13.4 us
    all_to_all x2, waiting for transfers between devices: 2.74 us -> 16.2 us  [deal(): lax.all_to_all(rows_val, AXES, split_axis=0, concat_axis=0, tiled=True)]
    pallas_call x1, Pallas kernels: 90.3 us -> 81.8 us  [head(): pl.pallas_call(functools.partial(head_kernel, devices=devices, members=me...]
    all_to_all x2, starting transfers between devices: 17.6 us -> 13.3 us  [deal(): lax.all_to_all(rows_val, AXES, split_axis=0, concat_axis=0, tiled=True)]
  transfers between devices with their start and end apart: 4 -> 4, of which waited for: 2 -> 2; matrix products, arithmetic and copies ran while one was open for 5% -> 4% of each run, Pallas kernels for 68% -> 65%
where the time goes in v4:
time: 390 us; the launch traced here: 389 us
  Pallas kernels  306 us (78%)
  waiting for transfers between devices  27.8 us (7%)
  local copies, waits for them, and re-layouts  19.5 us (5%)
  between operations  14.4 us (4%)
  starting transfers between devices  13.4 us (3%)
  other arithmetic  7.53 us (2%)
    pallas_call x1, Pallas kernels, tail(): pl.pallas_call(functools.partial(tail_kernel, devices=devices, members=me...  86.4 us
    pallas_call x1, Pallas kernels, head(): pl.pallas_call(functools.partial(head_kernel, devices=devices, members=me...  81.8 us
    pallas_call x1, Pallas kernels, middle(): pl.pallas_call(functools.partial(middle_kernel, chunk=512), grid=(rows //...  37.7 us
    pallas_call x1, Pallas kernels, attend_back(): pl.pallas_call(functools.partial(attend_back_kernel, chunk=chunk), grid=(...  36 us
    pallas_call x1, Pallas kernels, attend(): pl.pallas_call(functools.partial(attend_kernel, chunk=chunk), grid=(pairs...  20.7 us
    pallas_call x1, Pallas kernels, attn_weights(): pl.pallas_call(attn_weights_kernel, grid=(members,), in_specs=[fixed(feat...  19.5 us
    all_to_all x2, waiting for transfers between devices, deal(): lax.all_to_all(rows_val, AXES, split_axis=0, concat_axis=0, tiled=True)  16.2 us
    pallas_call x1, Pallas kernels, ffn_weights(): pl.pallas_call(ffn_weights_kernel, grid=(members, per), in_specs=[fixed,...  15.9 us
  transfers between devices with their start and end apart: 4, of which 2 were waited for; matrix products, arithmetic and copies ran while one was open for 4% of the time, Pallas kernels for 65%

profile of v4, /device:TPU:0, one launch (start us, length us, event | category | flops | bytes accessed | tf_op | source)
XLA Modules:
  0.0 389.0 jit_solution(18151067488877470934)
XLA Ops:
  7.2 0.0 all-gather.2.cloned.1.call-start
  7.2 1.7 pad_maximum_fusion
  8.9 0.0 all-gather.2.cloned.1.call-update
  9.0 0.7 reshape.150
  9.7 0.5 multiply_power_fusion.inverse_ref
  10.2 1.3 maximum_bitcast_fusion.bias_ref
  11.5 1.6 pad_maximum_fusion.1.shard_ref
  13.1 81.8 %head.1 = (bf16[32,32,768]{2,1,0:T(8,128)(2,1)}, bf16[2,2,2,2,2,192,384]{6,5,4,3,2,1,0:T(8,128)(2,1)}, f32[2,21,128]{2,1,0:T(8,128)}, f32[1024,128]{1,0:T(8,128)...) custom-call(bf16[32,32,768]{2,1,0:T(8,128)(2,1)} %rows_ref.1, bf16[192,384]{1,0:T(8,128)(2,1)} %pad_maximum_fusion.1.shard_ref, ...), custom_call_target="tpu_custom_call" | custom-call | tf_op jit(solution)/shard_map/head/pallas_call | solution.py:625
  94.9 0.0 copy-start.11
  94.9 0.0 copy-start.13
  94.9 0.0 copy-start.14
  94.9 0.0 copy-start.15
  94.9 0.0 copy-start.16
  94.9 0.0 copy-start.17
  95.0 0.0 copy-start.18
  95.0 0.0 copy-start.3
  95.0 0.0 copy-start.5
  95.0 0.0 copy-start.6
  95.0 10.4 %all-to-all-start = ((bf16[32,32,768]{2,1,0:T(8,128)(2,1)}), bf16[32,32,768]{2,1,0:T(8,128)(2,1)}, u32[]{:S(2)}, u32[]{:S(2)}) async-start(bf16[32,32,768]{2,1,0:T(8,128)(2,1)} %param.17), calls=%async_computation | async-start | bytes 3145728 | tf_op jit(solution)/shard_map/all_to_all | solution.py:778
  105.4 0.0 reduce-scatter.2.cloned.1.call-start
  105.5 0.0 copy-done.11
  105.6 0.6 copy.33
  106.2 0.0 copy-done.13
  106.2 0.0 copy-done.14
  106.2 0.0 copy-done.15
  106.2 0.0 copy-done.16
  106.3 0.0 copy-done.17
  106.3 0.0 copy-done.18
  106.3 2.3 copy-done.1
  108.7 8.2 %project.1.q_ref.k_ref.v_ref = bf16[3,1024,768]{2,1,0:T(8,128)(2,1)S(1)} custom-call(bf16[1024,768]{1,0:T(8,128)(2,1)S(1)} %bitcast.34, bf16[16,2,192,384]{3,2,1,0:T(8,128)(2,1)S(1)} %bitcast.31, f32[3,1,768]{2,1,0:T(1,128)S(1)} %broadcast_in_dim_reshape.3.b_ref, f32[1024,128]{1,0:T(8,128)S(1)} %copy-done.5, f32[1024,128]{1,0:T(8,128)S(1)} %copy-done.6), custom_call_target="tpu_custom_call" | custom-call | tf_op jit(solution)/shard_map/project/pallas_call | solution.py:74
  116.9 0.0 copy-start
  116.9 0.0 copy-done.4
  116.9 20.7 %attend.1 = (bf16[1024,768]{1,0:T(8,128)(2,1)S(1)}, f32[6,2,1024]{2,1,0:T(2,128)S(1)}) custom-call(bf16[3,1024,768]{2,1,0:T(8,128)(2,1)S(1)} %project.1.q_ref.k_ref.v_ref, bf16[3,1024,768]{2,1,0:T(8,128)(2,1)S(1)} %project.1.q_ref.k_ref.v_ref, bf16[3,1024,768]{2,1,0:T(8,128)(2,1)S(1)} %project.1.q_ref.k_ref.v_ref, bf16[1024,128]{1,0:T(8,128)(2,1)S(1)} %copy-done.4), custom_call_target="tpu_custom_call" | custom-call | tf_op jit(solution)/shard_map/attend/pallas_call | solution.py:135
  137.6 0.0 copy-done
  137.6 0.0 copy-start.2
  137.6 1.1 copy-done.2
  138.7 0.6 copy-done.7
  139.3 0.6 stack.31.vec_ref
  140.0 16.2 %all-to-all-done = bf16[32,32,768]{2,1,0:T(8,128)(2,1)} async-done(((bf16[32,32,768]{2,1,0:T(8,128)(2,1)}), bf16[32,32,768]{2,1,0:T(8,128)(2,1)}, u32[]{:S(2)}, u32[]{:S(2)}) %all-to-all-start) | async-done | bytes 1572896 | tf_op jit(solution)/shard_map/all_to_all | solution.py:778
  156.2 37.7 %middle.1 = (bf16[1024,768]{1,0:T(8,128)(2,1)}, bf16[1024,3072]{1,0:T(8,128)(2,1)}, bf16[1024,3072]{1,0:T(8,128)(2,1)}, bf16[1024,768]{1,0:T(8,128)(2,1)}, bf16[...) custom-call(bf16[1024,768]{1,0:T(8,128)(2,1)} %bitcast.32, ...), custom_call_target="tpu_custom_call" | custom-call | tf_op jit(solution)/shard_map/middle/pallas_call | solution.py:326
  194.0 15.9 %ffn_weights.1 = bf16[16,2,96,1536]{3,2,1,0:T(8,128)(2,1)} custom-call(bf16[1024,768]{1,0:T(8,128)(2,1)} %get-tuple-element.62.mid_ref, bf16[1024,768]{1,0:T(8,128)(2,1)} %get-tuple-element.63.g_down_ref, bf16[1024,3072]{1,0:T(8,128)(2,1)} %get-tuple-element.64.act_ref, bf16[1024,3072]{1,0:T(8,128)(2,1)} %get-tuple-element.65.g_up_ref), custom_call_target="tpu_custom_call" | custom-call | tf_op jit(solution)/shard_map/ffn_weights/pallas_call | solution.py:372
  209.9 0.0 reduce-scatter.2.cloned.1.call-update
  209.9 2.9 all-to-all-start.1
  212.9 36.0 %attend_back.1.raw_ref = bf16[3,1024,768]{2,1,0:T(8,128)(2,1)} custom-call(bf16[3,1024,768]{2,1,0:T(8,128)(2,1)} %copy-done, bf16[3,1024,768]{2,1,0:T(8,128)(2,1)} %copy-done, bf16[3,1024,768]{2,1,0:T(8,128)(2,1)} %copy-done, bf16[1024,128]{1,0:T(8,128)(2,1)} %get-tuple-element.46.bias_ref.live_ref, bf16[1024,768]{1,0:T(8,128)(2,1)} %copy-done.2, ...), custom_call_target="tpu_custom_call" | custom-call | tf_op jit(solution)/shard_map/attend_back/pallas_call | solution.py:208
  248.9 19.5 %attn_weights.1 = (bf16[16,2,192,384]{3,2,1,0:T(8,128)(2,1)}, bf16[1024,768]{1,0:T(8,128)(2,1)}, f32[8,768]{1,0:T(8,128)}) custom-call(bf16[1024,768]{1,0:T(8,128)(2,1)} %bitcast.33, bf16[1024,768]{1,0:T(8,128)(2,1)} %get-tuple-element.50.g_attn_ref, bf16[1024,768]{1,0:T(8,128)(2,1)} %copy-done.2, bf16[3,1024,768]{2,1,0:T(8,128)(2,1)} %attend_back.1.raw_ref, ...), custom_call_target="tpu_custom_call" | custom-call | tf_op jit(solution)/shard_map/attn_weights/pallas_call | solution.py:423
  268.4 0.7 slice.50
  269.2 0.5 broadcast.117
  269.7 0.7 reduce.15
  270.4 0.6 select_maximum_fusion.small_ref
  271.0 86.4 %tail.1 = (bf16[32,32,768]{2,1,0:T(8,128)(2,1)}, f32[192,384]{1,0:T(8,128)}, f32[16,768]{1,0:T(8,128)}) custom-call(bf16[32,32,768]{2,1,0:T(8,128)(2,1)} %bitcast.38, bf16[2,2,2,2,2,192,384]{6,5,4,3,2,1,0:T(8,128)(2,1)} %bitcast.37, f32[16,768]{1,0:T(8,128)} %select_maximum_fusion.small_ref), custom_call_target="tpu_custom_call" | custom-call | tf_op jit(solution)/shard_map/tail/pallas_call | solution.py:743
  357.5 0.7 slice.59
  358.2 1.3 slice.53
  359.5 1.6 slice.52
  361.2 0.6 reshape.163
  361.8 1.6 slice_reduce_fusion
  363.4 1.5 slice_bitcast_fusion.1
  364.9 0.0 all-to-all-done.1
  364.9 11.5 %reduce-scatter.2.cloned.1.call-done = bf16[96,1536]{1,0:T(8,128)(2,1)} async-done(((bf16[3072,1536]{1,0:T(8,128)(2,1)}), bf16[96,1536]{1,0:T(8,128)(2,1)}) %reduce-scatter.2.cloned.1.call-update) | async-done | bytes 294928 | tf_op jit(solution)/shard_map/reduce_scatter | solution.py:804
  376.4 1.1 convert_element_type.16
  377.5 0.7 slice_bitcast_fusion
  378.3 0.7 slice.66
  379.0 1.1 copy.38
  380.1 0.8 copy-done.8
  381.0 1.1 copy.39
  (29 shorter events, 0.1 us)
Async XLA Ops:
  7.2 149.0 %all-gather.2.cloned.1.call-start = ((), (), s32[]{:S(2)}) async-start(), calls=%async_computation.3 | async-start | bytes 9732096 | tf_op jit(solution)/shard_map/all_gather | solution.py:781
  94.9 10.6 %copy-start.11 = (f32[2,21,128]{2,1,0:T(8,128)S(1)}, f32[2,21,128]{2,1,0:T(8,128)}, u32[]{:S(2)}) copy-start(f32[2,21,128]{2,1,0:T(8,128)} %get-tuple-element.43) | copy-start | bytes 64516
  94.9 11.3 %copy-start.13 = (f32[768]{0:T(1024)S(1)}, f32[768]{0:T(1024)}, u32[]{:S(2)}) copy-start(f32[768]{0:T(1024)} %param.23) | copy-start | bytes 9220
  94.9 11.3 %copy-start.14 = (f32[768]{0:T(1024)S(1)}, f32[768]{0:T(1024)}, u32[]{:S(2)}) copy-start(f32[768]{0:T(1024)} %param.24) | copy-start | bytes 9220
  94.9 11.3 %copy-start.15 = (f32[768]{0:T(1024)S(1)}, f32[768]{0:T(1024)}, u32[]{:S(2)}) copy-start(f32[768]{0:T(1024)} %param.25) | copy-start | bytes 9220
  94.9 11.3 %copy-start.16 = (f32[768]{0:T(1024)S(1)}, f32[768]{0:T(1024)}, u32[]{:S(2)}) copy-start(f32[768]{0:T(1024)} %param.29) | copy-start | bytes 9220
  94.9 11.3 %copy-start.17 = (f32[768]{0:T(1024)S(1)}, f32[768]{0:T(1024)}, u32[]{:S(2)}) copy-start(f32[768]{0:T(1024)} %param.30) | copy-start | bytes 9220
  95.0 11.3 %copy-start.18 = (f32[768]{0:T(1024)S(1)}, f32[768]{0:T(1024)}, u32[]{:S(2)}) copy-start(f32[768]{0:T(1024)} %param.31) | copy-start | bytes 9220
  95.0 11.3 %copy-start.3 = (bf16[32,32,768]{2,1,0:T(8,128)(2,1)S(1)}, bf16[32,32,768]{2,1,0:T(8,128)(2,1)}, u32[]{:S(2)}) copy-start(bf16[32,32,768]{2,1,0:T(8,128)(2,1)} %get-tuple-element.40) | copy-start | bytes 4718596
  95.0 11.3 %copy-start.5 = (f32[1024,128]{1,0:T(8,128)S(1)}, f32[1024,128]{1,0:T(8,128)}, u32[]{:S(2)}) copy-start(f32[1024,128]{1,0:T(8,128)} %get-tuple-element.44.cos_ref) | copy-start | bytes 1572868
  95.0 11.3 %copy-start.6 = (f32[1024,128]{1,0:T(8,128)S(1)}, f32[1024,128]{1,0:T(8,128)}, u32[]{:S(2)}) copy-start(f32[1024,128]{1,0:T(8,128)} %get-tuple-element.45.sine_ref) | copy-start | bytes 1572868
  95.0 61.2 %all-to-all-start = ((bf16[32,32,768]{2,1,0:T(8,128)(2,1)}), bf16[32,32,768]{2,1,0:T(8,128)(2,1)}, u32[]{:S(2)}, u32[]{:S(2)}) async-start(bf16[32,32,768]{2,1,0:T(8,128)(2,1)} %param.17), calls=%async_computation | async-start | bytes 3145728 | tf_op jit(solution)/shard_map/all_to_all | solution.py:778
  105.4 271.0 %reduce-scatter.2.cloned.1.call-start = ((), (), s32[]{:S(2)}) async-start(), calls=%async_computation.4 | async-start | bytes 9732096 | tf_op jit(solution)/shard_map/reduce_scatter | solution.py:804
  106.3 2.3 copy-start.1
  108.7 8.2 %copy-start.4 = (bf16[1024,128]{1,0:T(8,128)(2,1)S(1)}, bf16[1024,128]{1,0:T(8,128)(2,1)}, u32[]{:S(2)}) copy-start(bf16[1024,128]{1,0:T(8,128)(2,1)} %get-tuple-element.46.bias_ref.live_ref) | copy-start | bytes 786436
  116.9 20.7 %copy-start = (bf16[3,1024,768]{2,1,0:T(8,128)(2,1)}, bf16[3,1024,768]{2,1,0:T(8,128)(2,1)S(1)}, u32[]{:S(2)}) copy-start(bf16[3,1024,768]{2,1,0:T(8,128)(2,1)S(1)} %project.1.q_ref.k_ref.v_ref) | copy-start | bytes 14155780
  137.6 1.1 copy-start.2
  138.7 0.6 copy-start.7
  209.9 155.0 %all-to-all-start.1 = ((bf16[32,32,768]{2,1,0:T(8,128)(2,1)}), bf16[32,32,768]{2,1,0:T(8,128)(2,1)S(1)}, u32[]{:S(2)}, u32[]{:S(2)}) async-start(bf16[32,32,768]{2,1,0:T(8,128)(2,1)} %bitcast.11), calls=%async_computation.1 | async-start | bytes 3145728 | tf_op jit(solution)/shard_map/all_to_all | solution.py:778
  248.9 20.8 %copy-start.12 = (f32[1,3072]{1,0:T(1,128)S(1)}, f32[1,3072]{1,0:T(1,128)}, u32[]{:S(2)}) copy-start(f32[1,3072]{1,0:T(1,128)} %get-tuple-element.58) | copy-start | bytes 36868
  248.9 21.5 %copy-start.10 = (f32[8,768]{1,0:T(8,128)S(1)}, f32[8,768]{1,0:T(8,128)}, u32[]{:S(2)}) copy-start(f32[8,768]{1,0:T(8,128)} %get-tuple-element.57) | copy-start | bytes 73732
  376.4 1.8 copy-start.9
  379.0 2.0 copy-start.8
Sparse Core Ops, SparseCore 0:
  11.5 134.1 all-gather.1
  210.1 166.3 reduce-scatter.1
